TPU v7x, 32 devices: a whole 2x2x4 slice. The times are simulated.
32 devices in a mesh: dp: 8 (over z, core), tensor: 4 (over y, x).
Axes of the slice: x: 2, y: 2, z: 4, core: 2. Of those that a mesh axis runs over, the one named last changes fastest.
Arguments:
- inputs: bfloat16 [8192, 2048], P(('dp', 'tensor'))
- doc_lengths: int32 [8, 4], P('dp'), may hold values from 0 to 1024, as said below
- attn_gain: bfloat16 [2048], P('dp'), may hold values from 0.099609375 to 1.8984375
- w_query: bfloat16 [2048, 2048], P('dp', 'tensor')
- w_key: bfloat16 [2048, 512], P('dp', 'tensor')
- value_weight: bfloat16 [2048, 512], P('dp', 'tensor'), may hold values from -0.125 to 0.125
- w_output: bfloat16 [2048, 2048], P('tensor', 'dp'), may hold values from -0.5 to 0.5
- mlp_gain: bfloat16 [2048], P('dp'), may hold values from 0.099609375 to 1.8984375
- w_gate: bfloat16 [2048, 8192], P('dp', 'tensor'), may hold values from -0.125 to 0.125
- w_up: bfloat16 [2048, 8192], P('dp', 'tensor'), may hold values from -0.125 to 0.125
- w_down: bfloat16 [8192, 2048], P('tensor', 'dp'), may hold values from -0.125 to 0.125
- out_grad: bfloat16 [8192, 2048], P(('dp', 'tensor')), may hold values from -6 to 6
Outputs:
- output: float32 [8192, 2048], P(('dp', 'tensor'))
- input_grad: float32 [8192, 2048], P(('dp', 'tensor'))
- attn_gain_grad: float32 [2048], P('dp')
- w_query_grad: float32 [2048, 2048], P('dp', 'tensor')
- w_key_grad: float32 [2048, 512], P('dp', 'tensor')
- w_value_grad: float32 [2048, 512], P('dp', 'tensor')
- w_output_grad: float32 [2048, 2048], P('tensor', 'dp')
- mlp_gain_grad: float32 [2048], P('dp')
- w_gate_grad: float32 [2048, 8192], P('dp', 'tensor')
- w_up_grad: float32 [2048, 8192], P('dp', 'tensor')
- w_down_grad: float32 [8192, 2048], P('tensor', 'dp')
Inputs may be any that keep to these rules, and one draw needn't show every extreme that they name: `doc_lengths`: row r lists the lengths of the 4 documents packed back to back from the first slot of dp index r; a row sums to at most 1024, zero lengths occur, and in every draw some row holds a single document of 1024 tokens.
All inputs are finite; a program needn't handle non-finite values.
Results may differ from a plain program's by a relative error of at most 0.017.
The roundings to bfloat16 on the way count: a program that leaves them out, or rounds other values in their place, can miss the bound.
Values may be sent and summed in bfloat16 or wider, within the bound.
A program may use at most 256 MiB of HBM per device.

v0:
```python
import jax
import jax.numpy as jnp
from jax import lax
from jax.sharding import PartitionSpec as P

HEAD_SIZE = 64
QBLK = 512


epsilon = 1e-05
rope_base = 500000.0


def layout(lengths, total_rows):
    row_index = jnp.arange(total_rows, dtype=jnp.int32)
    doc_ends = jnp.cumsum(lengths)
    passed = doc_ends[None, :] <= row_index[:, None]
    document_segment = jnp.sum(passed.astype(jnp.int32), axis=1)
    doc_start = jnp.sum(jnp.where(passed, lengths[None, :], 0), axis=1)
    positions = (row_index - doc_start).astype(jnp.float32)
    valid_rows = (document_segment < lengths.shape[0]).astype(jnp.float32)
    return (document_segment, positions, valid_rows)


def rope_tables(positions, head_dim):
    half_dim = head_dim // 2
    inverse_freq = rope_base ** (-(jnp.arange(half_dim, dtype=jnp.float32) * 2.0 / head_dim))
    angles = positions[:, None] * inverse_freq[None, :]
    return (jnp.cos(angles)[:, None, :], jnp.sin(angles)[:, None, :])


def rotate(tensor, cosine, sine_part, direction):
    half_dim = tensor.shape[-1] // 2
    first_half = tensor[..., :half_dim]
    second_half = tensor[..., half_dim:]
    return jnp.concatenate(
        [
            first_half * cosine - direction * second_half * sine_part,
            second_half * cosine + direction * first_half * sine_part,
        ],
        axis=-1,
    )


def rms_stats(hidden):
    scale_row = lax.rsqrt(jnp.mean(hidden * hidden, axis=-1, keepdims=True) + epsilon)
    return (scale_row, hidden * scale_row)


def norm_backward(grad_normed, unit_rows, scale_row, gain_wide):
    scaled = grad_normed * gain_wide
    return scale_row * (scaled - unit_rows * jnp.mean(scaled * unit_rows, axis=-1, keepdims=True))


def block_mask(document_segment, first_row, block_rows):
    row_index = jnp.arange(document_segment.shape[0], dtype=jnp.int32)
    query_rows = first_row + jnp.arange(block_rows, dtype=jnp.int32)
    query_segment = lax.dynamic_slice_in_dim(document_segment, first_row, block_rows, 0)
    return (query_segment[:, None] == document_segment[None, :]) & (
        row_index[None, :] <= query_rows[:, None]
    )


def attention_forward(queries, keys_rot, values, document_segment, block_rows):
    total_rows, kv_heads, group_size, head_dim = queries.shape
    score_scale = head_dim ** (-0.5)

    def one_block(block_index):
        first_row = block_index * block_rows
        query_block = lax.dynamic_slice_in_dim(queries, first_row, block_rows, 0)
        allowed = block_mask(document_segment, first_row, block_rows)
        scores = (
            jnp.einsum("qkgd,skd->kgqs", query_block, keys_rot, preferred_element_type=jnp.float32)
            * score_scale
        )
        scores = jnp.where(allowed, scores, -jnp.inf)
        row_max = jnp.max(scores, axis=-1, keepdims=True)
        log_total = row_max + jnp.log(jnp.sum(jnp.exp(scores - row_max), axis=-1, keepdims=True))
        weights = jnp.exp(scores - log_total).astype(jnp.bfloat16)
        attended = jnp.einsum("kgqs,skd->qkgd", weights, values, preferred_element_type=jnp.float32)
        return (attended.astype(jnp.bfloat16), log_total[..., 0])

    attended, log_total = lax.map(one_block, jnp.arange(total_rows // block_rows, dtype=jnp.int32))
    return (attended.reshape(total_rows, kv_heads, group_size, head_dim), log_total)


def attention_backward(
    queries, keys_rot, values, attended, grad_attended, log_total, document_segment, block_rows
):
    total_rows, kv_heads, group_size, head_dim = queries.shape
    score_scale = head_dim ** (-0.5)

    def one_block(running, block_index):
        key_grad, value_grad = running
        first_row = block_index * block_rows
        query_block = lax.dynamic_slice_in_dim(queries, first_row, block_rows, 0)
        block_gradient = lax.dynamic_slice_in_dim(grad_attended, first_row, block_rows, 0)
        out_block = lax.dynamic_slice_in_dim(attended, first_row, block_rows, 0)
        allowed = block_mask(document_segment, first_row, block_rows)
        scores = (
            jnp.einsum("qkgd,skd->kgqs", query_block, keys_rot, preferred_element_type=jnp.float32)
            * score_scale
        )
        scores = jnp.where(allowed, scores, -jnp.inf)
        prob_full = jnp.exp(scores - log_total[block_index][..., None])
        weights = prob_full.astype(jnp.bfloat16)
        value_grad = value_grad + jnp.einsum(
            "kgqs,qkgd->skd", weights, block_gradient, preferred_element_type=jnp.float32
        )
        grad_probs = jnp.einsum(
            "qkgd,skd->kgqs", block_gradient, values, preferred_element_type=jnp.float32
        )
        row_delta = jnp.einsum(
            "qkgd,qkgd->kgq", block_gradient, out_block, preferred_element_type=jnp.float32
        )
        grad_scores = (prob_full * (grad_probs - row_delta[..., None])).astype(jnp.bfloat16)
        query_grad = (
            jnp.einsum("kgqs,skd->qkgd", grad_scores, keys_rot, preferred_element_type=jnp.float32)
            * score_scale
        )
        key_grad = (
            key_grad
            + jnp.einsum(
                "kgqs,qkgd->skd", grad_scores, query_block, preferred_element_type=jnp.float32
            )
            * score_scale
        )
        return ((key_grad, value_grad), query_grad)

    zero_keys = jnp.zeros((total_rows, kv_heads, head_dim), jnp.float32)
    (key_grad, value_grad), query_grad = lax.scan(
        one_block, (zero_keys, zero_keys), jnp.arange(total_rows // block_rows, dtype=jnp.int32)
    )
    return (query_grad.reshape(total_rows, kv_heads * group_size, head_dim), key_grad, value_grad)


def attn_params(attn_gain, w_query, w_key, value_weight, w_output):
    return (
        lax.all_gather(attn_gain, "dp", axis=0, tiled=True),
        lax.all_gather(w_query, "dp", axis=0, tiled=True),
        lax.all_gather(w_key, "dp", axis=0, tiled=True),
        lax.all_gather(value_weight, "dp", axis=0, tiled=True),
        lax.all_gather(w_output, "dp", axis=1, tiled=True),
    )


def mlp_params(mlp_gain, w_gate, w_up, w_down):
    return (
        lax.all_gather(mlp_gain, "dp", axis=0, tiled=True),
        lax.all_gather(w_gate, "dp", axis=0, tiled=True),
        lax.all_gather(w_up, "dp", axis=0, tiled=True),
        lax.all_gather(w_down, "dp", axis=1, tiled=True),
    )


def per_device(
    inputs,
    doc_lengths,
    attn_gain,
    w_query,
    w_key,
    value_weight,
    w_output,
    mlp_gain,
    w_gate,
    w_up,
    w_down,
    out_grad,
):
    tensor_count = lax.axis_size("tensor")
    tensor_rank = lax.axis_index("tensor")
    own_rows = inputs.shape[0]
    total_rows = own_rows * tensor_count
    document_segment, positions, valid_rows = layout(doc_lengths[0], total_rows)
    valid_own = lax.dynamic_slice_in_dim(valid_rows, tensor_rank * own_rows, own_rows, 0)[:, None]
    cosine, sine_part = rope_tables(positions, HEAD_SIZE)
    gain_one, full_query, full_key, full_value, full_output = attn_params(
        attn_gain, w_query, w_key, value_weight, w_output
    )
    gain_two, full_gate, full_up, complete_down_weight = mlp_params(mlp_gain, w_gate, w_up, w_down)
    head_count = full_query.shape[1] // HEAD_SIZE
    kv_heads = full_key.shape[1] // HEAD_SIZE
    group_size = head_count // kv_heads
    residual = inputs.astype(jnp.float32)
    scale_one, unit_one = rms_stats(residual)
    normed_one = (unit_one * gain_one.astype(jnp.float32)).astype(jnp.bfloat16)
    normed_one_all = lax.all_gather(normed_one, "tensor", axis=0, tiled=True)
    query_full = jnp.dot(normed_one_all, full_query, preferred_element_type=jnp.float32).reshape(
        total_rows, head_count, HEAD_SIZE
    )
    queries = (
        rotate(query_full, cosine, sine_part, 1.0)
        .astype(jnp.bfloat16)
        .reshape(total_rows, kv_heads, group_size, HEAD_SIZE)
    )
    key_full = jnp.dot(normed_one_all, full_key, preferred_element_type=jnp.float32).reshape(
        total_rows, kv_heads, HEAD_SIZE
    )
    keys_rot = rotate(key_full, cosine, sine_part, 1.0).astype(jnp.bfloat16)
    values = jnp.dot(normed_one_all, full_value, preferred_element_type=jnp.float32).astype(
        jnp.bfloat16
    )
    values = values.reshape(total_rows, kv_heads, HEAD_SIZE)
    attended, log_total = attention_forward(queries, keys_rot, values, document_segment, QBLK)
    attended_flat = attended.reshape(total_rows, head_count * HEAD_SIZE)
    rows_part = attended_flat
    attn_out = lax.psum_scatter(
        jnp.dot(rows_part, full_output, preferred_element_type=jnp.float32),
        "tensor",
        scatter_dimension=0,
        tiled=True,
    )
    hidden = residual + valid_own * attn_out
    scale_two, unit_two = rms_stats(hidden)
    normed_two = (unit_two * gain_two.astype(jnp.float32)).astype(jnp.bfloat16)
    normed_two_all = lax.all_gather(normed_two, "tensor", axis=0, tiled=True)
    gate_pre = jnp.dot(normed_two_all, full_gate, preferred_element_type=jnp.float32)
    up_proj = jnp.dot(normed_two_all, full_up, preferred_element_type=jnp.float32)
    sigmoid_gate = jax.nn.sigmoid(gate_pre)
    activation = (gate_pre * sigmoid_gate * up_proj).astype(jnp.bfloat16)
    rows_part = activation
    mlp_out = lax.psum_scatter(
        jnp.dot(rows_part, complete_down_weight, preferred_element_type=jnp.float32),
        "tensor",
        scatter_dimension=0,
        tiled=True,
    )
    output = hidden + valid_own * mlp_out
    gain_one, full_query, full_key, full_value, full_output = attn_params(
        attn_gain, w_query, w_key, value_weight, w_output
    )
    gain_two, full_gate, full_up, complete_down_weight = mlp_params(mlp_gain, w_gate, w_up, w_down)
    grad_out = out_grad.astype(jnp.float32)
    grad_mlp = (grad_out * valid_own).astype(jnp.bfloat16)
    grad_mlp_all = lax.all_gather(grad_mlp, "tensor", axis=0, tiled=True)
    w_down_part = jnp.dot(activation.T, grad_mlp_all, preferred_element_type=jnp.float32)
    grad_act = jnp.dot(grad_mlp_all, complete_down_weight.T, preferred_element_type=jnp.float32)
    grad_gate = (
        grad_act * up_proj * sigmoid_gate * (1.0 + gate_pre * (1.0 - sigmoid_gate))
    ).astype(jnp.bfloat16)
    grad_up = (grad_act * gate_pre * sigmoid_gate).astype(jnp.bfloat16)
    grad_normed_two = lax.psum_scatter(
        jnp.dot(grad_gate, full_gate.T, preferred_element_type=jnp.float32)
        + jnp.dot(grad_up, full_up.T, preferred_element_type=jnp.float32),
        "tensor",
        scatter_dimension=0,
        tiled=True,
    )
    w_gate_part = jnp.dot(normed_two_all.T, grad_gate, preferred_element_type=jnp.float32)
    w_up_part = jnp.dot(normed_two_all.T, grad_up, preferred_element_type=jnp.float32)
    mlp_gain_part = jnp.sum(grad_normed_two * unit_two, axis=0)
    mlp_gain_slice, w_gate_grad, w_up_grad, w_down_grad = (
        lax.psum_scatter(mlp_gain_part, "dp", scatter_dimension=0, tiled=True),
        lax.psum_scatter(w_gate_part, "dp", scatter_dimension=0, tiled=True),
        lax.psum_scatter(w_up_part, "dp", scatter_dimension=0, tiled=True),
        lax.psum_scatter(w_down_part, "dp", scatter_dimension=1, tiled=True),
    )
    grad_hidden = grad_out + norm_backward(
        grad_normed_two, unit_two, scale_two, gain_two.astype(jnp.float32)
    )
    grad_attn = (grad_hidden * valid_own).astype(jnp.bfloat16)
    grad_attn_all = lax.all_gather(grad_attn, "tensor", axis=0, tiled=True)
    w_output_part = jnp.dot(attended_flat.T, grad_attn_all, preferred_element_type=jnp.float32)
    grad_attended = jnp.dot(
        grad_attn_all, full_output.T, preferred_element_type=jnp.float32
    ).astype(jnp.bfloat16)
    grad_attended = grad_attended.reshape(total_rows, kv_heads, group_size, HEAD_SIZE)
    query_grad, key_grad, value_grad = attention_backward(
        queries, keys_rot, values, attended, grad_attended, log_total, document_segment, QBLK
    )
    query_back = (
        rotate(query_grad, cosine, sine_part, -1.0)
        .astype(jnp.bfloat16)
        .reshape(total_rows, head_count * HEAD_SIZE)
    )
    key_back = (
        rotate(key_grad, cosine, sine_part, -1.0)
        .astype(jnp.bfloat16)
        .reshape(total_rows, kv_heads * HEAD_SIZE)
    )
    value_back = value_grad.astype(jnp.bfloat16).reshape(total_rows, kv_heads * HEAD_SIZE)
    grad_normed_one = lax.psum_scatter(
        jnp.dot(query_back, full_query.T, preferred_element_type=jnp.float32)
        + jnp.dot(key_back, full_key.T, preferred_element_type=jnp.float32)
        + jnp.dot(value_back, full_value.T, preferred_element_type=jnp.float32),
        "tensor",
        scatter_dimension=0,
        tiled=True,
    )
    w_query_part = jnp.dot(normed_one_all.T, query_back, preferred_element_type=jnp.float32)
    w_key_part = jnp.dot(normed_one_all.T, key_back, preferred_element_type=jnp.float32)
    w_value_part = jnp.dot(normed_one_all.T, value_back, preferred_element_type=jnp.float32)
    attn_gain_part = jnp.sum(grad_normed_one * unit_one, axis=0)
    attn_gain_slice, w_query_grad, w_key_grad, w_value_grad, w_output_grad = (
        lax.psum_scatter(attn_gain_part, "dp", scatter_dimension=0, tiled=True),
        lax.psum_scatter(w_query_part, "dp", scatter_dimension=0, tiled=True),
        lax.psum_scatter(w_key_part, "dp", scatter_dimension=0, tiled=True),
        lax.psum_scatter(w_value_part, "dp", scatter_dimension=0, tiled=True),
        lax.psum_scatter(w_output_part, "dp", scatter_dimension=1, tiled=True),
    )
    input_grad = grad_hidden + norm_backward(
        grad_normed_one, unit_one, scale_one, gain_one.astype(jnp.float32)
    )
    gain_sums = lax.psum((attn_gain_slice, mlp_gain_slice), "tensor")
    return (
        output,
        input_grad,
        gain_sums[0],
        w_query_grad,
        w_key_grad,
        w_value_grad,
        w_output_grad,
        gain_sums[1],
        w_gate_grad,
        w_up_grad,
        w_down_grad,
    )


def solution(mesh):
    placed = (
        P(("dp", "tensor"), None),
        P("dp", None),
        P("dp"),
        P("dp", "tensor"),
        P("dp", "tensor"),
        P("dp", "tensor"),
        P("tensor", "dp"),
        P("dp"),
        P("dp", "tensor"),
        P("dp", "tensor"),
        P("tensor", "dp"),
        P(("dp", "tensor"), None),
    )
    return jax.shard_map(
        per_device,
        mesh=mesh,
        in_specs=placed,
        out_specs=(
            P(("dp", "tensor"), None),
            P(("dp", "tensor"), None),
            P("dp"),
            P("dp", "tensor"),
            P("dp", "tensor"),
            P("dp", "tensor"),
            P("tensor", "dp"),
            P("dp"),
            P("dp", "tensor"),
            P("dp", "tensor"),
            P("tensor", "dp"),
        ),
        check_vma=False,
    )
```

profile of v0, /device:TPU:0, one launch (start us, length us, event | category | flops | bytes accessed | tf_op | source)
XLA Modules:
  0.0 1804.1 jit_solution(7006812651238048975)
XLA Ops:
  8.6 13.5 all-gather
  27.9 17.3 all_gather.51
  45.2 14.9 all_gather.52
  61.3 38.9 %all-gather.12.cloned.1.call-done = bf16[1024,2048]{1,0:T(8,128)(2,1)} async-done(((bf16[256,2048]{1,0:T(8,128)(2,1)}), bf16[1024,2048]{1,0:T(8,128)(2,1)}) %all-gather.12.cloned.1.call-update) | async-done | bytes 4194320 | tf_op jit(solution)/shard_map/all_gather | solution.py:187
  100.2 5.4 fusion.68
  109.2 27.3 %while.27 = (s32[]{:T(128)}, bf16[2,512,2,4,64]{1,4,3,2,0:T(8,128)(2,1)S(1)}, f32[2,2,4,512]{3,2,1,0:T(4,128)S(1)}, s32[2]{0:T(128)S(1)}, s32[1024]{0:T(1024)S(1...) while((s32[]{:T(128)}, ...), condition=%wide.region_7.8_spmd, body=%wide.region_4.7_spmd.sunk | while | flops 1121710592 | bytes 54147264 | solution.py:83
  138.9 7.6 fusion.70
  147.1 11.7 all-gather.1
  159.0 74.0 %reduce-scatter.12.cloned.1.call-done = f32[256,2048]{1,0:T(8,128)} async-done(((f32[1024,2048]{1,0:T(8,128)}), f32[256,2048]{1,0:T(8,128)}) %reduce-scatter.12.cloned.1.call-update) | async-done | bytes 2097168 | tf_op jit(solution)/shard_map/reduce_scatter | solution.py:207
  240.6 75.9 %all-gather.20.cloned.1.call-done = bf16[2048,2048]{1,0:T(8,128)(2,1)} async-done(((bf16[256,2048]{1,0:T(8,128)(2,1)}), bf16[2048,2048]{1,0:T(8,128)(2,1)}) %all-gather.20.cloned.1.call-update) | async-done | bytes 8388624 | tf_op jit(solution)/shard_map/all_gather | solution.py:150
  316.5 53.4 %all-gather.18.cloned.1.call-done = bf16[1024,2048]{1,0:T(8,128)(2,1)} async-done(((bf16[256,2048]{1,0:T(8,128)(2,1)}), bf16[1024,2048]{1,0:T(8,128)(2,1)}) %all-gather.18.cloned.1.call-update) | async-done | bytes 4194320 | tf_op jit(solution)/shard_map/all_gather | solution.py:216
  369.8 14.8 fusion.71
  384.6 68.9 %all-gather.22.cloned.1.call-done = bf16[2048,2048]{1,0:T(8,128)(2,1)} async-done(((bf16[256,2048]{1,0:T(8,128)(2,1)}), bf16[2048,2048]{1,0:T(8,128)(2,1)}) %all-gather.22.cloned.1.call-update) | async-done | bytes 8388624 | tf_op jit(solution)/shard_map/all_gather | solution.py:151
  453.5 14.4 fusion.72
  467.9 68.2 %all-gather.24.cloned.1.call-done = bf16[2048,2048]{1,0:T(8,128)(2,1)} async-done(((bf16[2048,256]{1,0:T(8,128)(2,1)}), bf16[2048,2048]{1,0:T(8,128)(2,1)}) %all-gather.24.cloned.1.call-update) | async-done | bytes 8388624 | tf_op jit(solution)/shard_map/all_gather | solution.py:152
  536.1 53.2 %all-gather.26.cloned.1.call-done = bf16[1024,2048]{1,0:T(8,128)(2,1)} async-done(((bf16[256,2048]{1,0:T(8,128)(2,1)}), bf16[1024,2048]{1,0:T(8,128)(2,1)}) %all-gather.26.cloned.1.call-update) | async-done | bytes 4194320 | tf_op jit(solution)/shard_map/all_gather | solution.py:235
  589.3 22.0 %multiply_convert_fusion = (bf16[1024,2048]{1,0:T(8,128)(2,1)}, bf16[1024,2048]{1,0:T(8,128)(2,1)}, bf16[1024,2048]{1,0:T(8,128)(2,1)}) fusion(f32[1024,2048]{1,0:T(8,128)} %fusion.71, f32[1024,2048]{1,0:T(8,128)} %fusion.72, bf16[1024,2048]{1,0:T(8,128)(2,1)} %all-gather.26.cloned.1.call-done, bf16[2048,2048]{1,0:T(8,128)(2,1)} %all-gather.24.cloned.1.call-done), kind=kOutput, calls=%fused_computation.62 | convolution fusion | flops 8623489024 | bytes 41943040 | tf_op jit(solution)/shard_map/dot_general | solution.py:237
  611.3 14.8 fusion.74
  626.1 12.9 convolution_add_fusion
  639.1 14.4 fusion.73
  653.6 71.9 %reduce-scatter.16.cloned.1.call-done = f32[256,2048]{1,0:T(8,128)} async-done(((f32[1024,2048]{1,0:T(8,128)}), f32[256,2048]{1,0:T(8,128)}) %reduce-scatter.16.cloned.1.call-update) | async-done | bytes 2097168 | tf_op jit(solution)/shard_map/reduce_scatter | solution.py:242
  728.3 86.7 %reduce-scatter.14.cloned.1.call-done = f32[256,2048]{1,0:T(8,128)} async-done(((f32[1024,2048]{1,0:T(8,128)}), f32[256,2048]{1,0:T(8,128)}) %reduce-scatter.14.cloned.1.call-update) | async-done | bytes 2097168 | tf_op jit(solution)/shard_map/reduce_scatter | solution.py:222
  824.4 48.4 %all-gather.28.cloned.1.call-done = bf16[1024,2048]{1,0:T(8,128)(2,1)} async-done(((bf16[256,2048]{1,0:T(8,128)(2,1)}), bf16[1024,2048]{1,0:T(8,128)(2,1)}) %all-gather.28.cloned.1.call-update) | async-done | bytes 4194320 | tf_op jit(solution)/shard_map/all_gather | solution.py:262
  872.8 5.5 convolution_convert_fusion
  878.3 132.7 %while.28 = (s32[]{:T(128)}, f32[1024,2,64]{0,2,1:T(8,128)}, f32[1024,2,64]{0,2,1:T(8,128)}, f32[2,512,2,4,64]{1,0,4,3,2:T(2,128)}, s32[2]{0:T(128)S(1)}, /*inde...) while((s32[]{:T(128)}, f32[1024,2,64]{0,2,1:T(8,128)}, ...), condition=%wide.region_14.15_spmd.clone, body=%wide.region_13.14_spmd.clone.sunk | while | flops 2729832960 | bytes 146422416 | solution.py:131
  886.1 9.4 fusion.164
  897.6 8.9 fusion.166
  910.9 19.6 %dynamic_update_slice.20 = f32[2,512,2,4,64]{1,0,4,3,2:T(2,128)} dynamic-update-slice(f32[2,512,2,4,64]{1,0,4,3,2:T(2,128)} %get-tuple-element.421, f32[1,512,2,4,64]{1,0,4,3,2:T(1,128)S(1)} %copy.60, s32[]{:T(128)} %get-tuple-element.418, s32[]{:T(128)} %constant.45.clone.1..sunk.1, s32[]{:T(128)} %constant.45.clone.1..sunk.1, s32[]{:T(128)} %constant.45.clone.1..sunk.1, s32[]{:T(128)} %constant.45.clone.1..sunk.1) | dynamic-update-slice | bytes 2097156 | tf_op jit(solution)/shard_map/while/body/jit(dynamic_update_index_in_dim)/dynamic_update_slice | solution.py:131
  935.7 9.0 fusion.168
  952.1 9.4 fusion.164
  963.6 8.9 fusion.166
  976.9 19.6 %dynamic_update_slice.20 = f32[2,512,2,4,64]{1,0,4,3,2:T(2,128)} dynamic-update-slice(f32[2,512,2,4,64]{1,0,4,3,2:T(2,128)} %get-tuple-element.421, f32[1,512,2,4,64]{1,0,4,3,2:T(1,128)S(1)} %copy.60, s32[]{:T(128)} %get-tuple-element.418, s32[]{:T(128)} %constant.45.clone.1..sunk.1, s32[]{:T(128)} %constant.45.clone.1..sunk.1, s32[]{:T(128)} %constant.45.clone.1..sunk.1, s32[]{:T(128)} %constant.45.clone.1..sunk.1) | dynamic-update-slice | bytes 2097156 | tf_op jit(solution)/shard_map/while/body/jit(dynamic_update_index_in_dim)/dynamic_update_slice | solution.py:131
  1001.7 9.1 fusion.168
  1012.2 5.6 fusion.76
  1040.3 6.7 fusion.77
  1048.3 6.7 fusion.80
  1055.0 15.4 fusion.81
  1070.5 15.5 fusion.82
  1086.3 15.2 fusion.83
  1103.4 14.2 reduce-scatter.18.cloned.1.call-done
  1119.8 28.5 %all-reduce.2 = (f32[2048]{0:T(1024)S(1)}, f32[2048]{0:T(1024)S(1)}) all-reduce(f32[2048]{0:T(1024)S(1)} %get-tuple-element.164, f32[2048]{0:T(1024)S(1)} %copy-done.33), channel_id=6, replica_groups=mesh['dp'=8,'tensor'=4] {'dp'}, use_global_device_ids=true, to_apply=%region_18.19.clone | all-reduce | flops 4096 | bytes 32768
  1148.5 9.5 all-reduce.3
  1163.0 23.4 %reduce-scatter.24.cloned.1.call-done = f32[256,128]{1,0:T(8,128)} async-done(((f32[2048,128]{1,0:T(8,128)}), f32[256,128]{1,0:T(8,128)}) %reduce-scatter.24.cloned.1.call-update) | async-done | bytes 131088 | tf_op jit(solution)/shard_map/reduce_scatter | solution.py:298
  1186.4 50.8 %reduce-scatter.20.cloned.1.call-done = f32[256,512]{1,0:T(8,128)} async-done(((f32[2048,512]{1,0:T(8,128)}), f32[256,512]{1,0:T(8,128)}) %reduce-scatter.20.cloned.1.call-update) | async-done | bytes 524304 | tf_op jit(solution)/shard_map/reduce_scatter | solution.py:296
  1237.3 51.1 %reduce-scatter.26.cloned.1.call-done = f32[512,256]{1,0:T(8,128)} async-done(((f32[512,2048]{1,0:T(8,128)}), f32[512,256]{1,0:T(8,128)}) %reduce-scatter.26.cloned.1.call-update) | async-done | bytes 524304 | tf_op jit(solution)/shard_map/reduce_scatter | solution.py:299
  1288.4 169.5 %reduce-scatter.28.cloned.1.call-done = f32[256,2048]{1,0:T(8,128)} async-done(((f32[2048,2048]{1,0:T(8,128)}), f32[256,2048]{1,0:T(8,128)}) %reduce-scatter.28.cloned.1.call-update) | async-done | bytes 2097168 | tf_op jit(solution)/shard_map/reduce_scatter | solution.py:254
  1457.8 169.6 %reduce-scatter.30.cloned.1.call-done = f32[256,2048]{1,0:T(8,128)} async-done(((f32[2048,2048]{1,0:T(8,128)}), f32[256,2048]{1,0:T(8,128)}) %reduce-scatter.30.cloned.1.call-update) | async-done | bytes 2097168 | tf_op jit(solution)/shard_map/reduce_scatter | solution.py:255
  1627.4 169.4 %reduce-scatter.32.cloned.1.call-done = f32[2048,256]{1,0:T(8,128)} async-done(((f32[2048,2048]{1,0:T(8,128)}), f32[2048,256]{1,0:T(8,128)}) %reduce-scatter.32.cloned.1.call-update) | async-done | bytes 2097168 | tf_op jit(solution)/shard_map/reduce_scatter | solution.py:256
  (258 shorter events, 126.6 us)
Async XLA Ops:
  7.2 20.4 %copy-start.40 = (s32[1,4]{1,0:T(1,128)S(1)}, s32[1,4]{1,0:T(1,128)}, u32[]{:S(2)}) copy-start(s32[1,4]{1,0:T(1,128)} %param.17) | copy-start | bytes 52
  7.2 20.7 %copy-start.31 = (bf16[256,128]{1,0:T(8,128)(2,1)S(1)}, bf16[256,128]{1,0:T(8,128)(2,1)}, u32[]{:S(2)}) copy-start(bf16[256,128]{1,0:T(8,128)(2,1)} %param.20) | copy-start | bytes 196612
  7.2 38.0 %copy-start.32 = (bf16[256,128]{1,0:T(8,128)(2,1)S(1)}, bf16[256,128]{1,0:T(8,128)(2,1)}, u32[]{:S(2)}) copy-start(bf16[256,128]{1,0:T(8,128)(2,1)} %param.21) | copy-start | bytes 196612
  7.2 54.1 %all-gather.14.cloned.1.call-start = ((), (), s32[]{:S(2)}) async-start(), calls=%async_computation.12 | async-start | bytes 2359296 | tf_op jit(solution)/shard_map/all_gather | solution.py:140
  7.9 92.2 %all-gather.12.cloned.1.call-start = ((), (), s32[]{:S(2)}) async-start(), calls=%async_computation.11 | async-start | bytes 5242880 | tf_op jit(solution)/shard_map/all_gather | solution.py:187
  26.8 112.1 %all-gather.16.cloned.1.call-start = ((), (), s32[]{:S(2)}) async-start(), calls=%async_computation.13 | async-start | bytes 2359296 | tf_op jit(solution)/shard_map/all_gather | solution.py:143
  27.5 205.4 %reduce-scatter.12.cloned.1.call-start = ((), (), s32[]{:S(2)}) async-start(), calls=%async_computation.14 | async-start | bytes 10485760 | tf_op jit(solution)/shard_map/reduce_scatter | solution.py:207
  45.2 60.7 %copy-start.14 = (bf16[2048,128]{1,0:T(8,128)(2,1)}, bf16[2048,128]{1,0:T(8,128)(2,1)S(1)}, u32[]{:S(2)}) copy-start(bf16[2048,128]{1,0:T(8,128)(2,1)S(1)} %all_gather.51) | copy-start | bytes 1572868
  60.1 47.6 %copy-start.12 = (bf16[2048,128]{1,0:T(8,128)(2,1)}, bf16[2048,128]{1,0:T(8,128)(2,1)S(1)}, u32[]{:S(2)}) copy-start(bf16[2048,128]{1,0:T(8,128)(2,1)S(1)} %all_gather.52) | copy-start | bytes 1572868
  61.3 46.1 %copy-start.16 = (f32[1024,32]{0,1:T(8,128)}, f32[1024,32]{0,1:T(8,128)S(1)}, u32[]{:S(2)}) copy-start(f32[1024,32]{0,1:T(8,128)S(1)} %get-tuple-element.233) | copy-start | bytes 393220
  136.5 22.4 %copy-start.18 = (s32[1024]{0:T(1024)}, s32[1024]{0:T(1024)S(1)}, u32[]{:S(2)}) copy-start(s32[1024]{0:T(1024)S(1)} %get-tuple-element.509) | copy-start | bytes 12292
  146.5 170.0 %all-gather.20.cloned.1.call-start = ((), (), s32[]{:S(2)}) async-start(), calls=%async_computation.16 | async-start | bytes 9437184 | tf_op jit(solution)/shard_map/all_gather | solution.py:150
  147.1 222.8 %all-gather.18.cloned.1.call-start = ((), (), s32[]{:S(2)}) async-start(), calls=%async_computation.15 | async-start | bytes 5242880 | tf_op jit(solution)/shard_map/all_gather | solution.py:216
  158.9 656.1 %copy-start.27 = (f32[8,1,256]{2,1,0:T(1,128)}, f32[8,1,256]{2,1,0:T(1,128)S(1)}, u32[]{:S(2)}) copy-start(f32[8,1,256]{2,1,0:T(1,128)S(1)} %convert_element_type.105) | copy-start | bytes 24580
  236.7 578.2 %copy-start.8 = (f32[256,2048]{1,0:T(8,128)}, f32[256,2048]{1,0:T(8,128)S(1)}, u32[]{:S(2)}) copy-start(f32[256,2048]{1,0:T(8,128)S(1)} %get-tuple-element.215) | copy-start | bytes 6291460
  236.7 578.2 %copy-start.34 = (f32[256]{0:T(256)}, f32[256]{0:T(256)S(1)}, u32[]{:S(2)}) copy-start(f32[256]{0:T(256)S(1)} %add_rsqrt_fusion) | copy-start | bytes 3076
  238.3 215.2 %all-gather.22.cloned.1.call-start = ((), (), s32[]{:S(2)}) async-start(), calls=%async_computation.17 | async-start | bytes 9437184 | tf_op jit(solution)/shard_map/all_gather | solution.py:151
  239.0 297.0 %all-gather.24.cloned.1.call-start = ((), (), s32[]{:S(2)}) async-start(), calls=%async_computation.18 | async-start | bytes 9437184 | tf_op jit(solution)/shard_map/all_gather | solution.py:152
  239.8 349.5 %all-gather.26.cloned.1.call-start = ((), (), s32[]{:S(2)}) async-start(), calls=%async_computation.20 | async-start | bytes 5242880 | tf_op jit(solution)/shard_map/all_gather | solution.py:235
  240.5 485.0 %reduce-scatter.16.cloned.1.call-start = ((), (), s32[]{:S(2)}) async-start(), calls=%async_computation.21 | async-start | bytes 10485760 | tf_op jit(solution)/shard_map/reduce_scatter | solution.py:242
  611.3 14.8 copy-start.41
  611.3 14.8 copy-start.46
  639.0 175.9 %reduce-scatter.14.cloned.1.call-start = ((), (), s32[]{:S(2)}) async-start(), calls=%async_computation.19 | async-start | bytes 10485760 | tf_op jit(solution)/shard_map/reduce_scatter | solution.py:222
  653.6 219.2 %all-gather.28.cloned.1.call-start = ((), (), s32[]{:S(2)}) async-start(), calls=%async_computation.22 | async-start | bytes 5242880 | tf_op jit(solution)/shard_map/all_gather | solution.py:262
  728.3 91.8 %copy-start.38 = (f32[256]{0:T(256)}, f32[256]{0:T(256)S(1)}, u32[]{:S(2)}) copy-start(f32[256]{0:T(256)S(1)} %broadcast_multiply_fusion.2) | copy-start | bytes 3076
  820.0 52.8 %copy-start.43 = (bf16[512,2048]{1,0:T(8,128)(2,1)S(1)}, bf16[512,2048]{1,0:T(8,128)(2,1)}, u32[]{:S(2)}) copy-start(bf16[512,2048]{1,0:T(8,128)(2,1)} %all-gather.16.cloned.1.call-done) | copy-start | bytes 6291460
  820.1 297.5 %reduce-scatter.18.cloned.1.call-start = ((), (), s32[]{:S(2)}) async-start(), calls=%async_computation.23 | async-start | bytes 10485760 | tf_op jit(solution)/shard_map/reduce_scatter | solution.py:282
  824.4 54.0 %copy-start.19 = (s32[1024]{0:T(1024)S(1)}, s32[1024]{0:T(1024)}, u32[]{:S(2)}) copy-start(s32[1024]{0:T(1024)} %copy-done.18) | copy-start | bytes 12292
  878.3 132.7 %copy-start.17 = (f32[1024,32]{0,1:T(8,128)S(1)}, f32[1024,32]{0,1:T(8,128)}, u32[]{:S(2)}) copy-start(f32[1024,32]{0,1:T(8,128)} %copy-done.16) | copy-start | bytes 393220
  886.1 11.5 copy-start.11
  886.1 11.5 copy-start.24
  909.8 20.7 %copy-start.6 = (f32[1024,2,64]{0,2,1:T(8,128)S(1)}, f32[1024,2,64]{0,2,1:T(8,128)}, u32[]{:S(2)}) copy-start(f32[1024,2,64]{0,2,1:T(8,128)} %get-tuple-element.419) | copy-start | bytes 1572868 | tf_op jit(solution)/shard_map/while
  975.8 20.7 %copy-start.6 = (f32[1024,2,64]{0,2,1:T(8,128)S(1)}, f32[1024,2,64]{0,2,1:T(8,128)}, u32[]{:S(2)}) copy-start(f32[1024,2,64]{0,2,1:T(8,128)} %get-tuple-element.419) | copy-start | bytes 1572868 | tf_op jit(solution)/shard_map/while
  1031.1 131.9 %reduce-scatter.22.cloned.1.call-start = ((), (), s32[]{:S(2)}) async-start(), calls=%async_computation.25 | async-start | bytes 1179648 | tf_op jit(solution)/shard_map/reduce_scatter | solution.py:297
  1035.6 150.8 %reduce-scatter.24.cloned.1.call-start = ((), (), s32[]{:S(2)}) async-start(), calls=%async_computation.26 | async-start | bytes 1179648 | tf_op jit(solution)/shard_map/reduce_scatter | solution.py:298
  1040.3 197.0 %reduce-scatter.20.cloned.1.call-start = ((), (), s32[]{:S(2)}) async-start(), calls=%async_computation.24 | async-start | bytes 4718592 | tf_op jit(solution)/shard_map/reduce_scatter | solution.py:296
  1047.0 241.3 %reduce-scatter.26.cloned.1.call-start = ((), (), s32[]{:S(2)}) async-start(), calls=%async_computation.27 | async-start | bytes 4718592 | tf_op jit(solution)/shard_map/reduce_scatter | solution.py:299
  1055.0 402.9 %reduce-scatter.28.cloned.1.call-start = ((), (), s32[]{:S(2)}) async-start(), calls=%async_computation.28 | async-start | bytes 18874368 | tf_op jit(solution)/shard_map/reduce_scatter | solution.py:254
  1070.4 557.0 %reduce-scatter.30.cloned.1.call-start = ((), (), s32[]{:S(2)}) async-start(), calls=%async_computation.29 | async-start | bytes 18874368 | tf_op jit(solution)/shard_map/reduce_scatter | solution.py:255
  1086.0 710.9 %reduce-scatter.32.cloned.1.call-start = ((), (), s32[]{:S(2)}) async-start(), calls=%async_computation.30 | async-start | bytes 18874368 | tf_op jit(solution)/shard_map/reduce_scatter | solution.py:256
  1101.5 16.1 copy-start.10
  1101.5 16.1 copy-start.30
  1101.5 16.1 copy-start.37
  1101.5 18.3 %copy-start.33 = (f32[2048]{0:T(1024)S(1)}, f32[2048]{0:T(1024)}, u32[]{:S(2)}) copy-start(f32[2048]{0:T(1024)} %get-tuple-element.162) | copy-start | bytes 24580
  1101.5 56.5 %copy-start.28 = (f32[8,1,256]{2,1,0:T(1,128)S(1)}, f32[8,1,256]{2,1,0:T(1,128)}, u32[]{:S(2)}) copy-start(f32[8,1,256]{2,1,0:T(1,128)} %copy-done.27) | copy-start | bytes 24580
  1101.5 56.4 %copy-start.35 = (f32[256]{0:T(256)S(1)}, f32[256]{0:T(256)}, u32[]{:S(2)}) copy-start(f32[256]{0:T(256)} %copy-done.34) | copy-start | bytes 3076
  1101.5 56.4 %copy-start.39 = (f32[256]{0:T(256)S(1)}, f32[256]{0:T(256)}, u32[]{:S(2)}) copy-start(f32[256]{0:T(256)} %copy-done.38) | copy-start | bytes 3076
  1101.5 56.4 %copy-start.9 = (f32[256,2048]{1,0:T(8,128)S(1)}, f32[256,2048]{1,0:T(8,128)}, u32[]{:S(2)}) copy-start(f32[256,2048]{1,0:T(8,128)} %copy-done.8) | copy-start | bytes 6291460
  (33 other events, 194.3 us)
Sparse Core Ops, SparseCore 0:
  9.6 36.1 all-gather.13
  48.3 51.8 all-gather.11
  101.7 30.5 all-gather.15
  146.6 86.3 reduce-scatter.11
  234.4 82.0 all-gather.19
  318.7 51.0 all-gather.17
  371.4 82.0 all-gather.21
  455.1 80.9 all-gather.23
  538.5 50.7 all-gather.25
  639.2 86.3 reduce-scatter.15
  728.6 86.3 reduce-scatter.13
  820.2 52.5 all-gather.27
  1031.2 86.3 reduce-scatter.17
  1120.2 32.5 reduce-scatter.21
  1155.6 30.8 reduce-scatter.23
  1189.1 48.0 reduce-scatter.19
  1240.0 48.3 reduce-scatter.25
  1291.2 166.6 reduce-scatter.27
  1460.8 166.6 reduce-scatter.29
  1630.2 166.6 reduce-scatter.31
where the time goes:
time: 1810 us; the launch traced here: 1800 us
  waiting for transfers between devices  1290 us (71%)
  matrix products  281 us (16%)
  blocking collectives  95.4 us (5%)
  local copies, waits for them, and re-layouts  61.6 us (3%)
  other arithmetic  49.3 us (3%)
    reduce_scatter x1, waiting for transfers between devices, per_device(): lax.psum_scatter(w_up_part, 'dp', scatter_dimension=0, tiled=True)  170 us
    reduce_scatter x1, waiting for transfers between devices, per_device(): lax.psum_scatter(w_gate_part, 'dp', scatter_dimension=0, tiled=True)  169 us
    reduce_scatter x1, waiting for transfers between devices, per_device(): lax.psum_scatter(w_down_part, 'dp', scatter_dimension=1, tiled=True)  169 us
    reduce_scatter x1, waiting for transfers between devices, per_device(): lax.psum_scatter(jnp.dot(rows_part, complete_down_weight, preferred_eleme...  86.7 us
    all_gather x1, waiting for transfers between devices, mlp_params(): lax.all_gather(w_gate, 'dp', axis=0, tiled=True)  75.9 us
    reduce_scatter x1, waiting for transfers between devices, per_device(): lax.psum_scatter(jnp.dot(rows_part, full_output, preferred_element_type=j...  74 us
    reduce_scatter x1, waiting for transfers between devices, per_device(): lax.psum_scatter(jnp.dot(grad_gate, full_gate.T, preferred_element_type=j...  71.9 us
    all_gather x1, waiting for transfers between devices, mlp_params(): lax.all_gather(w_up, 'dp', axis=0, tiled=True)  68.9 us
  transfers between devices with their start and end apart: 20, of which 17 were waited for; matrix products, arithmetic and copies ran while one was open for 10% of the time, Pallas kernels for 0%

commit v1 on v0

v1 whole, which is shorter than its diff:
```python
import jax
import jax.numpy as jnp
from jax import lax
from jax.sharding import PartitionSpec as P


HEAD_SIZE = 64
QBLK = 512


epsilon = 1e-05
rope_base = 500000.0


def layout(lengths, total_rows):
    row_index = jnp.arange(total_rows, dtype=jnp.int32)
    doc_ends = jnp.cumsum(lengths)
    passed = doc_ends[None, :] <= row_index[:, None]
    document_segment = jnp.sum(passed.astype(jnp.int32), axis=1)
    doc_start = jnp.sum(jnp.where(passed, lengths[None, :], 0), axis=1)
    positions = (row_index - doc_start).astype(jnp.float32)
    valid_rows = (document_segment < lengths.shape[0]).astype(jnp.float32)
    return (document_segment, positions, valid_rows)


def rope_tables(positions, head_dim):
    half_dim = head_dim // 2
    inverse_freq = rope_base ** (-(jnp.arange(half_dim, dtype=jnp.float32) * 2.0 / head_dim))
    angles = positions[:, None] * inverse_freq[None, :]
    return (jnp.cos(angles)[:, None, :], jnp.sin(angles)[:, None, :])


def rotate(tensor, cosine, sine_part, direction):
    half_dim = tensor.shape[-1] // 2
    first_half = tensor[..., :half_dim]
    second_half = tensor[..., half_dim:]
    return jnp.concatenate(
        [
            first_half * cosine - direction * second_half * sine_part,
            second_half * cosine + direction * first_half * sine_part,
        ],
        axis=-1,
    )


def rms_stats(hidden):
    scale_row = lax.rsqrt(jnp.mean(hidden * hidden, axis=-1, keepdims=True) + epsilon)
    return (scale_row, hidden * scale_row)


def norm_backward(grad_normed, unit_rows, scale_row, gain_wide):
    scaled = grad_normed * gain_wide
    return scale_row * (scaled - unit_rows * jnp.mean(scaled * unit_rows, axis=-1, keepdims=True))


def block_mask(document_segment, first_row, block_rows):
    row_index = jnp.arange(document_segment.shape[0], dtype=jnp.int32)
    query_rows = first_row + jnp.arange(block_rows, dtype=jnp.int32)
    query_segment = lax.dynamic_slice_in_dim(document_segment, first_row, block_rows, 0)
    return (query_segment[:, None] == document_segment[None, :]) & (
        row_index[None, :] <= query_rows[:, None]
    )


def attention_forward(queries, keys_rot, values, document_segment, block_rows):
    total_rows, kv_heads, group_size, head_dim = queries.shape
    score_scale = head_dim ** (-0.5)

    def one_block(block_index):
        first_row = block_index * block_rows
        query_block = lax.dynamic_slice_in_dim(queries, first_row, block_rows, 0)
        allowed = block_mask(document_segment, first_row, block_rows)
        scores = (
            jnp.einsum("qkgd,skd->kgqs", query_block, keys_rot, preferred_element_type=jnp.float32)
            * score_scale
        )
        scores = jnp.where(allowed, scores, -jnp.inf)
        row_max = jnp.max(scores, axis=-1, keepdims=True)
        log_total = row_max + jnp.log(jnp.sum(jnp.exp(scores - row_max), axis=-1, keepdims=True))
        weights = jnp.exp(scores - log_total).astype(jnp.bfloat16)
        attended = jnp.einsum("kgqs,skd->qkgd", weights, values, preferred_element_type=jnp.float32)
        return (attended.astype(jnp.bfloat16), log_total[..., 0])

    attended, log_total = lax.map(one_block, jnp.arange(total_rows // block_rows, dtype=jnp.int32))
    return (attended.reshape(total_rows, kv_heads, group_size, head_dim), log_total)


def attention_backward(
    queries, keys_rot, values, attended, grad_attended, log_total, document_segment, block_rows
):
    total_rows, kv_heads, group_size, head_dim = queries.shape
    score_scale = head_dim ** (-0.5)

    def one_block(running, block_index):
        key_grad, value_grad = running
        first_row = block_index * block_rows
        query_block = lax.dynamic_slice_in_dim(queries, first_row, block_rows, 0)
        block_gradient = lax.dynamic_slice_in_dim(grad_attended, first_row, block_rows, 0)
        out_block = lax.dynamic_slice_in_dim(attended, first_row, block_rows, 0)
        allowed = block_mask(document_segment, first_row, block_rows)
        scores = (
            jnp.einsum("qkgd,skd->kgqs", query_block, keys_rot, preferred_element_type=jnp.float32)
            * score_scale
        )
        scores = jnp.where(allowed, scores, -jnp.inf)
        prob_full = jnp.exp(scores - log_total[block_index][..., None])
        weights = prob_full.astype(jnp.bfloat16)
        value_grad = value_grad + jnp.einsum(
            "kgqs,qkgd->skd", weights, block_gradient, preferred_element_type=jnp.float32
        )
        grad_probs = jnp.einsum(
            "qkgd,skd->kgqs", block_gradient, values, preferred_element_type=jnp.float32
        )
        row_delta = jnp.einsum(
            "qkgd,qkgd->kgq", block_gradient, out_block, preferred_element_type=jnp.float32
        )
        grad_scores = (prob_full * (grad_probs - row_delta[..., None])).astype(jnp.bfloat16)
        query_grad = (
            jnp.einsum("kgqs,skd->qkgd", grad_scores, keys_rot, preferred_element_type=jnp.float32)
            * score_scale
        )
        key_grad = (
            key_grad
            + jnp.einsum(
                "kgqs,qkgd->skd", grad_scores, query_block, preferred_element_type=jnp.float32
            )
            * score_scale
        )
        return ((key_grad, value_grad), query_grad)

    zero_keys = jnp.zeros((total_rows, kv_heads, head_dim), jnp.float32)
    (key_grad, value_grad), query_grad = lax.scan(
        one_block, (zero_keys, zero_keys), jnp.arange(total_rows // block_rows, dtype=jnp.int32)
    )
    return (query_grad.reshape(total_rows, kv_heads * group_size, head_dim), key_grad, value_grad)


def shift_pairs(count, mask):
    return [(i, i ^ mask) for i in range(count)]


def gather_rows_plain(block, axis):
    count = lax.axis_size(axis)
    if count != 4:
        return lax.all_gather(block, axis, axis=0, tiled=True)
    me = lax.axis_index(axis)
    rows = block.shape[0]
    half = rows // 2
    from_x = lax.ppermute(block, axis, shift_pairs(count, 1))
    from_y = lax.ppermute(block, axis, shift_pairs(count, 2))
    far_top = lax.ppermute(from_x[:half], axis, shift_pairs(count, 2))
    far_low = lax.ppermute(from_y[half:], axis, shift_pairs(count, 1))
    whole = jnp.zeros((count * rows, block.shape[1]), block.dtype)
    for mask, piece, extra in (
        (0, block, 0),
        (1, from_x, 0),
        (2, from_y, 0),
        (3, far_top, 0),
        (3, far_low, half),
    ):
        whole = lax.dynamic_update_slice(whole, piece, ((me ^ mask) * rows + extra, 0))
    return whole


def scatter_rows_plain(partial, axis):
    count = lax.axis_size(axis)
    if count != 4:
        return lax.psum_scatter(partial, axis, scatter_dimension=0, tiled=True).astype(jnp.float32)
    me = lax.axis_index(axis)
    rows = partial.shape[0] // count
    half = rows // 2

    def part(mask, extra):
        return lax.dynamic_slice_in_dim(partial, (me ^ mask) * rows + extra, half, 0)

    def send(piece, mask):
        return lax.ppermute(piece, axis, shift_pairs(count, mask))

    relay_top = send(part(3, 0), 1).astype(jnp.float32)
    relay_low = send(part(3, half), 2).astype(jnp.float32)
    near_top = send(part(1, 0), 1).astype(jnp.float32)
    near_low = send(part(2, half), 2).astype(jnp.float32)
    joined_top = send((part(2, 0) + relay_top).astype(jnp.bfloat16), 2).astype(jnp.float32)
    joined_low = send((part(1, half) + relay_low).astype(jnp.bfloat16), 1).astype(jnp.float32)
    return jnp.concatenate(
        [part(0, 0) + near_top + joined_top, part(0, half) + near_low + joined_low], axis=0
    )


def product(left, right):
    return jnp.dot(left, right, preferred_element_type=jnp.float32)


def ordered(*values):
    return lax.optimization_barrier(values)


def sum_shards(partial, dimension):
    return lax.psum_scatter(partial, "dp", scatter_dimension=dimension, tiled=True)


def narrow(value):
    return value.astype(jnp.bfloat16)


def whole_block(
    inputs,
    doc_lengths,
    attn_gain,
    w_query,
    w_key,
    value_weight,
    w_output,
    mlp_gain,
    w_gate,
    w_up,
    w_down,
    out_grad,
):
    tensor_rank = lax.axis_index("tensor")
    own_rows = inputs.shape[0]
    total_rows = own_rows * lax.axis_size("tensor")
    query_cols, key_cols = w_query.shape[1], w_key.shape[1]
    joint = query_cols + 2 * key_cols
    document_segment, positions, valid_rows = layout(doc_lengths[0], total_rows)
    valid_own = lax.dynamic_slice_in_dim(valid_rows, tensor_rank * own_rows, own_rows, 0)[:, None]
    cosine, sine_part = rope_tables(positions, HEAD_SIZE)
    gains = jnp.pad(jnp.stack([attn_gain, mlp_gain], axis=1), ((0, 0), (0, 126)))
    packed = lax.all_gather(
        jnp.concatenate([w_query, w_key, value_weight, gains], axis=1), "dp", axis=0, tiled=True
    )
    full_joint = packed[:, :joint]
    gain_one = packed[:, joint].astype(jnp.float32)
    gain_two = packed[:, joint + 1].astype(jnp.float32)
    full_output = lax.all_gather(w_output, "dp", axis=1, tiled=True)
    full_gate = lax.all_gather(w_gate, "dp", axis=0, tiled=True)
    full_up = lax.all_gather(w_up, "dp", axis=0, tiled=True)
    full_down = lax.all_gather(w_down, "dp", axis=1, tiled=True)

    grad_out = out_grad.astype(jnp.float32)
    head_count = query_cols // HEAD_SIZE
    kv_heads = key_cols // HEAD_SIZE
    group_size = head_count // kv_heads
    residual = inputs.astype(jnp.float32)
    scale_one, unit_one = rms_stats(residual)
    inputs_all = gather_rows_plain(inputs, "tensor")
    cotangent_all = gather_rows_plain(out_grad, "tensor")
    normed_one_all = narrow(rms_stats(inputs_all.astype(jnp.float32))[1] * gain_one)
    grad_mlp_all = cotangent_all * narrow(valid_rows)[:, None]
    joint_full = product(normed_one_all, full_joint)
    query_full = joint_full[:, :query_cols].reshape(total_rows, head_count, HEAD_SIZE)
    key_full = joint_full[:, query_cols : query_cols + key_cols].reshape(
        total_rows, kv_heads, HEAD_SIZE
    )
    queries = narrow(rotate(query_full, cosine, sine_part, 1.0)).reshape(
        total_rows, kv_heads, group_size, HEAD_SIZE
    )
    keys_rot = narrow(rotate(key_full, cosine, sine_part, 1.0))
    values = narrow(joint_full[:, query_cols + key_cols :]).reshape(total_rows, kv_heads, HEAD_SIZE)
    attended, log_total = attention_forward(queries, keys_rot, values, document_segment, QBLK)
    attended_flat = attended.reshape(total_rows, query_cols)
    attn_out = scatter_rows_plain(narrow(product(attended_flat, full_output)), "tensor")
    hidden = residual + valid_own * attn_out
    scale_two, unit_two = rms_stats(hidden)
    normed_two_all = gather_rows_plain(narrow(unit_two * gain_two), "tensor")
    gate_pre = product(normed_two_all, full_gate)
    up_proj = product(normed_two_all, full_up)
    sigmoid_gate = jax.nn.sigmoid(gate_pre)
    activation = narrow(gate_pre * sigmoid_gate * up_proj)
    down_part = narrow(product(activation.T, grad_mlp_all))
    gate_pre, up_proj, down_part = ordered(gate_pre, up_proj, down_part)
    w_down_grad = sum_shards(down_part, 1)
    sigmoid_gate = jax.nn.sigmoid(gate_pre)
    grad_act = product(grad_mlp_all, full_down.T)
    grad_gate = narrow(grad_act * up_proj * sigmoid_gate * (1.0 + gate_pre * (1.0 - sigmoid_gate)))
    grad_up = narrow(grad_act * gate_pre * sigmoid_gate)
    normed_part = narrow(product(grad_gate, full_gate.T) + product(grad_up, full_up.T))
    grad_gate, grad_up, normed_part = ordered(grad_gate, grad_up, normed_part)
    grad_normed_two = scatter_rows_plain(normed_part, "tensor")
    gate_part = narrow(product(normed_two_all.T, grad_gate))
    up_part = narrow(product(normed_two_all.T, grad_up))
    grad_normed_two, gate_part, up_part = ordered(grad_normed_two, gate_part, up_part)
    w_gate_grad = sum_shards(gate_part, 0)
    w_up_grad = sum_shards(up_part, 0)
    mlp_gain_part = jnp.sum(grad_normed_two * unit_two, axis=0)
    grad_hidden = grad_out + norm_backward(grad_normed_two, unit_two, scale_two, gain_two)
    grad_attn = narrow(grad_hidden * valid_own)
    activation, grad_attn = ordered(activation, grad_attn)
    grad_attn_all = gather_rows_plain(grad_attn, "tensor")
    mlp_part = narrow(product(activation, full_down))
    grad_attn_all, mlp_part = ordered(grad_attn_all, mlp_part)
    mlp_out = scatter_rows_plain(mlp_part, "tensor")
    output = hidden + valid_own * mlp_out
    w_output_grad = sum_shards(narrow(product(attended_flat.T, grad_attn_all)), 1)
    grad_attended = narrow(product(grad_attn_all, full_output.T)).reshape(
        total_rows, kv_heads, group_size, HEAD_SIZE
    )
    query_grad, key_grad, value_grad = attention_backward(
        queries, keys_rot, values, attended, grad_attended, log_total, document_segment, QBLK
    )
    joint_back = jnp.concatenate(
        [
            narrow(rotate(query_grad, cosine, sine_part, -1.0)).reshape(total_rows, query_cols),
            narrow(rotate(key_grad, cosine, sine_part, -1.0)).reshape(total_rows, key_cols),
            narrow(value_grad).reshape(total_rows, key_cols),
        ],
        axis=1,
    )
    joint_grad = sum_shards(narrow(product(normed_one_all.T, joint_back)), 0).astype(jnp.float32)
    grad_normed_one = scatter_rows_plain(narrow(product(joint_back, full_joint.T)), "tensor")
    attn_gain_part = jnp.sum(grad_normed_one * unit_one, axis=0)
    input_grad = grad_hidden + norm_backward(grad_normed_one, unit_one, scale_one, gain_one)
    gain_sums = lax.psum(jnp.stack([attn_gain_part, mlp_gain_part]), ("dp", "tensor"))
    gain_rows = attn_gain.shape[0]
    gain_own = lax.dynamic_slice_in_dim(gain_sums, lax.axis_index("dp") * gain_rows, gain_rows, 1)
    return (
        output,
        input_grad,
        gain_own[0],
        joint_grad[:, :query_cols],
        joint_grad[:, query_cols : query_cols + key_cols],
        joint_grad[:, query_cols + key_cols :],
        w_output_grad.astype(jnp.float32),
        gain_own[1],
        w_gate_grad.astype(jnp.float32),
        w_up_grad.astype(jnp.float32),
        w_down_grad.astype(jnp.float32),
    )


def solution(mesh):
    placed = (
        P(("dp", "tensor"), None),
        P("dp", None),
        P("dp"),
        P("dp", "tensor"),
        P("dp", "tensor"),
        P("dp", "tensor"),
        P("tensor", "dp"),
        P("dp"),
        P("dp", "tensor"),
        P("dp", "tensor"),
        P("tensor", "dp"),
        P(("dp", "tensor"), None),
    )
    return jax.shard_map(
        whole_block,
        mesh=mesh,
        in_specs=placed,
        out_specs=(
            P(("dp", "tensor"), None),
            P(("dp", "tensor"), None),
            P("dp"),
            P("dp", "tensor"),
            P("dp", "tensor"),
            P("dp", "tensor"),
            P("tensor", "dp"),
            P("dp"),
            P("dp", "tensor"),
            P("dp", "tensor"),
            P("tensor", "dp"),
        ),
        check_vma=False,
    )
```

time: 1810 us -> 963 us (0.53)
  waiting for transfers between devices: 1290 us -> 410 us
  blocking collectives: 95.4 us -> 41 us
  local copies, waits for them, and re-layouts: 61.6 us -> 113 us
  starting transfers between devices: 1.27 us -> 48.1 us
  matrix products: 281 us -> 248 us
  other arithmetic: 49.3 us -> 67.6 us
    reduce_scatter x11 -> x5, waiting for transfers between devices: 881 us -> 167 us  [sum_shards(): lax.psum_scatter(partial, 'dp', scatter_dimension=dimension, tiled=True)]
    all_gather x9 -> x5, waiting for transfers between devices: 407 us -> 69.4 us  [the longest x1 50.2 us: whole_block(): full_down = lax.all_gather(w_down, 'dp', axis=1, tiled=True)]
    ppermute x0 -> x40, waiting for transfers between devices: none -> 170 us  [the longest x24 96.2 us: send(): return lax.ppermute(piece, axis, shift_pairs(count, mask))]
    all_gather x4 -> x0, blocking collectives: 57.4 us -> none  [the longest x1 17.3 us: attn_params(): lax.all_gather(w_key, 'dp', axis=0, tiled=True)]
    ppermute x0 -> x40, starting transfers between devices: none -> 47.7 us  [the longest x24 27 us: send(): return lax.ppermute(piece, axis, shift_pairs(count, mask))]
    psum x1, blocking collectives: 9.46 us -> 41 us  [whole_block(): lax.psum(jnp.stack([attn_gain_part, mlp_gain_part]), ('dp', 'tensor'))]
    dot_general x21 -> x15, matrix products: 196 us -> 166 us  [product(): return jnp.dot(left, right, preferred_element_type=jnp.float32)]
    unnamed x1 -> x0, blocking collectives: 28.5 us -> none
  transfers between devices with their start and end apart: 20 -> 50, of which waited for: 17 -> 26; matrix products, arithmetic and copies ran while one was open for 10% -> 37% of each run, Pallas kernels for 0% -> 0%
where the time goes in v1:
time: 963 us; the launch traced here: 950 us
  waiting for transfers between devices  410 us (43%)
  matrix products  248 us (26%)
  local copies, waits for them, and re-layouts  113 us (12%)
  other arithmetic  67.6 us (7%)
  starting transfers between devices  48.1 us (5%)
  blocking collectives  41 us (4%)
  between operations  15.6 us (2%)
    reduce_scatter x5, waiting for transfers between devices, sum_shards(): lax.psum_scatter(partial, 'dp', scatter_dimension=dimension, tiled=True)  167 us
    dot_general x15, matrix products, product(): return jnp.dot(left, right, preferred_element_type=jnp.float32)  166 us
    ppermute x24, waiting for transfers between devices, send(): return lax.ppermute(piece, axis, shift_pairs(count, mask))  96.2 us
    all_gather x1, waiting for transfers between devices, whole_block(): full_down = lax.all_gather(w_down, 'dp', axis=1, tiled=True)  50.2 us
    ppermute x4, waiting for transfers between devices, gather_rows_plain(): from_x = lax.ppermute(block, axis, shift_pairs(count, 1))  42.5 us
    dynamic_update_slice x4, local copies, waits for them, and re-layouts, attention_backward(): lax.scan(one_block, (zero_keys, zero_keys), jnp.arange(total_rows // bloc...  41.4 us
    psum x1, blocking collectives, whole_block(): lax.psum(jnp.stack([attn_gain_part, mlp_gain_part]), ('dp', 'tensor'))  41 us
    ppermute x24, starting transfers between devices, send(): return lax.ppermute(piece, axis, shift_pairs(count, mask))  27 us
  transfers between devices with their start and end apart: 50, of which 26 were waited for; matrix products, arithmetic and copies ran while one was open for 37% of the time, Pallas kernels for 0%

profile of v1, /device:TPU:0, one launch (start us, length us, event | category | flops | bytes accessed | tf_op | source)
XLA Modules:
  0.0 950.3 jit_solution(13734686200592428553)
XLA Ops:
  21.2 17.9 %collective-permute-done = bf16[256,2048]{1,0:T(8,128)(2,1)S(1)} collective-permute-done((bf16[256,2048]{1,0:T(8,128)(2,1)}, bf16[256,2048]{1,0:T(8,128)(2,1)S(1)}, u32[]{:S(2)}, u32[]{:S(2)}) %collective-permute-start) | collective-permute-done | bytes 1048608 | tf_op jit(solution)/shard_map/ppermute | solution.py:149
  48.9 4.5 collective-permute-done.2
  63.1 6.9 fusion.66
  71.4 27.3 %while.27 = (s32[]{:T(128)}, bf16[2,512,2,4,64]{1,4,3,2,0:T(8,128)(2,1)S(1)}, f32[2,2,4,512]{3,2,1,0:T(4,128)S(1)}, s32[2]{0:T(128)S(1)}, s32[1024]{0:T(1024)S(1...) while((s32[]{:T(128)}, ...), condition=%wide.region_7.8_spmd, body=%wide.region_4.7_spmd.sunk | while | flops 1121710592 | bytes 55195868 | solution.py:84
  109.1 12.3 %collective-permute-done.5 = bf16[128,2048]{1,0:T(8,128)(2,1)S(1)} collective-permute-done((bf16[128,2048]{1,0:T(8,128)(2,1)S(1)}, bf16[128,2048]{1,0:T(8,128)(2,1)S(1)}, u32[]{:S(2)}, u32[]{:S(2)}) %collective-permute-start.5) | collective-permute-done | bytes 524320 | tf_op jit(solution)/shard_map/ppermute | solution.py:177
  124.4 5.2 collective-permute-done.4
  131.2 6.3 collective-permute-done.6
  143.0 5.7 collective-permute-done.7
  148.7 6.8 collective-permute-done.9
  163.7 14.2 %collective-permute-done.14 = bf16[256,2048]{1,0:T(8,128)(2,1)} collective-permute-done((bf16[256,2048]{1,0:T(8,128)(2,1)S(1)}, bf16[256,2048]{1,0:T(8,128)(2,1)}, u32[]{:S(2)}, u32[]{:S(2)}) %collective-permute-start.14) | collective-permute-done | bytes 1048608 | tf_op jit(solution)/shard_map/ppermute | solution.py:149
  197.2 9.9 %collective-permute-done.17 = bf16[128,2048]{1,0:T(8,128)(2,1)S(1)} collective-permute-done((bf16[128,2048]{1,0:T(8,128)(2,1)S(1)}, bf16[128,2048]{1,0:T(8,128)(2,1)S(1)}, u32[]{:S(2)}, u32[]{:S(2)}) %collective-permute-start.17) | collective-permute-done | bytes 524320 | tf_op jit(solution)/shard_map/ppermute | solution.py:152
  212.3 4.9 collective-permute-done.13
  218.0 14.6 %fusion.86 = f32[1024,2048]{1,0:T(8,128)} fusion(bf16[1024,2048]{1,0:T(8,128)(2,1)} %constant_dynamic-update-slice_fusion.10, bf16[2048,2048]{1,0:T(8,128)(2,1)} %all-gather.10.cloned.1.call-done), kind=kOutput, calls=%fused_computation.204 | convolution fusion | flops 8589934592 | bytes 20971520 | tf_op jit(solution)/shard_map/dot_general | solution.py:191
  232.7 19.1 %all-gather.12.cloned.1.call-done = bf16[2048,2048]{1,0:T(8,128)(2,1)} async-done(((bf16[256,2048]{1,0:T(8,128)(2,1)}), bf16[2048,2048]{1,0:T(8,128)(2,1)}) %all-gather.12.cloned.1.call-update) | async-done | bytes 8388624 | tf_op jit(solution)/shard_map/all_gather | solution.py:237
  251.8 16.6 %multiply_convert_fusion.2 = (bf16[1024,2048]{1,0:T(8,128)(2,1)S(1)}, f32[1024,2048]{1,0:T(8,128)}) fusion(f32[1024,2048]{1,0:T(8,128)} %fusion.86, bf16[1024,2048]{1,0:T(8,128)(2,1)} %constant_dynamic-update-slice_fusion.10, bf16[2048,2048]{1,0:T(8,128)(2,1)} %all-gather.12.cloned.1.call-done), kind=kOutput, calls=%fused_computation.70 | convolution fusion | flops 8602517504 | bytes 33554432 | tf_op jit(solution)/shard_map/dot_general | solution.py:191
  270.4 13.6 %convolution_convert_fusion.2 = bf16[2048,2048]{1,0:T(8,128)(2,1)} fusion(bf16[1024,2048]{1,0:T(8,128)(2,1)S(1)} %get-tuple-element.139, bf16[1024,2048]{1,0:T(8,128)(2,1)} %constant_dynamic-update-slice_fusion.5, bf16[1024]{0:T(1024)(128)(2,1)S(1)} %get-tuple-element.288), kind=kOutput, calls=%fused_computation.73 | convolution fusion | flops 8596226048 | bytes 16779264 | tf_op jit(solution)/shard_map/dot_general | solution.py:191
  284.0 50.2 %all-gather.14.cloned.1.call-done = bf16[2048,2048]{1,0:T(8,128)(2,1)} async-done(((bf16[2048,256]{1,0:T(8,128)(2,1)}), bf16[2048,2048]{1,0:T(8,128)(2,1)}) %all-gather.14.cloned.1.call-update) | async-done | bytes 8388624 | tf_op jit(solution)/shard_map/all_gather | solution.py:238
  334.2 23.0 %multiply_convert_fusion = (bf16[1024,2048]{1,0:T(8,128)(2,1)}, bf16[1024,2048]{1,0:T(8,128)(2,1)}) fusion(f32[1024,2048]{1,0:T(8,128)} %fusion.86, f32[1024,2048]{1,0:T(8,128)} %get-tuple-element.132, bf16[2048,2048]{1,0:T(8,128)(2,1)} %all-gather.14.cloned.1.call-done, bf16[1024,2048]{1,0:T(8,128)(2,1)} %constant_dynamic-update-slice_fusion.5, ...), kind=kOutput, calls=%fused_computation.67 | convolution fusion | flops 8619294720 | bytes 37750784 | tf_op jit(solution)/shard_map/dot_general | solution.py:191
  357.2 12.7 %fusion.87 = f32[1024,2048]{1,0:T(8,128)S(1)} fusion(bf16[1024,2048]{1,0:T(8,128)(2,1)} %get-tuple-element.135, bf16[2048,2048]{1,0:T(8,128)(2,1)} %all-gather.10.cloned.1.call-done), kind=kOutput, calls=%fused_computation.205 | convolution fusion | flops 8589934592 | bytes 20971520 | tf_op jit(solution)/shard_map/dot_general | solution.py:191
  369.9 11.7 %add_convert_fusion = bf16[1024,2048]{1,0:T(8,128)(2,1)S(1)} fusion(f32[1024,2048]{1,0:T(8,128)S(1)} %fusion.87, bf16[1024,2048]{1,0:T(8,128)(2,1)S(1)} %copy-done.58, bf16[2048,2048]{1,0:T(8,128)(2,1)} %all-gather.12.cloned.1.call-done), kind=kOutput, calls=%fused_computation.66 | convolution fusion | flops 8594128896 | bytes 25165824 | tf_op jit(solution)/shard_map/dot_general | solution.py:191
  390.8 8.8 collective-permute-done.19
  402.2 14.0 %convolution_convert_fusion = bf16[2048,2048]{1,0:T(8,128)(2,1)} fusion(bf16[1024,2048]{1,0:T(8,128)(2,1)} %constant_dynamic-update-slice_fusion.10, bf16[1024,2048]{1,0:T(8,128)(2,1)} %get-tuple-element.136), kind=kOutput, calls=%fused_computation.71 | convolution fusion | flops 8594128896 | bytes 16777216 | tf_op jit(solution)/shard_map/dot_general | solution.py:191
  421.0 13.8 %convolution_convert_fusion.1 = bf16[2048,2048]{1,0:T(8,128)(2,1)} fusion(bf16[1024,2048]{1,0:T(8,128)(2,1)} %constant_dynamic-update-slice_fusion.10, bf16[1024,2048]{1,0:T(8,128)(2,1)S(1)} %copy-done.61), kind=kOutput, calls=%fused_computation.72 | convolution fusion | flops 8594128896 | bytes 16777216 | tf_op jit(solution)/shard_map/dot_general | solution.py:191
  440.8 12.6 %convolution_convert_fusion.3 = bf16[1024,2048]{1,0:T(8,128)(2,1)} fusion(bf16[1024,2048]{1,0:T(8,128)(2,1)S(1)} %copy-done.60, bf16[2048,2048]{1,0:T(8,128)(2,1)} %all-gather.14.cloned.1.call-done), kind=kOutput, calls=%fused_computation.74 | convolution fusion | flops 8592031744 | bytes 16777216 | tf_op jit(solution)/shard_map/dot_general | solution.py:191
  453.3 8.5 collective-permute-done.24
  465.5 7.8 collective-permute-done.26
  480.5 5.2 convolution_convert_fusion.8
  485.7 131.0 %while.28 = (s32[]{:T(128)}, f32[1024,2,64]{0,2,1:T(8,128)}, f32[1024,2,64]{0,2,1:T(8,128)}, f32[2,512,2,4,64]{1,0,4,3,2:T(2,128)}, s32[2]{0:T(128)S(1)}, /*inde...) while((s32[]{:T(128)}, f32[1024,2,64]{0,2,1:T(8,128)}, ...), condition=%wide.region_12.13_spmd.clone, body=%wide.region_11.12_spmd.clone.sunk | while | flops 2729832960 | bytes 148257296 | solution.py:132
  494.1 8.2 fusion.148
  504.2 8.9 fusion.150
  517.5 19.6 %dynamic_update_slice.120 = f32[2,512,2,4,64]{1,0,4,3,2:T(2,128)} dynamic-update-slice(f32[2,512,2,4,64]{1,0,4,3,2:T(2,128)} %get-tuple-element.478, f32[1,512,2,4,64]{1,0,4,3,2:T(1,128)S(1)} %copy.61, s32[]{:T(128)} %get-tuple-element.475, s32[]{:T(128)} %constant.53.clone.1..sunk.1, s32[]{:T(128)} %constant.53.clone.1..sunk.1, s32[]{:T(128)} %constant.53.clone.1..sunk.1, s32[]{:T(128)} %constant.53.clone.1..sunk.1) | dynamic-update-slice | bytes 2097156 | tf_op jit(solution)/shard_map/while/body/jit(dynamic_update_index_in_dim)/dynamic_update_slice | solution.py:132
  537.1 5.1 fusion.151
  542.3 8.9 fusion.152
  559.3 8.2 fusion.148
  569.4 8.9 fusion.150
  582.7 19.6 %dynamic_update_slice.120 = f32[2,512,2,4,64]{1,0,4,3,2:T(2,128)} dynamic-update-slice(f32[2,512,2,4,64]{1,0,4,3,2:T(2,128)} %get-tuple-element.478, f32[1,512,2,4,64]{1,0,4,3,2:T(1,128)S(1)} %copy.61, s32[]{:T(128)} %get-tuple-element.475, s32[]{:T(128)} %constant.53.clone.1..sunk.1, s32[]{:T(128)} %constant.53.clone.1..sunk.1, s32[]{:T(128)} %constant.53.clone.1..sunk.1, s32[]{:T(128)} %constant.53.clone.1..sunk.1) | dynamic-update-slice | bytes 2097156 | tf_op jit(solution)/shard_map/while/body/jit(dynamic_update_index_in_dim)/dynamic_update_slice | solution.py:132
  602.3 5.1 fusion.151
  607.4 9.1 fusion.152
  621.5 7.7 convolution_convert_fusion.6
  631.3 5.7 convolution_convert_fusion.5
  646.2 8.6 collective-permute-done.35
  657.1 16.3 %collective-permute-done.29 = bf16[128,2048]{1,0:T(8,128)(2,1)S(1)} collective-permute-done((bf16[128,2048]{1,0:T(8,128)(2,1)S(1)}, bf16[128,2048]{1,0:T(8,128)(2,1)S(1)}, u32[]{:S(2)}, u32[]{:S(2)}) %collective-permute-start.29) | collective-permute-done | bytes 524320 | tf_op jit(solution)/shard_map/ppermute | solution.py:177
  680.2 5.2 collective-permute-done.28
  691.3 16.8 %collective-permute-done.30 = bf16[128,2048]{1,0:T(8,128)(2,1)S(1)} collective-permute-done((bf16[128,2048]{1,0:T(8,128)(2,1)S(1)}, bf16[128,2048]{1,0:T(8,128)(2,1)S(1)}, u32[]{:S(2)}, u32[]{:S(2)}) %collective-permute-start.30) | collective-permute-done | bytes 524320 | tf_op jit(solution)/shard_map/ppermute | solution.py:177
  713.6 41.0 %psum.7 = f32[2,2048]{1,0:T(2,128)S(1)} all-reduce(f32[2,2048]{1,0:T(2,128)S(1)} %pad_maximum_fusion.9), channel_id=1, replica_groups=mesh['dp'=8,'tensor'=4] {'dp','tensor'}, use_global_device_ids=true, to_apply=%region_16.17 | all-reduce | flops 4096 | bytes 32768 | tf_op jit(solution)/shard_map/psum | solution.py:313
  756.8 6.1 fusion.71
  770.9 79.2 %reduce-scatter.10.cloned.1.call-done = bf16[256,2048]{1,0:T(8,128)(2,1)} async-done(((bf16[2048,2048]{1,0:T(8,128)(2,1)}), bf16[256,2048]{1,0:T(8,128)(2,1)}) %reduce-scatter.10.cloned.1.call-update) | async-done | bytes 1048592 | tf_op jit(solution)/shard_map/reduce_scatter | solution.py:199
  852.9 87.4 %reduce-scatter.12.cloned.1.call-done = bf16[256,2048]{1,0:T(8,128)(2,1)} async-done(((bf16[2048,2048]{1,0:T(8,128)(2,1)}), bf16[256,2048]{1,0:T(8,128)(2,1)}) %reduce-scatter.12.cloned.1.call-update) | async-done | bytes 1048592 | tf_op jit(solution)/shard_map/reduce_scatter | solution.py:199
  (374 shorter events, 225.1 us)
Async XLA Ops:
  7.2 53.5 %all-gather.6.cloned.1.call-start = ((), (), s32[]{:S(2)}) async-start(), calls=%async_computation.5 | async-start | bytes 4128768 | tf_op jit(solution)/shard_map/all_gather | solution.py:229
  10.6 90.5 %all-gather.8.cloned.1.call-start = ((), (), s32[]{:S(2)}) async-start(), calls=%async_computation.6 | async-start | bytes 2359296 | tf_op jit(solution)/shard_map/all_gather | solution.py:235
  11.3 206.7 %all-gather.10.cloned.1.call-start = ((), (), s32[]{:S(2)}) async-start(), calls=%async_computation.7 | async-start | bytes 9437184 | tf_op jit(solution)/shard_map/all_gather | solution.py:236
  12.1 239.7 %all-gather.12.cloned.1.call-start = ((), (), s32[]{:S(2)}) async-start(), calls=%async_computation.8 | async-start | bytes 9437184 | tf_op jit(solution)/shard_map/all_gather | solution.py:237
  12.6 321.6 %all-gather.14.cloned.1.call-start = ((), (), s32[]{:S(2)}) async-start(), calls=%async_computation.9 | async-start | bytes 9437184 | tf_op jit(solution)/shard_map/all_gather | solution.py:238
  12.7 26.4 %collective-permute-start = (bf16[256,2048]{1,0:T(8,128)(2,1)}, bf16[256,2048]{1,0:T(8,128)(2,1)S(1)}, u32[]{:S(2)}, u32[]{:S(2)}) collective-permute-start(bf16[256,2048]{1,0:T(8,128)(2,1)} %param.16), channel_id=1, source_target_pairs={{0,1},{1,0},{2,3},{3,2},{4,5},{5,4},{6,7},{7,6},{8,9},{9,8},{10,11... | collective-permute-start | bytes 3145736 | tf_op jit(solution)/shard_map/ppermute | solution.py:149
  15.7 27.2 %collective-permute-start.1 = (bf16[256,2048]{1,0:T(8,128)(2,1)}, bf16[256,2048]{1,0:T(8,128)(2,1)}, u32[]{:S(2)}, u32[]{:S(2)}) collective-permute-start(bf16[256,2048]{1,0:T(8,128)(2,1)} %param.16), channel_id=1, source_target_pairs={{0,2},{1,3},{2,0},{3,1},{4,6},{5,7},{6,4},{7,5},{8,10},{9,11},{10,... | collective-permute-start | bytes 3145736 | tf_op jit(solution)/shard_map/ppermute | solution.py:150
  17.3 745.7 %reduce-scatter.8.cloned.1.call-start = ((), (), s32[]{:S(2)}) async-start(), calls=%async_computation.11 | async-start | bytes 2359296 | tf_op jit(solution)/shard_map/reduce_scatter | solution.py:199
  39.9 13.5 %collective-permute-start.2 = (bf16[128,2048]{1,0:T(8,128)(2,1)}, bf16[128,2048]{1,0:T(8,128)(2,1)}, u32[]{:S(2)}, u32[]{:S(2)}) collective-permute-start(bf16[128,2048]{1,0:T(8,128)(2,1)} %slice.109), channel_id=1, source_target_pairs={{0,2},{1,3},{2,0},{3,1},{4,6},{5,7},{6,4},{7,5},{8,10},{9,11},{10,... | collective-permute-start | bytes 1572872 | tf_op jit(solution)/shard_map/ppermute | solution.py:151
  44.0 12.7 %collective-permute-start.3 = (bf16[128,2048]{1,0:T(8,128)(2,1)S(1)}, bf16[128,2048]{1,0:T(8,128)(2,1)S(1)}, u32[]{:S(2)}, u32[]{:S(2)}) collective-permute-start(bf16[128,2048]{1,0:T(8,128)(2,1)S(1)} %slice.110), channel_id=1, source_target_pairs={{0,1},{1,0},{2,3},{3,2},{4,5},{5,4},{6,7},{7,6},{8,9},{9,8},{10,11... | collective-permute-start | bytes 1572872 | tf_op jit(solution)/shard_map/ppermute | solution.py:152
  106.6 14.8 %collective-permute-start.5 = (bf16[128,2048]{1,0:T(8,128)(2,1)S(1)}, bf16[128,2048]{1,0:T(8,128)(2,1)S(1)}, u32[]{:S(2)}, u32[]{:S(2)}) collective-permute-start(bf16[128,2048]{1,0:T(8,128)(2,1)S(1)} %get-tuple-element.269), channel_id=1, source_target_pairs={{0,1},{1,0},{2,3},{3,2},{4,5},{5,4},{6,7},{7,6},{8,9},{9,8},{10,11... | collective-permute-start | bytes 1572872 | tf_op jit(solution)/shard_map/ppermute | solution.py:177
  108.1 21.5 %collective-permute-start.4 = (bf16[128,2048]{1,0:T(8,128)(2,1)}, bf16[128,2048]{1,0:T(8,128)(2,1)S(1)}, u32[]{:S(2)}, u32[]{:S(2)}) collective-permute-start(bf16[128,2048]{1,0:T(8,128)(2,1)} %get-tuple-element.266), channel_id=1, source_target_pairs={{0,1},{1,0},{2,3},{3,2},{4,5},{5,4},{6,7},{7,6},{8,9},{9,8},{10,11... | collective-permute-start | bytes 1572872 | tf_op jit(solution)/shard_map/ppermute | solution.py:177
  108.7 20.9 %collective-permute-start.8 = (bf16[128,2048]{1,0:T(8,128)(2,1)}, bf16[128,2048]{1,0:T(8,128)(2,1)S(1)}, u32[]{:S(2)}, u32[]{:S(2)}) collective-permute-start(bf16[128,2048]{1,0:T(8,128)(2,1)} %get-tuple-element.267), channel_id=1, source_target_pairs={{0,2},{1,3},{2,0},{3,1},{4,6},{5,7},{6,4},{7,5},{8,10},{9,11},{10,... | collective-permute-start | bytes 1572872 | tf_op jit(solution)/shard_map/ppermute | solution.py:177
  122.3 15.1 %collective-permute-start.6 = (bf16[128,2048]{1,0:T(8,128)(2,1)}, bf16[128,2048]{1,0:T(8,128)(2,1)}, u32[]{:S(2)}, u32[]{:S(2)}) collective-permute-start(bf16[128,2048]{1,0:T(8,128)(2,1)} %add_convert_fusion.9), channel_id=1, source_target_pairs={{0,2},{1,3},{2,0},{3,1},{4,6},{5,7},{6,4},{7,5},{8,10},{9,11},{10,... | collective-permute-start | bytes 1572872 | tf_op jit(solution)/shard_map/ppermute | solution.py:177
  122.8 25.9 %collective-permute-start.7 = (bf16[128,2048]{1,0:T(8,128)(2,1)}, bf16[128,2048]{1,0:T(8,128)(2,1)}, u32[]{:S(2)}, u32[]{:S(2)}) collective-permute-start(bf16[128,2048]{1,0:T(8,128)(2,1)} %get-tuple-element.268), channel_id=1, source_target_pairs={{0,2},{1,3},{2,0},{3,1},{4,6},{5,7},{6,4},{7,5},{8,10},{9,11},{10,... | collective-permute-start | bytes 1572872 | tf_op jit(solution)/shard_map/ppermute | solution.py:177
  140.4 15.1 %collective-permute-start.9 = (bf16[128,2048]{1,0:T(8,128)(2,1)}, bf16[128,2048]{1,0:T(8,128)(2,1)}, u32[]{:S(2)}, u32[]{:S(2)}) collective-permute-start(bf16[128,2048]{1,0:T(8,128)(2,1)} %get-tuple-element.265), channel_id=1, source_target_pairs={{0,1},{1,0},{2,3},{3,2},{4,5},{5,4},{6,7},{7,6},{8,9},{9,8},{10,11... | collective-permute-start | bytes 1572872 | tf_op jit(solution)/shard_map/ppermute | solution.py:177
  141.9 36.1 %collective-permute-start.14 = (bf16[256,2048]{1,0:T(8,128)(2,1)S(1)}, bf16[256,2048]{1,0:T(8,128)(2,1)}, u32[]{:S(2)}, u32[]{:S(2)}) collective-permute-start(bf16[256,2048]{1,0:T(8,128)(2,1)S(1)} %copy-done.14), channel_id=1, source_target_pairs={{0,1},{1,0},{2,3},{3,2},{4,5},{5,4},{6,7},{7,6},{8,9},{9,8},{10,11... | collective-permute-start | bytes 3145736 | tf_op jit(solution)/shard_map/ppermute | solution.py:149
  142.4 42.4 %collective-permute-start.15 = (bf16[256,2048]{1,0:T(8,128)(2,1)S(1)}, bf16[256,2048]{1,0:T(8,128)(2,1)}, u32[]{:S(2)}, u32[]{:S(2)}) collective-permute-start(bf16[256,2048]{1,0:T(8,128)(2,1)S(1)} %copy-done.14), channel_id=1, source_target_pairs={{0,2},{1,3},{2,0},{3,1},{4,6},{5,7},{6,4},{7,5},{8,10},{9,11},{10,... | collective-permute-start | bytes 3145736 | tf_op jit(solution)/shard_map/ppermute | solution.py:150
  162.3 34.3 %collective-permute-start.10 = (bf16[256,2048]{1,0:T(8,128)(2,1)S(1)}, bf16[256,2048]{1,0:T(8,128)(2,1)S(1)}, u32[]{:S(2)}, u32[]{:S(2)}) collective-permute-start(bf16[256,2048]{1,0:T(8,128)(2,1)S(1)} %get-tuple-element.239), channel_id=1, source_target_pairs={{0,1},{1,0},{2,3},{3,2},{4,5},{5,4},{6,7},{7,6},{8,9},{9,8},{10,11... | collective-permute-start | bytes 3145736 | tf_op jit(solution)/shard_map/ppermute | solution.py:149
  179.1 14.6 %collective-permute-start.16 = (bf16[128,2048]{1,0:T(8,128)(2,1)S(1)}, bf16[128,2048]{1,0:T(8,128)(2,1)S(1)}, u32[]{:S(2)}, u32[]{:S(2)}) collective-permute-start(bf16[128,2048]{1,0:T(8,128)(2,1)S(1)} %slice.123), channel_id=1, source_target_pairs={{0,2},{1,3},{2,0},{3,1},{4,6},{5,7},{6,4},{7,5},{8,10},{9,11},{10,... | collective-permute-start | bytes 1572872 | tf_op jit(solution)/shard_map/ppermute | solution.py:151
  179.7 28.2 %collective-permute-start.11 = (bf16[256,2048]{1,0:T(8,128)(2,1)S(1)}, bf16[256,2048]{1,0:T(8,128)(2,1)S(1)}, u32[]{:S(2)}, u32[]{:S(2)}) collective-permute-start(bf16[256,2048]{1,0:T(8,128)(2,1)S(1)} %get-tuple-element.239), channel_id=1, source_target_pairs={{0,2},{1,3},{2,0},{3,1},{4,6},{5,7},{6,4},{7,5},{8,10},{9,11},{10,... | collective-permute-start | bytes 3145736 | tf_op jit(solution)/shard_map/ppermute | solution.py:150
  185.9 21.2 %collective-permute-start.17 = (bf16[128,2048]{1,0:T(8,128)(2,1)S(1)}, bf16[128,2048]{1,0:T(8,128)(2,1)S(1)}, u32[]{:S(2)}, u32[]{:S(2)}) collective-permute-start(bf16[128,2048]{1,0:T(8,128)(2,1)S(1)} %slice.124), channel_id=1, source_target_pairs={{0,1},{1,0},{2,3},{3,2},{4,5},{5,4},{6,7},{7,6},{8,9},{9,8},{10,11... | collective-permute-start | bytes 1572872 | tf_op jit(solution)/shard_map/ppermute | solution.py:152
  196.6 14.9 %collective-permute-start.12 = (bf16[128,2048]{1,0:T(8,128)(2,1)S(1)}, bf16[128,2048]{1,0:T(8,128)(2,1)S(1)}, u32[]{:S(2)}, u32[]{:S(2)}) collective-permute-start(bf16[128,2048]{1,0:T(8,128)(2,1)S(1)} %slice.121), channel_id=1, source_target_pairs={{0,2},{1,3},{2,0},{3,1},{4,6},{5,7},{6,4},{7,5},{8,10},{9,11},{10,... | collective-permute-start | bytes 1572872 | tf_op jit(solution)/shard_map/ppermute | solution.py:151
  384.7 14.8 %collective-permute-start.19 = (bf16[128,2048]{1,0:T(8,128)(2,1)S(1)}, bf16[128,2048]{1,0:T(8,128)(2,1)S(1)}, u32[]{:S(2)}, u32[]{:S(2)}) collective-permute-start(bf16[128,2048]{1,0:T(8,128)(2,1)S(1)} %get-tuple-element.263), channel_id=1, source_target_pairs={{0,1},{1,0},{2,3},{3,2},{4,5},{5,4},{6,7},{7,6},{8,9},{9,8},{10,11... | collective-permute-start | bytes 1572872 | tf_op jit(solution)/shard_map/ppermute | solution.py:177
  388.7 28.1 %collective-permute-start.18 = (bf16[128,2048]{1,0:T(8,128)(2,1)S(1)}, bf16[128,2048]{1,0:T(8,128)(2,1)S(1)}, u32[]{:S(2)}, u32[]{:S(2)}) collective-permute-start(bf16[128,2048]{1,0:T(8,128)(2,1)S(1)} %get-tuple-element.260), channel_id=1, source_target_pairs={{0,1},{1,0},{2,3},{3,2},{4,5},{5,4},{6,7},{7,6},{8,9},{9,8},{10,11... | collective-permute-start | bytes 1572872 | tf_op jit(solution)/shard_map/ppermute | solution.py:177
  389.3 27.5 %collective-permute-start.22 = (bf16[128,2048]{1,0:T(8,128)(2,1)S(1)}, bf16[128,2048]{1,0:T(8,128)(2,1)S(1)}, u32[]{:S(2)}, u32[]{:S(2)}) collective-permute-start(bf16[128,2048]{1,0:T(8,128)(2,1)S(1)} %get-tuple-element.261), channel_id=1, source_target_pairs={{0,2},{1,3},{2,0},{3,1},{4,6},{5,7},{6,4},{7,5},{8,10},{9,11},{10,... | collective-permute-start | bytes 1572872 | tf_op jit(solution)/shard_map/ppermute | solution.py:177
  400.7 16.1 %collective-permute-start.20 = (bf16[128,2048]{1,0:T(8,128)(2,1)S(1)}, bf16[128,2048]{1,0:T(8,128)(2,1)S(1)}, u32[]{:S(2)}, u32[]{:S(2)}) collective-permute-start(bf16[128,2048]{1,0:T(8,128)(2,1)S(1)} %add_convert_fusion.7), channel_id=1, source_target_pairs={{0,2},{1,3},{2,0},{3,1},{4,6},{5,7},{6,4},{7,5},{8,10},{9,11},{10,... | collective-permute-start | bytes 1572872 | tf_op jit(solution)/shard_map/ppermute | solution.py:177
  416.3 18.6 %collective-permute-start.21 = (bf16[128,2048]{1,0:T(8,128)(2,1)}, bf16[128,2048]{1,0:T(8,128)(2,1)}, u32[]{:S(2)}, u32[]{:S(2)}) collective-permute-start(bf16[128,2048]{1,0:T(8,128)(2,1)} %get-tuple-element.262), channel_id=1, source_target_pairs={{0,2},{1,3},{2,0},{3,1},{4,6},{5,7},{6,4},{7,5},{8,10},{9,11},{10,... | collective-permute-start | bytes 1572872 | tf_op jit(solution)/shard_map/ppermute | solution.py:177
  419.6 15.3 %collective-permute-start.23 = (bf16[128,2048]{1,0:T(8,128)(2,1)}, bf16[128,2048]{1,0:T(8,128)(2,1)}, u32[]{:S(2)}, u32[]{:S(2)}) collective-permute-start(bf16[128,2048]{1,0:T(8,128)(2,1)} %get-tuple-element.259), channel_id=1, source_target_pairs={{0,1},{1,0},{2,3},{3,2},{4,5},{5,4},{6,7},{7,6},{8,9},{9,8},{10,11... | collective-permute-start | bytes 1572872 | tf_op jit(solution)/shard_map/ppermute | solution.py:177
  439.0 22.8 %collective-permute-start.24 = (bf16[256,2048]{1,0:T(8,128)(2,1)S(1)}, bf16[256,2048]{1,0:T(8,128)(2,1)S(1)}, u32[]{:S(2)}, u32[]{:S(2)}) collective-permute-start(bf16[256,2048]{1,0:T(8,128)(2,1)S(1)} %multiply_convert_fusion.3), channel_id=1, source_target_pairs={{0,1},{1,0},{2,3},{3,2},{4,5},{5,4},{6,7},{7,6},{8,9},{9,8},{10,11... | collective-permute-start | bytes 3145736 | tf_op jit(solution)/shard_map/ppermute | solution.py:149
  439.6 24.3 %collective-permute-start.25 = (bf16[256,2048]{1,0:T(8,128)(2,1)S(1)}, bf16[256,2048]{1,0:T(8,128)(2,1)S(1)}, u32[]{:S(2)}, u32[]{:S(2)}) collective-permute-start(bf16[256,2048]{1,0:T(8,128)(2,1)S(1)} %multiply_convert_fusion.3), channel_id=1, source_target_pairs={{0,2},{1,3},{2,0},{3,1},{4,6},{5,7},{6,4},{7,5},{8,10},{9,11},{10,... | collective-permute-start | bytes 3145736 | tf_op jit(solution)/shard_map/ppermute | solution.py:150
  461.8 11.5 %collective-permute-start.26 = (bf16[128,2048]{1,0:T(8,128)(2,1)S(1)}, bf16[128,2048]{1,0:T(8,128)(2,1)S(1)}, u32[]{:S(2)}, u32[]{:S(2)}) collective-permute-start(bf16[128,2048]{1,0:T(8,128)(2,1)S(1)} %slice.125), channel_id=1, source_target_pairs={{0,2},{1,3},{2,0},{3,1},{4,6},{5,7},{6,4},{7,5},{8,10},{9,11},{10,... | collective-permute-start | bytes 1572872 | tf_op jit(solution)/shard_map/ppermute | solution.py:151
  480.4 284.4 %reduce-scatter.6.cloned.1.call-start = ((), (), s32[]{:S(2)}) async-start(), calls=%async_computation.10 | async-start | bytes 3538944 | tf_op jit(solution)/shard_map/reduce_scatter | solution.py:199
  629.2 139.0 %reduce-scatter.14.cloned.1.call-start = ((), (), s32[]{:S(2)}) async-start(), calls=%async_computation.14 | async-start | bytes 9437184 | tf_op jit(solution)/shard_map/reduce_scatter | solution.py:199
  630.0 220.1 %reduce-scatter.10.cloned.1.call-start = ((), (), s32[]{:S(2)}) async-start(), calls=%async_computation.12 | async-start | bytes 9437184 | tf_op jit(solution)/shard_map/reduce_scatter | solution.py:199
  630.7 309.6 %reduce-scatter.12.cloned.1.call-start = ((), (), s32[]{:S(2)}) async-start(), calls=%async_computation.13 | async-start | bytes 9437184 | tf_op jit(solution)/shard_map/reduce_scatter | solution.py:199
  640.1 14.8 %collective-permute-start.35 = (bf16[128,2048]{1,0:T(8,128)(2,1)S(1)}, bf16[128,2048]{1,0:T(8,128)(2,1)S(1)}, u32[]{:S(2)}, u32[]{:S(2)}) collective-permute-start(bf16[128,2048]{1,0:T(8,128)(2,1)S(1)} %get-tuple-element.251), channel_id=1, source_target_pairs={{0,1},{1,0},{2,3},{3,2},{4,5},{5,4},{6,7},{7,6},{8,9},{9,8},{10,11... | collective-permute-start | bytes 1572872 | tf_op jit(solution)/shard_map/ppermute | solution.py:177
  640.6 35.8 %collective-permute-start.34 = (bf16[128,2048]{1,0:T(8,128)(2,1)S(1)}, bf16[128,2048]{1,0:T(8,128)(2,1)S(1)}, u32[]{:S(2)}, u32[]{:S(2)}) collective-permute-start(bf16[128,2048]{1,0:T(8,128)(2,1)S(1)} %get-tuple-element.248), channel_id=1, source_target_pairs={{0,1},{1,0},{2,3},{3,2},{4,5},{5,4},{6,7},{7,6},{8,9},{9,8},{10,11... | collective-permute-start | bytes 1572872 | tf_op jit(solution)/shard_map/ppermute | solution.py:177
  642.1 35.6 %collective-permute-start.38 = (bf16[128,2048]{1,0:T(8,128)(2,1)S(1)}, bf16[128,2048]{1,0:T(8,128)(2,1)S(1)}, u32[]{:S(2)}, u32[]{:S(2)}) collective-permute-start(bf16[128,2048]{1,0:T(8,128)(2,1)S(1)} %get-tuple-element.249), channel_id=1, source_target_pairs={{0,2},{1,3},{2,0},{3,1},{4,6},{5,7},{6,4},{7,5},{8,10},{9,11},{10,... | collective-permute-start | bytes 1572872 | tf_op jit(solution)/shard_map/ppermute | solution.py:177
  645.1 28.3 %collective-permute-start.29 = (bf16[128,2048]{1,0:T(8,128)(2,1)S(1)}, bf16[128,2048]{1,0:T(8,128)(2,1)S(1)}, u32[]{:S(2)}, u32[]{:S(2)}) collective-permute-start(bf16[128,2048]{1,0:T(8,128)(2,1)S(1)} %get-tuple-element.257), channel_id=1, source_target_pairs={{0,1},{1,0},{2,3},{3,2},{4,5},{5,4},{6,7},{7,6},{8,9},{9,8},{10,11... | collective-permute-start | bytes 1572872 | tf_op jit(solution)/shard_map/ppermute | solution.py:177
  655.0 23.5 %collective-permute-start.36 = (bf16[128,2048]{1,0:T(8,128)(2,1)S(1)}, bf16[128,2048]{1,0:T(8,128)(2,1)S(1)}, u32[]{:S(2)}, u32[]{:S(2)}) collective-permute-start(bf16[128,2048]{1,0:T(8,128)(2,1)S(1)} %add_convert_fusion.2), channel_id=1, source_target_pairs={{0,2},{1,3},{2,0},{3,1},{4,6},{5,7},{6,4},{7,5},{8,10},{9,11},{10,... | collective-permute-start | bytes 1572872 | tf_op jit(solution)/shard_map/ppermute | solution.py:177
  655.6 56.8 %collective-permute-start.37 = (bf16[128,2048]{1,0:T(8,128)(2,1)}, bf16[128,2048]{1,0:T(8,128)(2,1)S(1)}, u32[]{:S(2)}, u32[]{:S(2)}) collective-permute-start(bf16[128,2048]{1,0:T(8,128)(2,1)} %get-tuple-element.250), channel_id=1, source_target_pairs={{0,2},{1,3},{2,0},{3,1},{4,6},{5,7},{6,4},{7,5},{8,10},{9,11},{10,... | collective-permute-start | bytes 1572872 | tf_op jit(solution)/shard_map/ppermute | solution.py:177
  673.4 12.0 %collective-permute-start.28 = (bf16[128,2048]{1,0:T(8,128)(2,1)S(1)}, bf16[128,2048]{1,0:T(8,128)(2,1)S(1)}, u32[]{:S(2)}, u32[]{:S(2)}) collective-permute-start(bf16[128,2048]{1,0:T(8,128)(2,1)S(1)} %get-tuple-element.254), channel_id=1, source_target_pairs={{0,1},{1,0},{2,3},{3,2},{4,5},{5,4},{6,7},{7,6},{8,9},{9,8},{10,11... | collective-permute-start | bytes 1572872 | tf_op jit(solution)/shard_map/ppermute | solution.py:177
  676.4 14.9 %collective-permute-start.32 = (bf16[128,2048]{1,0:T(8,128)(2,1)S(1)}, bf16[128,2048]{1,0:T(8,128)(2,1)S(1)}, u32[]{:S(2)}, u32[]{:S(2)}) collective-permute-start(bf16[128,2048]{1,0:T(8,128)(2,1)S(1)} %get-tuple-element.255), channel_id=1, source_target_pairs={{0,2},{1,3},{2,0},{3,1},{4,6},{5,7},{6,4},{7,5},{8,10},{9,11},{10,... | collective-permute-start | bytes 1572872 | tf_op jit(solution)/shard_map/ppermute | solution.py:177
  677.7 77.5 %collective-permute-start.31 = (bf16[128,2048]{1,0:T(8,128)(2,1)}, bf16[128,2048]{1,0:T(8,128)(2,1)}, u32[]{:S(2)}, u32[]{:S(2)}) collective-permute-start(bf16[128,2048]{1,0:T(8,128)(2,1)} %get-tuple-element.256), channel_id=1, source_target_pairs={{0,2},{1,3},{2,0},{3,1},{4,6},{5,7},{6,4},{7,5},{8,10},{9,11},{10,... | collective-permute-start | bytes 1572872 | tf_op jit(solution)/shard_map/ppermute | solution.py:177
  678.5 29.6 %collective-permute-start.30 = (bf16[128,2048]{1,0:T(8,128)(2,1)S(1)}, bf16[128,2048]{1,0:T(8,128)(2,1)S(1)}, u32[]{:S(2)}, u32[]{:S(2)}) collective-permute-start(bf16[128,2048]{1,0:T(8,128)(2,1)S(1)} %add_convert_fusion.5), channel_id=1, source_target_pairs={{0,2},{1,3},{2,0},{3,1},{4,6},{5,7},{6,4},{7,5},{8,10},{9,11},{10,... | collective-permute-start | bytes 1572872 | tf_op jit(solution)/shard_map/ppermute | solution.py:177
  685.4 26.9 %collective-permute-start.39 = (bf16[128,2048]{1,0:T(8,128)(2,1)S(1)}, bf16[128,2048]{1,0:T(8,128)(2,1)S(1)}, u32[]{:S(2)}, u32[]{:S(2)}) collective-permute-start(bf16[128,2048]{1,0:T(8,128)(2,1)S(1)} %get-tuple-element.247), channel_id=1, source_target_pairs={{0,1},{1,0},{2,3},{3,2},{4,5},{5,4},{6,7},{7,6},{8,9},{9,8},{10,11... | collective-permute-start | bytes 1572872 | tf_op jit(solution)/shard_map/ppermute | solution.py:177
  710.9 44.3 %collective-permute-start.33 = (bf16[128,2048]{1,0:T(8,128)(2,1)}, bf16[128,2048]{1,0:T(8,128)(2,1)}, u32[]{:S(2)}, u32[]{:S(2)}) collective-permute-start(bf16[128,2048]{1,0:T(8,128)(2,1)} %get-tuple-element.253), channel_id=1, source_target_pairs={{0,1},{1,0},{2,3},{3,2},{4,5},{5,4},{6,7},{7,6},{8,9},{9,8},{10,11... | collective-permute-start | bytes 1572872 | tf_op jit(solution)/shard_map/ppermute | solution.py:177
  (73 other events, 909.1 us)
Sparse Core Ops, SparseCore 0:
  10.7 45.2 all-gather.5
  57.6 29.4 all-gather.7
  88.7 81.0 all-gather.9
  171.2 80.5 all-gather.11
  253.2 80.9 all-gather.13
  480.5 33.8 reduce-scatter.7
  629.3 38.2 reduce-scatter.5
  669.9 89.8 reduce-scatter.13
  762.1 87.9 reduce-scatter.9
  852.2 87.9 reduce-scatter.11

commit v2 on v1

v2 whole, which is shorter than its diff:
```python
import functools

import jax
import jax.numpy as jnp
from jax import lax
from jax.experimental import pallas as pl
from jax.experimental.pallas import tpu as pltpu
from jax.sharding import PartitionSpec as P


HEAD_SIZE = 64
QBLK = 256


epsilon = 1e-05
rope_base = 500000.0


def layout(lengths, total_rows):
    row_index = jnp.arange(total_rows, dtype=jnp.int32)
    doc_ends = jnp.cumsum(lengths)
    passed = doc_ends[None, :] <= row_index[:, None]
    document_segment = jnp.sum(passed.astype(jnp.int32), axis=1)
    doc_start = jnp.sum(jnp.where(passed, lengths[None, :], 0), axis=1)
    positions = (row_index - doc_start).astype(jnp.float32)
    valid_rows = (document_segment < lengths.shape[0]).astype(jnp.float32)
    return (document_segment, positions, valid_rows)


def rope_tables(positions, head_dim):
    half_dim = head_dim // 2
    inverse_freq = rope_base ** (-(jnp.arange(half_dim, dtype=jnp.float32) * 2.0 / head_dim))
    angles = positions[None, :] * inverse_freq[:, None]
    return (jnp.cos(angles), jnp.sin(angles))


def rms_stats(hidden):
    scale_row = lax.rsqrt(jnp.mean(hidden * hidden, axis=-1, keepdims=True) + epsilon)
    return (scale_row, hidden * scale_row)


def norm_backward(grad_normed, unit_rows, scale_row, gain_wide):
    scaled = grad_normed * gain_wide
    return scale_row * (scaled - unit_rows * jnp.mean(scaled * unit_rows, axis=-1, keepdims=True))


def rope_rows(ref, base, cosine, sine_part):
    half = HEAD_SIZE // 2
    first = ref[pl.ds(base, half), :]
    second = ref[pl.ds(base + half, half), :]
    return first * cosine - second * sine_part, second * cosine + first * sine_part


def fill_bias(bias_ref, seg_row_ref, seg_col_ref, start, block):
    keys = start + block
    key_index = lax.broadcasted_iota(jnp.int32, (keys, block), 0)
    query_index = lax.broadcasted_iota(jnp.int32, (keys, block), 1) + start
    allowed = (seg_col_ref[:keys, :] == seg_row_ref[:, start : start + block]) & (
        key_index <= query_index
    )
    bias_ref[:keys, :] = jnp.where(allowed, 0.0, -jnp.inf)


def head_base(index):
    return pl.multiple_of(index * HEAD_SIZE, HEAD_SIZE)


def turned(value):
    return jnp.transpose(value.astype(jnp.float32)).astype(jnp.bfloat16)


def attend_kernel(
    heads, kv_heads, block, joint_ref, cos_ref, sin_ref, seg_row_ref, seg_col_ref,
    rot_ref, att_ref, log_ref, krow_ref, bias_ref,
):
    rows = joint_ref.shape[1]
    half = HEAD_SIZE // 2
    group = heads // kv_heads
    value_base = (heads + kv_heads) * HEAD_SIZE

    def rotate_head(index, scale):
        base = head_base(index)
        first, second = rope_rows(joint_ref, base, cos_ref[...], sin_ref[...])
        rot_ref[pl.ds(base, half), :] = (first * scale).astype(jnp.bfloat16)
        rot_ref[pl.ds(base + half, half), :] = (second * scale).astype(jnp.bfloat16)

    @pl.loop(0, heads)
    def _(index):
        rotate_head(index, HEAD_SIZE ** (-0.5))

    @pl.loop(0, kv_heads)
    def _(index):
        rotate_head(heads + index, 1.0)
        krow_ref[index] = turned(rot_ref[pl.ds(head_base(heads + index), HEAD_SIZE), :])

    rot_ref[value_base:, :] = joint_ref[value_base:, :].astype(jnp.bfloat16)
    for start in range(0, rows, block):
        keys = start + block
        fill_bias(bias_ref, seg_row_ref, seg_col_ref, start, block)

        @pl.loop(0, heads)
        def _(head):
            kv_head = head // group
            query = rot_ref[pl.ds(head_base(head), HEAD_SIZE), start:keys]
            scores = (
                jnp.dot(krow_ref[kv_head, :keys, :], query, preferred_element_type=jnp.float32)
                + bias_ref[:keys, :]
            )
            top = jnp.max(scores, axis=0, keepdims=True)
            powers = jnp.exp(scores - top)
            total = jnp.sum(powers, axis=0, keepdims=True)
            weights = (powers * (1.0 / total)).astype(jnp.bfloat16)
            value = rot_ref[pl.ds(head_base(heads + kv_heads + kv_head), HEAD_SIZE), :keys]
            att_ref[pl.ds(head_base(head), HEAD_SIZE), start:keys] = jnp.dot(
                value, weights, preferred_element_type=jnp.float32
            ).astype(jnp.bfloat16)
            log_ref[pl.ds(head, 1), start:keys] = top + jnp.log(total)


def attend_back_kernel(
    heads, kv_heads, block, rot_ref, att_ref, out_ref, log_ref, cos_ref, sin_ref,
    seg_row_ref, seg_col_ref, back_ref, krow_ref, vrow_ref, dkey_ref, dvalue_ref, bias_ref,
):
    rows = rot_ref.shape[1]
    half = HEAD_SIZE // 2
    group = heads // kv_heads
    last = (((1,), (1,)), ((), ()))

    def turn_back(first, second, base, start, stop):
        cosine, sine_part = cos_ref[:, start:stop], sin_ref[:, start:stop]
        back_ref[pl.ds(base, half), start:stop] = (
            first * cosine + second * sine_part
        ).astype(jnp.bfloat16)
        back_ref[pl.ds(base + half, half), start:stop] = (
            second * cosine - first * sine_part
        ).astype(jnp.bfloat16)

    @pl.loop(0, kv_heads)
    def _(index):
        krow_ref[index] = turned(rot_ref[pl.ds(head_base(heads + index), HEAD_SIZE), :])
        vrow_ref[index] = turned(rot_ref[pl.ds(head_base(heads + kv_heads + index), HEAD_SIZE), :])

    dkey_ref[...] = jnp.zeros_like(dkey_ref)
    dvalue_ref[...] = jnp.zeros_like(dvalue_ref)
    for start in range(0, rows, block):
        keys = start + block
        fill_bias(bias_ref, seg_row_ref, seg_col_ref, start, block)

        @pl.loop(0, heads)
        def _(head):
            kv_head = head // group
            own = pl.ds(head_base(head), HEAD_SIZE)
            query = rot_ref[own, start:keys]
            grad = out_ref[own, start:keys]
            delta = jnp.sum(
                grad.astype(jnp.float32) * att_ref[own, start:keys].astype(jnp.float32),
                axis=0,
                keepdims=True,
            )
            scores = (
                jnp.dot(krow_ref[kv_head, :keys, :], query, preferred_element_type=jnp.float32)
                + bias_ref[:keys, :]
            )
            probs = jnp.exp(scores - log_ref[pl.ds(head, 1), start:keys])
            grad_probs = jnp.dot(
                vrow_ref[kv_head, :keys, :], grad, preferred_element_type=jnp.float32
            )
            grad_scores = (probs * (grad_probs - delta)).astype(jnp.bfloat16)
            dvalue_ref[kv_head, :keys, :] += lax.dot_general(
                probs.astype(jnp.bfloat16), grad, last, preferred_element_type=jnp.float32
            )
            dkey_ref[kv_head, :keys, :] += lax.dot_general(
                grad_scores, query, last, preferred_element_type=jnp.float32
            )
            key = rot_ref[pl.ds(head_base(heads + kv_head), HEAD_SIZE), :keys]
            dquery = jnp.dot(key, grad_scores, preferred_element_type=jnp.float32) * (
                HEAD_SIZE ** (-0.5)
            )
            turn_back(dquery[:half], dquery[half:], head_base(head), start, keys)

    @pl.loop(0, kv_heads)
    def _(index):
        dkey = jnp.transpose(dkey_ref[index])
        turn_back(dkey[:half], dkey[half:], head_base(heads + index), 0, rows)
        back_ref[pl.ds(head_base(heads + kv_heads + index), HEAD_SIZE), :] = jnp.transpose(
            dvalue_ref[index]
        ).astype(jnp.bfloat16)


def activation_back_kernel(pair_ref, grad_ref, out_ref):
    units = grad_ref.shape[1]
    gate, up = pair_ref[:, :units], pair_ref[:, units:]
    grad = grad_ref[...]
    sigmoid_gate = 1.0 / (1.0 + jnp.exp(-gate))
    grad_gate = grad * up * sigmoid_gate * (1.0 + gate * (1.0 - sigmoid_gate))
    out_ref[:, :units] = grad_gate.astype(jnp.bfloat16)
    out_ref[:, units:] = (grad * gate * sigmoid_gate).astype(jnp.bfloat16)


def activation_back(pair, grad):
    rows, units = grad.shape
    block = min(rows, 128)

    def at(row):
        return (row, 0)

    return pl.pallas_call(
        activation_back_kernel,
        out_shape=jax.ShapeDtypeStruct(pair.shape, jnp.bfloat16),
        grid=(rows // block,),
        in_specs=[pl.BlockSpec((block, 2 * units), at), pl.BlockSpec((block, units), at)],
        out_specs=pl.BlockSpec((block, 2 * units), at),
        cost_estimate=pl.CostEstimate(
            flops=20 * pair.size, bytes_accessed=8 * pair.size, transcendentals=pair.size
        ),
        name="activation_back",
    )(pair, grad)


def in_vmem(count):
    return [pl.BlockSpec(memory_space=pltpu.VMEM)] * count


def attend(joint, cosine, sine_part, seg_row, seg_col, heads, kv_heads, block):
    rows = joint.shape[1]
    flops = 2 * heads * rows * rows * HEAD_SIZE
    return pl.pallas_call(
        functools.partial(attend_kernel, heads, kv_heads, block),
        out_shape=(
            jax.ShapeDtypeStruct(joint.shape, jnp.bfloat16),
            jax.ShapeDtypeStruct((heads * HEAD_SIZE, rows), jnp.bfloat16),
            jax.ShapeDtypeStruct((heads, rows), jnp.float32),
        ),
        in_specs=in_vmem(5),
        out_specs=tuple(in_vmem(3)),
        scratch_shapes=[
            pltpu.VMEM((kv_heads, rows, HEAD_SIZE), jnp.bfloat16),
            pltpu.VMEM((rows, block), jnp.float32),
        ],
        cost_estimate=pl.CostEstimate(
            flops=8 * flops, bytes_accessed=8 * joint.size, transcendentals=heads * rows * rows
        ),
        name="attend",
    )(joint, cosine, sine_part, seg_row, seg_col)


def attend_back(rotated, attended, grad, log_total, cosine, sine_part, seg_row, seg_col, heads, kv_heads, block):
    rows = rotated.shape[1]
    flops = 2 * heads * rows * rows * HEAD_SIZE
    return pl.pallas_call(
        functools.partial(attend_back_kernel, heads, kv_heads, block),
        out_shape=jax.ShapeDtypeStruct(rotated.shape, jnp.bfloat16),
        in_specs=in_vmem(8),
        out_specs=pl.BlockSpec(memory_space=pltpu.VMEM),
        scratch_shapes=[
            pltpu.VMEM((kv_heads, rows, HEAD_SIZE), jnp.bfloat16),
            pltpu.VMEM((kv_heads, rows, HEAD_SIZE), jnp.bfloat16),
            pltpu.VMEM((kv_heads, rows, HEAD_SIZE), jnp.float32),
            pltpu.VMEM((kv_heads, rows, HEAD_SIZE), jnp.float32),
            pltpu.VMEM((rows, block), jnp.float32),
        ],
        cost_estimate=pl.CostEstimate(
            flops=20 * flops, bytes_accessed=8 * rotated.size, transcendentals=heads * rows * rows
        ),
        name="attend_back",
    )(rotated, attended, grad, log_total, cosine, sine_part, seg_row, seg_col)


def shift_pairs(count, mask):
    return [(i, i ^ mask) for i in range(count)]


def gather_rows_plain(block, axis):
    count = lax.axis_size(axis)
    if count != 4:
        return lax.all_gather(block, axis, axis=0, tiled=True)
    me = lax.axis_index(axis)
    rows = block.shape[0]
    half = rows // 2
    from_x = lax.ppermute(block, axis, shift_pairs(count, 1))
    from_y = lax.ppermute(block, axis, shift_pairs(count, 2))
    far_top = lax.ppermute(from_x[:half], axis, shift_pairs(count, 2))
    far_low = lax.ppermute(from_y[half:], axis, shift_pairs(count, 1))
    whole = jnp.zeros((count * rows, block.shape[1]), block.dtype)
    for mask, piece, extra in (
        (0, block, 0),
        (1, from_x, 0),
        (2, from_y, 0),
        (3, far_top, 0),
        (3, far_low, half),
    ):
        whole = lax.dynamic_update_slice(whole, piece, ((me ^ mask) * rows + extra, 0))
    return whole


def scatter_rows_plain(partial, axis):
    count = lax.axis_size(axis)
    if count != 4:
        return lax.psum_scatter(partial, axis, scatter_dimension=0, tiled=True).astype(jnp.float32)
    me = lax.axis_index(axis)
    rows = partial.shape[0] // count
    half = rows // 2

    def part(mask, extra):
        return lax.dynamic_slice_in_dim(partial, (me ^ mask) * rows + extra, half, 0)

    def send(piece, mask):
        return lax.ppermute(piece, axis, shift_pairs(count, mask))

    relay_top = send(part(3, 0), 1).astype(jnp.float32)
    relay_low = send(part(3, half), 2).astype(jnp.float32)
    near_top = send(part(1, 0), 1).astype(jnp.float32)
    near_low = send(part(2, half), 2).astype(jnp.float32)
    joined_top = send((part(2, 0) + relay_top).astype(jnp.bfloat16), 2).astype(jnp.float32)
    joined_low = send((part(1, half) + relay_low).astype(jnp.bfloat16), 1).astype(jnp.float32)
    return jnp.concatenate(
        [part(0, 0) + near_top + joined_top, part(0, half) + near_low + joined_low], axis=0
    )


def product(left, right):
    return jnp.dot(left, right, preferred_element_type=jnp.float32)


def contract(left, right, left_axis, right_axis):
    return lax.dot_general(
        left,
        right,
        (((left_axis,), (right_axis,)), ((), ())),
        preferred_element_type=jnp.float32,
    )


def ordered(*values):
    return lax.optimization_barrier(values)


def sum_shards(partial, dimension):
    return lax.psum_scatter(partial, "dp", scatter_dimension=dimension, tiled=True)


def narrow(value):
    return value.astype(jnp.bfloat16)


def whole_block(
    inputs,
    doc_lengths,
    attn_gain,
    w_query,
    w_key,
    value_weight,
    w_output,
    mlp_gain,
    w_gate,
    w_up,
    w_down,
    out_grad,
):
    tensor_rank = lax.axis_index("tensor")
    own_rows = inputs.shape[0]
    total_rows = own_rows * lax.axis_size("tensor")
    query_cols, key_cols = w_query.shape[1], w_key.shape[1]
    joint = query_cols + 2 * key_cols
    document_segment, positions, valid_rows = layout(doc_lengths[0], total_rows)
    valid_own = lax.dynamic_slice_in_dim(valid_rows, tensor_rank * own_rows, own_rows, 0)[:, None]
    cosine, sine_part = rope_tables(positions, HEAD_SIZE)
    gains = jnp.pad(jnp.stack([attn_gain, mlp_gain], axis=1), ((0, 0), (0, 126)))
    packed = lax.all_gather(
        jnp.concatenate([w_query, w_key, value_weight, gains, w_output.T], axis=1),
        "dp",
        axis=0,
        tiled=True,
    )
    full_joint = packed[:, :joint]
    gain_one = packed[:, joint].astype(jnp.float32)
    gain_two = packed[:, joint + 1].astype(jnp.float32)
    full_output = packed[:, joint + gains.shape[1] :]
    full_pair = lax.all_gather(
        jnp.concatenate([w_gate, w_up], axis=1), "dp", axis=0, tiled=True
    )
    full_down = lax.all_gather(w_down, "dp", axis=1, tiled=True)

    grad_out = out_grad.astype(jnp.float32)
    head_count = query_cols // HEAD_SIZE
    kv_heads = key_cols // HEAD_SIZE
    residual = inputs.astype(jnp.float32)
    scale_one, unit_one = rms_stats(residual)
    inputs_all = gather_rows_plain(inputs, "tensor")
    cotangent_all = gather_rows_plain(out_grad, "tensor")
    normed_one_all = narrow(rms_stats(inputs_all.astype(jnp.float32))[1] * gain_one)
    grad_mlp_all = cotangent_all * narrow(valid_rows)[:, None]
    seg_row, seg_col = document_segment[None, :], document_segment[:, None]
    joint_turned = contract(full_joint, normed_one_all, 0, 1)
    rotated, attended, log_total = attend(
        joint_turned, cosine, sine_part, seg_row, seg_col, head_count, kv_heads, QBLK
    )
    attn_out = scatter_rows_plain(narrow(contract(attended, full_output, 0, 1)), "tensor")
    hidden = residual + valid_own * attn_out
    scale_two, unit_two = rms_stats(hidden)
    normed_two_all = gather_rows_plain(narrow(unit_two * gain_two), "tensor")
    hidden_units = w_gate.shape[1]
    pair_pre = product(normed_two_all, full_pair)
    gate_pre, up_proj = pair_pre[:, :hidden_units], pair_pre[:, hidden_units:]
    activation = narrow(gate_pre * jax.nn.sigmoid(gate_pre) * up_proj)
    down_part = narrow(product(activation.T, grad_mlp_all))
    pair_pre, down_part = ordered(pair_pre, down_part)
    w_down_grad = sum_shards(down_part, 1)
    grad_act = product(grad_mlp_all, full_down.T)
    grad_pair = activation_back(pair_pre, grad_act)
    normed_part = narrow(contract(grad_pair, full_pair, 1, 1))
    grad_pair, normed_part = ordered(grad_pair, normed_part)
    grad_normed_two = scatter_rows_plain(normed_part, "tensor")
    pair_part = narrow(contract(normed_two_all, grad_pair, 0, 0))
    grad_normed_two, pair_part = ordered(grad_normed_two, pair_part)
    pair_grad = sum_shards(pair_part, 0).astype(jnp.float32)
    mlp_gain_part = jnp.sum(grad_normed_two * unit_two, axis=0)
    grad_hidden = grad_out + norm_backward(grad_normed_two, unit_two, scale_two, gain_two)
    grad_attn = narrow(grad_hidden * valid_own)
    activation, grad_attn = ordered(activation, grad_attn)
    grad_attn_all = gather_rows_plain(grad_attn, "tensor")
    mlp_part = narrow(product(activation, full_down))
    grad_attn_all, mlp_part = ordered(grad_attn_all, mlp_part)
    mlp_out = scatter_rows_plain(mlp_part, "tensor")
    output = hidden + valid_own * mlp_out
    out_part = narrow(contract(grad_attn_all, attended, 0, 1))
    grad_attended = narrow(contract(full_output, grad_attn_all, 0, 1))
    joint_back = attend_back(
        rotated,
        attended,
        grad_attended,
        log_total,
        cosine,
        sine_part,
        seg_row,
        seg_col,
        head_count,
        kv_heads,
        QBLK,
    )
    joint_part = narrow(contract(normed_one_all, joint_back, 0, 1))
    tail_grad = sum_shards(jnp.concatenate([joint_part, out_part], axis=1), 0).astype(jnp.float32)
    grad_normed_one = scatter_rows_plain(narrow(contract(joint_back, full_joint, 0, 1)), "tensor")
    attn_gain_part = jnp.sum(grad_normed_one * unit_one, axis=0)
    input_grad = grad_hidden + norm_backward(grad_normed_one, unit_one, scale_one, gain_one)
    gain_sums = lax.psum(jnp.stack([attn_gain_part, mlp_gain_part]), ("dp", "tensor"))
    gain_rows = attn_gain.shape[0]
    gain_own = lax.dynamic_slice_in_dim(gain_sums, lax.axis_index("dp") * gain_rows, gain_rows, 1)
    return (
        output,
        input_grad,
        gain_own[0],
        tail_grad[:, :query_cols],
        tail_grad[:, query_cols : query_cols + key_cols],
        tail_grad[:, query_cols + key_cols : joint],
        tail_grad[:, joint:].T,
        gain_own[1],
        pair_grad[:, :hidden_units],
        pair_grad[:, hidden_units:],
        w_down_grad.astype(jnp.float32),
    )


def solution(mesh):
    placed = (
        P(("dp", "tensor"), None),
        P("dp", None),
        P("dp"),
        P("dp", "tensor"),
        P("dp", "tensor"),
        P("dp", "tensor"),
        P("tensor", "dp"),
        P("dp"),
        P("dp", "tensor"),
        P("dp", "tensor"),
        P("tensor", "dp"),
        P(("dp", "tensor"), None),
    )
    return jax.shard_map(
        whole_block,
        mesh=mesh,
        in_specs=placed,
        out_specs=(
            P(("dp", "tensor"), None),
            P(("dp", "tensor"), None),
            P("dp"),
            P("dp", "tensor"),
            P("dp", "tensor"),
            P("dp", "tensor"),
            P("tensor", "dp"),
            P("dp"),
            P("dp", "tensor"),
            P("dp", "tensor"),
            P("tensor", "dp"),
        ),
        check_vma=False,
    )
```

time: 963 us -> 866 us (0.90)
  matrix products: 248 us -> 144 us
  Pallas kernels: 0 us -> 61.7 us
  local copies, waits for them, and re-layouts: 113 us -> 65.2 us
  waiting for transfers between devices: 410 us -> 436 us
  other arithmetic: 67.6 us -> 43.6 us
    dot_general x15 -> x4, matrix products: 166 us -> 62.9 us  [product(): return jnp.dot(left, right, preferred_element_type=jnp.float32)]
    pallas_call x0 -> x3, Pallas kernels: none -> 61.7 us  [the longest x1 25.1 us: attend(): pl.pallas_call(functools.partial(attend_kernel, heads, kv_heads, block),...]
    all_gather x4 -> x2, waiting for transfers between devices: 19.1 us -> 75.9 us  [the longest x1 63.6 us: whole_block(): lax.all_gather(jnp.concatenate([w_gate, w_up], axis=1), 'dp', axis=0, til...]
    all_gather x1, waiting for transfers between devices: 50.2 us -> 0.01 us  [whole_block(): full_down = lax.all_gather(w_down, 'dp', axis=1, tiled=True)]
    dynamic_update_slice x4 -> x0, local copies, waits for them, and re-layouts: 41.4 us -> none  [attention_backward(): lax.scan(one_block, (zero_keys, zero_keys), jnp.arange(total_rows // bloc...]
    ppermute x24, waiting for transfers between devices: 96.2 us -> 107 us  [send(): return lax.ppermute(piece, axis, shift_pairs(count, mask))]
    reduce_scatter x5 -> x3, waiting for transfers between devices: 167 us -> 177 us  [sum_shards(): lax.psum_scatter(partial, 'dp', scatter_dimension=dimension, tiled=True)]
    dot_general x14 -> x8, matrix products: 82.3 us -> 81.2 us  [contract(): lax.dot_general(left, right, (((left_axis,), (right_axis,)), ((), ())), p...]
  transfers between devices with their start and end apart: 50 -> 46, of which waited for: 26 -> 30; matrix products, arithmetic and copies ran while one was open for 37% -> 17% of each run, Pallas kernels for 0% -> 3%
where the time goes in v2:
time: 866 us; the launch traced here: 860 us
  waiting for transfers between devices  436 us (50%)
  matrix products  144 us (17%)
  local copies, waits for them, and re-layouts  65.2 us (8%)
  Pallas kernels  61.7 us (7%)
  starting transfers between devices  54.2 us (6%)
  other arithmetic  43.6 us (5%)
  blocking collectives  40.7 us (5%)
  between operations  15.3 us (2%)
    reduce_scatter x3, waiting for transfers between devices, sum_shards(): lax.psum_scatter(partial, 'dp', scatter_dimension=dimension, tiled=True)  177 us
    ppermute x24, waiting for transfers between devices, send(): return lax.ppermute(piece, axis, shift_pairs(count, mask))  107 us
    dot_general x8, matrix products, contract(): lax.dot_general(left, right, (((left_axis,), (right_axis,)), ((), ())), p...  81.2 us
    all_gather x1, waiting for transfers between devices, whole_block(): lax.all_gather(jnp.concatenate([w_gate, w_up], axis=1), 'dp', axis=0, til...  63.6 us
    dot_general x4, matrix products, product(): return jnp.dot(left, right, preferred_element_type=jnp.float32)  62.9 us
    ppermute x4, waiting for transfers between devices, gather_rows_plain(): from_x = lax.ppermute(block, axis, shift_pairs(count, 1))  43.4 us
    psum x1, blocking collectives, whole_block(): lax.psum(jnp.stack([attn_gain_part, mlp_gain_part]), ('dp', 'tensor'))  40.7 us
    ppermute x24, starting transfers between devices, send(): return lax.ppermute(piece, axis, shift_pairs(count, mask))  30 us
  transfers between devices with their start and end apart: 46, of which 30 were waited for; matrix products, arithmetic and copies ran while one was open for 17% of the time, Pallas kernels for 3%

profile of v2, /device:TPU:0, one launch (start us, length us, event | category | flops | bytes accessed | tf_op | source)
XLA Modules:
  0.0 860.4 jit_solution(15554504293442278043)
XLA Ops:
  17.3 3.0 collective-permute-start
  25.8 17.6 %collective-permute-done = bf16[256,2048]{1,0:T(8,128)(2,1)S(1)} collective-permute-done((bf16[256,2048]{1,0:T(8,128)(2,1)S(1)}, bf16[256,2048]{1,0:T(8,128)(2,1)S(1)}, u32[]{:S(2)}, u32[]{:S(2)}) %collective-permute-start) | collective-permute-done | bytes 1048608 | tf_op jit(solution)/shard_map/ppermute | solution.py:280
  52.1 5.7 collective-permute-done.2
  61.9 3.1 fusion
  65.1 12.3 %all-gather.4.cloned.1.call-done = bf16[2048,1408]{0,1:T(8,128)(2,1)} async-done(((bf16[256,1408]{0,1:T(8,128)(2,1)}), bf16[2048,1408]{0,1:T(8,128)(2,1)}) %all-gather.4.cloned.1.call-update) | async-done | bytes 5767184 | tf_op jit(solution)/shard_map/all_gather | solution.py:369
  78.2 8.3 fusion.11.joint_ref
  86.6 25.1 %attend.1 = (bf16[768,1024]{1,0:T(8,128)(2,1)}, bf16[512,1024]{1,0:T(8,128)(2,1)}, f32[8,1024]{1,0:T(8,128)}) custom-call(f32[768,1024]{1,0:T(8,128)} %fusion.11.joint_ref, f32[32,1024]{1,0:T(8,128)} %get-tuple-element.116.cos_ref, f32[32,1024]{1,0:T(8,128)} %get-tuple-element.115.sin_ref, s32[1,1024]{1,0:T(1,128)} %bitcast.40, s32[1024,1]{1,0:T(8,128)} %copy.40.seg_col_ref), custom_call_target="tpu_custom_call" | custom-call | flops 8589934592 | bytes 6291456 | tf_op jit(solution)/shard_map/attend/pallas_call | solution.py:227
  111.6 4.3 convolution_convert_fusion.4
  120.7 11.2 %collective-permute-done.5 = bf16[128,2048]{1,0:T(8,128)(2,1)S(1)} collective-permute-done((bf16[128,2048]{1,0:T(8,128)(2,1)S(1)}, bf16[128,2048]{1,0:T(8,128)(2,1)S(1)}, u32[]{:S(2)}, u32[]{:S(2)}) %collective-permute-start.5) | collective-permute-done | bytes 524320 | tf_op jit(solution)/shard_map/ppermute | solution.py:308
  134.9 7.8 collective-permute-done.4
  144.2 3.7 collective-permute-done.6
  148.0 3.1 convert_add_fusion.8
  154.6 4.6 collective-permute-done.7
  159.2 7.0 collective-permute-done.9
  169.2 3.0 broadcast.75.clone.1
  174.7 13.9 %collective-permute-done.14 = bf16[256,2048]{1,0:T(8,128)(2,1)} collective-permute-done((bf16[256,2048]{1,0:T(8,128)(2,1)S(1)}, bf16[256,2048]{1,0:T(8,128)(2,1)}, u32[]{:S(2)}, u32[]{:S(2)}) %collective-permute-start.14) | collective-permute-done | bytes 1048608 | tf_op jit(solution)/shard_map/ppermute | solution.py:280
  205.4 5.6 collective-permute-done.10
  212.5 5.9 collective-permute-done.17
  219.3 3.4 collective-permute-done.11
  229.1 2.9 collective-permute-done.13
  232.9 14.6 %fusion.4.grad_ref = f32[1024,2048]{1,0:T(8,128)} fusion(bf16[2048,2048]{1,0:T(8,128)(2,1)} %all-gather.8.cloned.1.call-done, bf16[1024,2048]{1,0:T(8,128)(2,1)} %constant_dynamic-update-slice_fusion.5, bf16[1024]{0:T(1024)(128)(2,1)S(1)} %get-tuple-element.117), kind=kOutput, calls=%fused_computation.14 | convolution fusion | flops 8592031744 | bytes 20973568 | tf_op jit(solution)/shard_map/dot_general | solution.py:322
  247.5 63.6 %all-gather.6.cloned.1.call-done = bf16[2048,4096]{1,0:T(8,128)(2,1)} async-done(((bf16[256,4096]{1,0:T(8,128)(2,1)}), bf16[2048,4096]{1,0:T(8,128)(2,1)}) %all-gather.6.cloned.1.call-update) | async-done | bytes 16777232 | tf_op jit(solution)/shard_map/all_gather | solution.py:379
  311.1 21.9 %fusion.38.pair_ref = f32[1024,4096]{1,0:T(8,128)S(1)} fusion(bf16[1024,2048]{1,0:T(8,128)(2,1)} %constant_dynamic-update-slice_fusion.10, bf16[2048,4096]{1,0:T(8,128)(2,1)} %all-gather.6.cloned.1.call-done), kind=kOutput, calls=%fused_computation.135 | convolution fusion | flops 17179869184 | bytes 37748736 | tf_op jit(solution)/shard_map/dot_general | solution.py:322
  333.1 5.7 copy-done
  343.4 13.5 %convolution_convert_fusion.1 = bf16[2048,2048]{1,0:T(8,128)(2,1)} fusion(bf16[1024,2048]{1,0:T(8,128)(2,1)S(1)} %fusion.3, bf16[1024,2048]{1,0:T(8,128)(2,1)} %constant_dynamic-update-slice_fusion.5, bf16[1024]{0:T(1024)(128)(2,1)S(1)} %get-tuple-element.117), kind=kOutput, calls=%fused_computation.8 | convolution fusion | flops 8596226048 | bytes 16779264 | tf_op jit(solution)/shard_map/dot_general | solution.py:322
  356.9 13.9 %activation_back.1 = bf16[1024,4096]{1,0:T(8,128)(2,1)} custom-call(f32[1024,4096]{1,0:T(8,128)} %copy-done, f32[1024,2048]{1,0:T(8,128)} %fusion.4.grad_ref), custom_call_target="tpu_custom_call" | custom-call | flops 83886080 | bytes 33554432 | tf_op jit(solution)/shard_map/activation_back/pallas_call | solution.py:207
  370.8 22.8 %convolution_convert_fusion.2 = bf16[1024,2048]{1,0:T(8,128)(2,1)S(1)} fusion(bf16[1024,4096]{1,0:T(8,128)(2,1)} %activation_back.1, bf16[2048,4096]{1,0:T(8,128)(2,1)} %all-gather.6.cloned.1.call-done), kind=kOutput, calls=%fused_computation.10 | convolution fusion | flops 17181966336 | bytes 29360128 | tf_op jit(solution)/shard_map/dot_general | solution.py:326
  398.4 11.3 %collective-permute-done.19 = bf16[128,2048]{1,0:T(8,128)(2,1)S(1)} collective-permute-done((bf16[128,2048]{1,0:T(8,128)(2,1)S(1)}, bf16[128,2048]{1,0:T(8,128)(2,1)S(1)}, u32[]{:S(2)}, u32[]{:S(2)}) %collective-permute-start.19) | collective-permute-done | bytes 524320 | tf_op jit(solution)/shard_map/ppermute | solution.py:308
  412.0 8.3 collective-permute-done.18
  420.3 4.5 collective-permute-done.20
  427.4 24.7 %convolution_convert_fusion = bf16[2048,4096]{1,0:T(8,128)(2,1)} fusion(bf16[1024,2048]{1,0:T(8,128)(2,1)} %constant_dynamic-update-slice_fusion.10, bf16[1024,4096]{1,0:T(8,128)(2,1)} %activation_back.1), kind=kOutput, calls=%fused_computation | convolution fusion | flops 17188257792 | bytes 29360128 | tf_op jit(solution)/shard_map/dot_general | solution.py:326
  458.1 12.8 %convolution_convert_fusion.3 = bf16[1024,2048]{1,0:T(8,128)(2,1)} fusion(bf16[1024,2048]{1,0:T(8,128)(2,1)S(1)} %copy-done.11, bf16[2048,2048]{1,0:T(8,128)(2,1)} %all-gather.8.cloned.1.call-done), kind=kOutput, calls=%fused_computation.11 | convolution fusion | flops 8592031744 | bytes 16777216 | tf_op jit(solution)/shard_map/dot_general | solution.py:322
  470.9 6.3 collective-permute-done.24
  482.5 5.4 collective-permute-done.26
  489.9 3.7 convolution_convert_fusion.7
  493.6 5.1 fusion.25.out_ref
  498.7 22.7 %attend_back.1 = bf16[768,1024]{1,0:T(8,128)(2,1)} custom-call(bf16[768,1024]{1,0:T(8,128)(2,1)} %get-tuple-element.32.rot_ref, bf16[512,1024]{1,0:T(8,128)(2,1)} %get-tuple-element.24.att_ref, bf16[512,1024]{1,0:T(8,128)(2,1)} %fusion.25.out_ref, f32[8,1024]{1,0:T(8,128)} %get-tuple-element.34.log_ref, f32[32,1024]{1,0:T(8,128)} %get-tuple-element.116.cos_ref, ...), custom_call_target="tpu_custom_call" | custom-call | flops 21474836480 | bytes 6291456 | tf_op jit(solution)/shard_map/attend_back/pallas_call | solution.py:250
  521.3 6.4 convolution_convert_fusion.6
  531.6 5.8 convolution_convert_fusion.5
  548.2 7.4 collective-permute-done.35
  557.9 17.3 %collective-permute-done.29 = bf16[128,2048]{1,0:T(8,128)(2,1)S(1)} collective-permute-done((bf16[128,2048]{1,0:T(8,128)(2,1)S(1)}, bf16[128,2048]{1,0:T(8,128)(2,1)S(1)}, u32[]{:S(2)}, u32[]{:S(2)}) %collective-permute-start.29) | collective-permute-done | bytes 524320 | tf_op jit(solution)/shard_map/ppermute | solution.py:308
  582.1 7.2 collective-permute-done.28
  593.0 14.8 %collective-permute-done.30 = bf16[128,2048]{1,0:T(8,128)(2,1)S(1)} collective-permute-done((bf16[128,2048]{1,0:T(8,128)(2,1)S(1)}, bf16[128,2048]{1,0:T(8,128)(2,1)S(1)}, u32[]{:S(2)}, u32[]{:S(2)}) %collective-permute-start.30) | collective-permute-done | bytes 524320 | tf_op jit(solution)/shard_map/ppermute | solution.py:308
  613.5 40.7 %psum.7 = f32[2,2048]{1,0:T(2,128)S(1)} all-reduce(f32[2,2048]{1,0:T(2,128)S(1)} %pad_maximum_fusion.4), channel_id=1, replica_groups=mesh['dp'=8,'tensor'=4] {'dp','tensor'}, use_global_device_ids=true, to_apply=%region_10.11 | all-reduce | flops 4096 | bytes 32768 | tf_op jit(solution)/shard_map/psum | solution.py:446
  656.5 6.3 fusion.16
  669.2 11.0 %reduce-scatter.8.cloned.1.call-done = bf16[2048,256]{1,0:T(8,128)(2,1)} async-done(((bf16[2048,2048]{1,0:T(8,128)(2,1)}), bf16[2048,256]{1,0:T(8,128)(2,1)}) %reduce-scatter.8.cloned.1.call-update) | async-done | bytes 1048592 | tf_op jit(solution)/shard_map/reduce_scatter | solution.py:339
  682.8 166.2 %reduce-scatter.6.cloned.1.call-done = bf16[256,4096]{1,0:T(8,128)(2,1)} async-done(((bf16[2048,4096]{1,0:T(8,128)(2,1)}), bf16[256,4096]{1,0:T(8,128)(2,1)}) %reduce-scatter.6.cloned.1.call-update) | async-done | bytes 2097168 | tf_op jit(solution)/shard_map/reduce_scatter | solution.py:339
  849.0 4.1 fusion.35
  (231 shorter events, 145.7 us)
Async XLA Ops:
  7.2 70.1 %all-gather.4.cloned.1.call-start = ((), (), s32[]{:S(2)}) async-start(), calls=%async_computation.3 | async-start | bytes 6488064 | tf_op jit(solution)/shard_map/all_gather | solution.py:369
  13.6 219.2 %all-gather.8.cloned.1.call-start = ((), (), s32[]{:S(2)}) async-start(), calls=%async_computation.5 | async-start | bytes 9437184 | tf_op jit(solution)/shard_map/all_gather | solution.py:382
  14.4 296.7 %all-gather.6.cloned.1.call-start = ((), (), s32[]{:S(2)}) async-start(), calls=%async_computation.4 | async-start | bytes 18874368 | tf_op jit(solution)/shard_map/all_gather | solution.py:379
  17.2 645.6 %reduce-scatter.4.cloned.1.call-start = ((), (), s32[]{:S(2)}) async-start(), calls=%async_computation.6 | async-start | bytes 5898240 | tf_op jit(solution)/shard_map/reduce_scatter | solution.py:339
  17.3 26.2 %collective-permute-start = (bf16[256,2048]{1,0:T(8,128)(2,1)S(1)}, bf16[256,2048]{1,0:T(8,128)(2,1)S(1)}, u32[]{:S(2)}, u32[]{:S(2)}) collective-permute-start(bf16[256,2048]{1,0:T(8,128)(2,1)S(1)} %copy-done.4), channel_id=1, source_target_pairs={{0,1},{1,0},{2,3},{3,2},{4,5},{5,4},{6,7},{7,6},{8,9},{9,8},{10,11... | collective-permute-start | bytes 3145736 | tf_op jit(solution)/shard_map/ppermute | solution.py:280
  20.3 28.0 %collective-permute-start.1 = (bf16[256,2048]{1,0:T(8,128)(2,1)S(1)}, bf16[256,2048]{1,0:T(8,128)(2,1)S(1)}, u32[]{:S(2)}, u32[]{:S(2)}) collective-permute-start(bf16[256,2048]{1,0:T(8,128)(2,1)S(1)} %copy-done.4), channel_id=1, source_target_pairs={{0,2},{1,3},{2,0},{3,1},{4,6},{5,7},{6,4},{7,5},{8,10},{9,11},{10,... | collective-permute-start | bytes 3145736 | tf_op jit(solution)/shard_map/ppermute | solution.py:281
  44.3 13.5 %collective-permute-start.2 = (bf16[128,2048]{1,0:T(8,128)(2,1)}, bf16[128,2048]{1,0:T(8,128)(2,1)}, u32[]{:S(2)}, u32[]{:S(2)}) collective-permute-start(bf16[128,2048]{1,0:T(8,128)(2,1)} %slice.89), channel_id=1, source_target_pairs={{0,2},{1,3},{2,0},{3,1},{4,6},{5,7},{6,4},{7,5},{8,10},{9,11},{10,... | collective-permute-start | bytes 1572872 | tf_op jit(solution)/shard_map/ppermute | solution.py:282
  48.4 12.7 %collective-permute-start.3 = (bf16[128,2048]{1,0:T(8,128)(2,1)S(1)}, bf16[128,2048]{1,0:T(8,128)(2,1)S(1)}, u32[]{:S(2)}, u32[]{:S(2)}) collective-permute-start(bf16[128,2048]{1,0:T(8,128)(2,1)S(1)} %slice.90), channel_id=1, source_target_pairs={{0,1},{1,0},{2,3},{3,2},{4,5},{5,4},{6,7},{7,6},{8,9},{9,8},{10,11... | collective-permute-start | bytes 1572872 | tf_op jit(solution)/shard_map/ppermute | solution.py:283
  78.2 93.9 %copy-start.21 = (f32[2048,1]{0,1:T(1,128)}, f32[2048,1]{0,1:T(1,128)S(1)}, u32[]{:S(2)}) copy-start(f32[2048,1]{0,1:T(1,128)S(1)} %get-tuple-element.80) | copy-start | bytes 24580
  116.0 38.5 %copy-start.26 = (s32[1024]{0:T(1024)S(1)}, s32[1024]{0:T(1024)}, u32[]{:S(2)}) copy-start(s32[1024]{0:T(1024)} %copy-done.25) | copy-start | bytes 12292
  117.1 14.8 %collective-permute-start.5 = (bf16[128,2048]{1,0:T(8,128)(2,1)S(1)}, bf16[128,2048]{1,0:T(8,128)(2,1)S(1)}, u32[]{:S(2)}, u32[]{:S(2)}) collective-permute-start(bf16[128,2048]{1,0:T(8,128)(2,1)S(1)} %get-tuple-element.105), channel_id=1, source_target_pairs={{0,1},{1,0},{2,3},{3,2},{4,5},{5,4},{6,7},{7,6},{8,9},{9,8},{10,11... | collective-permute-start | bytes 1572872 | tf_op jit(solution)/shard_map/ppermute | solution.py:308
  118.7 23.9 %collective-permute-start.4 = (bf16[128,2048]{1,0:T(8,128)(2,1)}, bf16[128,2048]{1,0:T(8,128)(2,1)S(1)}, u32[]{:S(2)}, u32[]{:S(2)}) collective-permute-start(bf16[128,2048]{1,0:T(8,128)(2,1)} %get-tuple-element.102), channel_id=1, source_target_pairs={{0,1},{1,0},{2,3},{3,2},{4,5},{5,4},{6,7},{7,6},{8,9},{9,8},{10,11... | collective-permute-start | bytes 1572872 | tf_op jit(solution)/shard_map/ppermute | solution.py:308
  119.2 23.5 %collective-permute-start.8 = (bf16[128,2048]{1,0:T(8,128)(2,1)}, bf16[128,2048]{1,0:T(8,128)(2,1)S(1)}, u32[]{:S(2)}, u32[]{:S(2)}) collective-permute-start(bf16[128,2048]{1,0:T(8,128)(2,1)} %get-tuple-element.103), channel_id=1, source_target_pairs={{0,2},{1,3},{2,0},{3,1},{4,6},{5,7},{6,4},{7,5},{8,10},{9,11},{10,... | collective-permute-start | bytes 1572872 | tf_op jit(solution)/shard_map/ppermute | solution.py:308
  132.9 15.1 %collective-permute-start.6 = (bf16[128,2048]{1,0:T(8,128)(2,1)}, bf16[128,2048]{1,0:T(8,128)(2,1)}, u32[]{:S(2)}, u32[]{:S(2)}) collective-permute-start(bf16[128,2048]{1,0:T(8,128)(2,1)} %add_convert_fusion.7), channel_id=1, source_target_pairs={{0,2},{1,3},{2,0},{3,1},{4,6},{5,7},{6,4},{7,5},{8,10},{9,11},{10,... | collective-permute-start | bytes 1572872 | tf_op jit(solution)/shard_map/ppermute | solution.py:308
  134.4 24.8 %collective-permute-start.7 = (bf16[128,2048]{1,0:T(8,128)(2,1)}, bf16[128,2048]{1,0:T(8,128)(2,1)}, u32[]{:S(2)}, u32[]{:S(2)}) collective-permute-start(bf16[128,2048]{1,0:T(8,128)(2,1)} %get-tuple-element.104), channel_id=1, source_target_pairs={{0,2},{1,3},{2,0},{3,1},{4,6},{5,7},{6,4},{7,5},{8,10},{9,11},{10,... | collective-permute-start | bytes 1572872 | tf_op jit(solution)/shard_map/ppermute | solution.py:308
  151.1 15.1 %collective-permute-start.9 = (bf16[128,2048]{1,0:T(8,128)(2,1)}, bf16[128,2048]{1,0:T(8,128)(2,1)}, u32[]{:S(2)}, u32[]{:S(2)}) collective-permute-start(bf16[128,2048]{1,0:T(8,128)(2,1)} %get-tuple-element.101), channel_id=1, source_target_pairs={{0,1},{1,0},{2,3},{3,2},{4,5},{5,4},{6,7},{7,6},{8,9},{9,8},{10,11... | collective-permute-start | bytes 1572872 | tf_op jit(solution)/shard_map/ppermute | solution.py:308
  152.5 36.2 %collective-permute-start.14 = (bf16[256,2048]{1,0:T(8,128)(2,1)S(1)}, bf16[256,2048]{1,0:T(8,128)(2,1)}, u32[]{:S(2)}, u32[]{:S(2)}) collective-permute-start(bf16[256,2048]{1,0:T(8,128)(2,1)S(1)} %copy-done.6), channel_id=1, source_target_pairs={{0,1},{1,0},{2,3},{3,2},{4,5},{5,4},{6,7},{7,6},{8,9},{9,8},{10,11... | collective-permute-start | bytes 3145736 | tf_op jit(solution)/shard_map/ppermute | solution.py:280
  153.1 42.4 %collective-permute-start.15 = (bf16[256,2048]{1,0:T(8,128)(2,1)S(1)}, bf16[256,2048]{1,0:T(8,128)(2,1)}, u32[]{:S(2)}, u32[]{:S(2)}) collective-permute-start(bf16[256,2048]{1,0:T(8,128)(2,1)S(1)} %copy-done.6), channel_id=1, source_target_pairs={{0,2},{1,3},{2,0},{3,1},{4,6},{5,7},{6,4},{7,5},{8,10},{9,11},{10,... | collective-permute-start | bytes 3145736 | tf_op jit(solution)/shard_map/ppermute | solution.py:281
  173.4 37.6 %collective-permute-start.10 = (bf16[256,2048]{1,0:T(8,128)(2,1)S(1)}, bf16[256,2048]{1,0:T(8,128)(2,1)S(1)}, u32[]{:S(2)}, u32[]{:S(2)}) collective-permute-start(bf16[256,2048]{1,0:T(8,128)(2,1)S(1)} %get-tuple-element.77), channel_id=1, source_target_pairs={{0,1},{1,0},{2,3},{3,2},{4,5},{5,4},{6,7},{7,6},{8,9},{9,8},{10,11... | collective-permute-start | bytes 3145736 | tf_op jit(solution)/shard_map/ppermute | solution.py:280
  189.7 14.9 %collective-permute-start.16 = (bf16[128,2048]{1,0:T(8,128)(2,1)S(1)}, bf16[128,2048]{1,0:T(8,128)(2,1)S(1)}, u32[]{:S(2)}, u32[]{:S(2)}) collective-permute-start(bf16[128,2048]{1,0:T(8,128)(2,1)S(1)} %slice.98), channel_id=1, source_target_pairs={{0,2},{1,3},{2,0},{3,1},{4,6},{5,7},{6,4},{7,5},{8,10},{9,11},{10,... | collective-permute-start | bytes 1572872 | tf_op jit(solution)/shard_map/ppermute | solution.py:282
  191.2 31.5 %collective-permute-start.11 = (bf16[256,2048]{1,0:T(8,128)(2,1)S(1)}, bf16[256,2048]{1,0:T(8,128)(2,1)S(1)}, u32[]{:S(2)}, u32[]{:S(2)}) collective-permute-start(bf16[256,2048]{1,0:T(8,128)(2,1)S(1)} %get-tuple-element.77), channel_id=1, source_target_pairs={{0,2},{1,3},{2,0},{3,1},{4,6},{5,7},{6,4},{7,5},{8,10},{9,11},{10,... | collective-permute-start | bytes 3145736 | tf_op jit(solution)/shard_map/ppermute | solution.py:281
  196.6 21.9 %collective-permute-start.17 = (bf16[128,2048]{1,0:T(8,128)(2,1)S(1)}, bf16[128,2048]{1,0:T(8,128)(2,1)S(1)}, u32[]{:S(2)}, u32[]{:S(2)}) collective-permute-start(bf16[128,2048]{1,0:T(8,128)(2,1)S(1)} %slice.99), channel_id=1, source_target_pairs={{0,1},{1,0},{2,3},{3,2},{4,5},{5,4},{6,7},{7,6},{8,9},{9,8},{10,11... | collective-permute-start | bytes 1572872 | tf_op jit(solution)/shard_map/ppermute | solution.py:283
  211.1 17.3 %collective-permute-start.12 = (bf16[128,2048]{1,0:T(8,128)(2,1)S(1)}, bf16[128,2048]{1,0:T(8,128)(2,1)S(1)}, u32[]{:S(2)}, u32[]{:S(2)}) collective-permute-start(bf16[128,2048]{1,0:T(8,128)(2,1)S(1)} %slice.94), channel_id=1, source_target_pairs={{0,2},{1,3},{2,0},{3,1},{4,6},{5,7},{6,4},{7,5},{8,10},{9,11},{10,... | collective-permute-start | bytes 1572872 | tf_op jit(solution)/shard_map/ppermute | solution.py:282
  222.7 9.2 %collective-permute-start.13 = (bf16[128,2048]{1,0:T(8,128)(2,1)S(1)}, bf16[128,2048]{1,0:T(8,128)(2,1)S(1)}, u32[]{:S(2)}, u32[]{:S(2)}) collective-permute-start(bf16[128,2048]{1,0:T(8,128)(2,1)S(1)} %slice.95), channel_id=1, source_target_pairs={{0,1},{1,0},{2,3},{3,2},{4,5},{5,4},{6,7},{7,6},{8,9},{9,8},{10,11... | collective-permute-start | bytes 1572872 | tf_op jit(solution)/shard_map/ppermute | solution.py:283
  394.9 14.8 %collective-permute-start.19 = (bf16[128,2048]{1,0:T(8,128)(2,1)S(1)}, bf16[128,2048]{1,0:T(8,128)(2,1)S(1)}, u32[]{:S(2)}, u32[]{:S(2)}) collective-permute-start(bf16[128,2048]{1,0:T(8,128)(2,1)S(1)} %get-tuple-element.99), channel_id=1, source_target_pairs={{0,1},{1,0},{2,3},{3,2},{4,5},{5,4},{6,7},{7,6},{8,9},{9,8},{10,11... | collective-permute-start | bytes 1572872 | tf_op jit(solution)/shard_map/ppermute | solution.py:308
  396.4 23.8 %collective-permute-start.18 = (bf16[128,2048]{1,0:T(8,128)(2,1)S(1)}, bf16[128,2048]{1,0:T(8,128)(2,1)S(1)}, u32[]{:S(2)}, u32[]{:S(2)}) collective-permute-start(bf16[128,2048]{1,0:T(8,128)(2,1)S(1)} %get-tuple-element.96), channel_id=1, source_target_pairs={{0,1},{1,0},{2,3},{3,2},{4,5},{5,4},{6,7},{7,6},{8,9},{9,8},{10,11... | collective-permute-start | bytes 1572872 | tf_op jit(solution)/shard_map/ppermute | solution.py:308
  397.0 23.3 %collective-permute-start.22 = (bf16[128,2048]{1,0:T(8,128)(2,1)S(1)}, bf16[128,2048]{1,0:T(8,128)(2,1)S(1)}, u32[]{:S(2)}, u32[]{:S(2)}) collective-permute-start(bf16[128,2048]{1,0:T(8,128)(2,1)S(1)} %get-tuple-element.97), channel_id=1, source_target_pairs={{0,2},{1,3},{2,0},{3,1},{4,6},{5,7},{6,4},{7,5},{8,10},{9,11},{10,... | collective-permute-start | bytes 1572872 | tf_op jit(solution)/shard_map/ppermute | solution.py:308
  409.9 14.9 %collective-permute-start.20 = (bf16[128,2048]{1,0:T(8,128)(2,1)S(1)}, bf16[128,2048]{1,0:T(8,128)(2,1)S(1)}, u32[]{:S(2)}, u32[]{:S(2)}) collective-permute-start(bf16[128,2048]{1,0:T(8,128)(2,1)S(1)} %add_convert_fusion.5), channel_id=1, source_target_pairs={{0,2},{1,3},{2,0},{3,1},{4,6},{5,7},{6,4},{7,5},{8,10},{9,11},{10,... | collective-permute-start | bytes 1572872 | tf_op jit(solution)/shard_map/ppermute | solution.py:308
  411.4 40.8 %collective-permute-start.21 = (bf16[128,2048]{1,0:T(8,128)(2,1)}, bf16[128,2048]{1,0:T(8,128)(2,1)}, u32[]{:S(2)}, u32[]{:S(2)}) collective-permute-start(bf16[128,2048]{1,0:T(8,128)(2,1)} %get-tuple-element.98), channel_id=1, source_target_pairs={{0,2},{1,3},{2,0},{3,1},{4,6},{5,7},{6,4},{7,5},{8,10},{9,11},{10,... | collective-permute-start | bytes 1572872 | tf_op jit(solution)/shard_map/ppermute | solution.py:308
  426.0 26.2 %collective-permute-start.23 = (bf16[128,2048]{1,0:T(8,128)(2,1)}, bf16[128,2048]{1,0:T(8,128)(2,1)}, u32[]{:S(2)}, u32[]{:S(2)}) collective-permute-start(bf16[128,2048]{1,0:T(8,128)(2,1)} %get-tuple-element.95), channel_id=1, source_target_pairs={{0,1},{1,0},{2,3},{3,2},{4,5},{5,4},{6,7},{7,6},{8,9},{9,8},{10,11... | collective-permute-start | bytes 1572872 | tf_op jit(solution)/shard_map/ppermute | solution.py:308
  456.0 21.3 %collective-permute-start.24 = (bf16[256,2048]{1,0:T(8,128)(2,1)S(1)}, bf16[256,2048]{1,0:T(8,128)(2,1)S(1)}, u32[]{:S(2)}, u32[]{:S(2)}) collective-permute-start(bf16[256,2048]{1,0:T(8,128)(2,1)S(1)} %multiply_convert_fusion), channel_id=1, source_target_pairs={{0,1},{1,0},{2,3},{3,2},{4,5},{5,4},{6,7},{7,6},{8,9},{9,8},{10,11... | collective-permute-start | bytes 3145736 | tf_op jit(solution)/shard_map/ppermute | solution.py:280
  456.6 23.9 %collective-permute-start.25 = (bf16[256,2048]{1,0:T(8,128)(2,1)S(1)}, bf16[256,2048]{1,0:T(8,128)(2,1)S(1)}, u32[]{:S(2)}, u32[]{:S(2)}) collective-permute-start(bf16[256,2048]{1,0:T(8,128)(2,1)S(1)} %multiply_convert_fusion), channel_id=1, source_target_pairs={{0,2},{1,3},{2,0},{3,1},{4,6},{5,7},{6,4},{7,5},{8,10},{9,11},{10,... | collective-permute-start | bytes 3145736 | tf_op jit(solution)/shard_map/ppermute | solution.py:281
  477.3 10.6 %collective-permute-start.26 = (bf16[128,2048]{1,0:T(8,128)(2,1)S(1)}, bf16[128,2048]{1,0:T(8,128)(2,1)S(1)}, u32[]{:S(2)}, u32[]{:S(2)}) collective-permute-start(bf16[128,2048]{1,0:T(8,128)(2,1)S(1)} %slice.100), channel_id=1, source_target_pairs={{0,2},{1,3},{2,0},{3,1},{4,6},{5,7},{6,4},{7,5},{8,10},{9,11},{10,... | collective-permute-start | bytes 1572872 | tf_op jit(solution)/shard_map/ppermute | solution.py:282
  480.6 9.2 %collective-permute-start.27 = (bf16[128,2048]{1,0:T(8,128)(2,1)S(1)}, bf16[128,2048]{1,0:T(8,128)(2,1)S(1)}, u32[]{:S(2)}, u32[]{:S(2)}) collective-permute-start(bf16[128,2048]{1,0:T(8,128)(2,1)S(1)} %slice.101), channel_id=1, source_target_pairs={{0,1},{1,0},{2,3},{3,2},{4,5},{5,4},{6,7},{7,6},{8,9},{9,8},{10,11... | collective-permute-start | bytes 1572872 | tf_op jit(solution)/shard_map/ppermute | solution.py:283
  530.5 149.7 %reduce-scatter.8.cloned.1.call-start = ((), (), s32[]{:S(2)}) async-start(), calls=%async_computation.8 | async-start | bytes 9437184 | tf_op jit(solution)/shard_map/reduce_scatter | solution.py:339
  531.0 318.0 %reduce-scatter.6.cloned.1.call-start = ((), (), s32[]{:S(2)}) async-start(), calls=%async_computation.7 | async-start | bytes 18874368 | tf_op jit(solution)/shard_map/reduce_scatter | solution.py:339
  540.6 15.0 %collective-permute-start.35 = (bf16[128,2048]{1,0:T(8,128)(2,1)}, bf16[128,2048]{1,0:T(8,128)(2,1)S(1)}, u32[]{:S(2)}, u32[]{:S(2)}) collective-permute-start(bf16[128,2048]{1,0:T(8,128)(2,1)} %get-tuple-element.87), channel_id=1, source_target_pairs={{0,1},{1,0},{2,3},{3,2},{4,5},{5,4},{6,7},{7,6},{8,9},{9,8},{10,11... | collective-permute-start | bytes 1572872 | tf_op jit(solution)/shard_map/ppermute | solution.py:308
  542.3 35.8 %collective-permute-start.34 = (bf16[128,2048]{1,0:T(8,128)(2,1)}, bf16[128,2048]{1,0:T(8,128)(2,1)S(1)}, u32[]{:S(2)}, u32[]{:S(2)}) collective-permute-start(bf16[128,2048]{1,0:T(8,128)(2,1)} %get-tuple-element.84), channel_id=1, source_target_pairs={{0,1},{1,0},{2,3},{3,2},{4,5},{5,4},{6,7},{7,6},{8,9},{9,8},{10,11... | collective-permute-start | bytes 1572872 | tf_op jit(solution)/shard_map/ppermute | solution.py:308
  542.7 36.9 %collective-permute-start.38 = (bf16[128,2048]{1,0:T(8,128)(2,1)S(1)}, bf16[128,2048]{1,0:T(8,128)(2,1)S(1)}, u32[]{:S(2)}, u32[]{:S(2)}) collective-permute-start(bf16[128,2048]{1,0:T(8,128)(2,1)S(1)} %get-tuple-element.85), channel_id=1, source_target_pairs={{0,2},{1,3},{2,0},{3,1},{4,6},{5,7},{6,4},{7,5},{8,10},{9,11},{10,... | collective-permute-start | bytes 1572872 | tf_op jit(solution)/shard_map/ppermute | solution.py:308
  546.2 29.0 %collective-permute-start.29 = (bf16[128,2048]{1,0:T(8,128)(2,1)S(1)}, bf16[128,2048]{1,0:T(8,128)(2,1)S(1)}, u32[]{:S(2)}, u32[]{:S(2)}) collective-permute-start(bf16[128,2048]{1,0:T(8,128)(2,1)S(1)} %get-tuple-element.93), channel_id=1, source_target_pairs={{0,1},{1,0},{2,3},{3,2},{4,5},{5,4},{6,7},{7,6},{8,9},{9,8},{10,11... | collective-permute-start | bytes 1572872 | tf_op jit(solution)/shard_map/ppermute | solution.py:308
  555.8 24.4 %collective-permute-start.36 = (bf16[128,2048]{1,0:T(8,128)(2,1)S(1)}, bf16[128,2048]{1,0:T(8,128)(2,1)S(1)}, u32[]{:S(2)}, u32[]{:S(2)}) collective-permute-start(bf16[128,2048]{1,0:T(8,128)(2,1)S(1)} %add_convert_fusion.1), channel_id=1, source_target_pairs={{0,2},{1,3},{2,0},{3,1},{4,6},{5,7},{6,4},{7,5},{8,10},{9,11},{10,... | collective-permute-start | bytes 1572872 | tf_op jit(solution)/shard_map/ppermute | solution.py:308
  556.9 55.4 %collective-permute-start.37 = (bf16[128,2048]{1,0:T(8,128)(2,1)}, bf16[128,2048]{1,0:T(8,128)(2,1)S(1)}, u32[]{:S(2)}, u32[]{:S(2)}) collective-permute-start(bf16[128,2048]{1,0:T(8,128)(2,1)} %get-tuple-element.86), channel_id=1, source_target_pairs={{0,2},{1,3},{2,0},{3,1},{4,6},{5,7},{6,4},{7,5},{8,10},{9,11},{10,... | collective-permute-start | bytes 1572872 | tf_op jit(solution)/shard_map/ppermute | solution.py:308
  575.2 14.1 %collective-permute-start.28 = (bf16[128,2048]{1,0:T(8,128)(2,1)S(1)}, bf16[128,2048]{1,0:T(8,128)(2,1)S(1)}, u32[]{:S(2)}, u32[]{:S(2)}) collective-permute-start(bf16[128,2048]{1,0:T(8,128)(2,1)S(1)} %get-tuple-element.90), channel_id=1, source_target_pairs={{0,1},{1,0},{2,3},{3,2},{4,5},{5,4},{6,7},{7,6},{8,9},{9,8},{10,11... | collective-permute-start | bytes 1572872 | tf_op jit(solution)/shard_map/ppermute | solution.py:308
  578.1 14.9 %collective-permute-start.32 = (bf16[128,2048]{1,0:T(8,128)(2,1)S(1)}, bf16[128,2048]{1,0:T(8,128)(2,1)S(1)}, u32[]{:S(2)}, u32[]{:S(2)}) collective-permute-start(bf16[128,2048]{1,0:T(8,128)(2,1)S(1)} %get-tuple-element.91), channel_id=1, source_target_pairs={{0,2},{1,3},{2,0},{3,1},{4,6},{5,7},{6,4},{7,5},{8,10},{9,11},{10,... | collective-permute-start | bytes 1572872 | tf_op jit(solution)/shard_map/ppermute | solution.py:308
  579.6 75.3 %collective-permute-start.31 = (bf16[128,2048]{1,0:T(8,128)(2,1)}, bf16[128,2048]{1,0:T(8,128)(2,1)}, u32[]{:S(2)}, u32[]{:S(2)}) collective-permute-start(bf16[128,2048]{1,0:T(8,128)(2,1)} %get-tuple-element.92), channel_id=1, source_target_pairs={{0,2},{1,3},{2,0},{3,1},{4,6},{5,7},{6,4},{7,5},{8,10},{9,11},{10,... | collective-permute-start | bytes 1572872 | tf_op jit(solution)/shard_map/ppermute | solution.py:308
  580.2 27.5 %collective-permute-start.30 = (bf16[128,2048]{1,0:T(8,128)(2,1)S(1)}, bf16[128,2048]{1,0:T(8,128)(2,1)S(1)}, u32[]{:S(2)}, u32[]{:S(2)}) collective-permute-start(bf16[128,2048]{1,0:T(8,128)(2,1)S(1)} %add_convert_fusion.3), channel_id=1, source_target_pairs={{0,2},{1,3},{2,0},{3,1},{4,6},{5,7},{6,4},{7,5},{8,10},{9,11},{10,... | collective-permute-start | bytes 1572872 | tf_op jit(solution)/shard_map/ppermute | solution.py:308
  589.3 23.0 %collective-permute-start.39 = (bf16[128,2048]{1,0:T(8,128)(2,1)S(1)}, bf16[128,2048]{1,0:T(8,128)(2,1)S(1)}, u32[]{:S(2)}, u32[]{:S(2)}) collective-permute-start(bf16[128,2048]{1,0:T(8,128)(2,1)S(1)} %get-tuple-element.83), channel_id=1, source_target_pairs={{0,1},{1,0},{2,3},{3,2},{4,5},{5,4},{6,7},{7,6},{8,9},{9,8},{10,11... | collective-permute-start | bytes 1572872 | tf_op jit(solution)/shard_map/ppermute | solution.py:308
  610.5 44.4 %collective-permute-start.33 = (bf16[128,2048]{1,0:T(8,128)(2,1)}, bf16[128,2048]{1,0:T(8,128)(2,1)}, u32[]{:S(2)}, u32[]{:S(2)}) collective-permute-start(bf16[128,2048]{1,0:T(8,128)(2,1)} %get-tuple-element.89), channel_id=1, source_target_pairs={{0,1},{1,0},{2,3},{3,2},{4,5},{5,4},{6,7},{7,6},{8,9},{9,8},{10,11... | collective-permute-start | bytes 1572872 | tf_op jit(solution)/shard_map/ppermute | solution.py:308
  (34 other events, 370.4 us)
Sparse Core Ops, SparseCore 0:
  13.8 63.5 all-gather.3
  78.9 80.6 all-gather.7
  161.8 149.2 all-gather.5
  530.6 58.2 reduce-scatter.3
  591.1 89.0 reduce-scatter.7
  682.4 166.6 reduce-scatter.5

commit v3 on v2

--- a/solution.py
+++ b/solution.py
@@ -4,6 +4,7 @@
 import jax.numpy as jnp
 from jax import lax
 from jax.experimental import pallas as pl
+from jax.experimental.layout import Layout, with_layout_constraint
 from jax.experimental.pallas import tpu as pltpu
 from jax.sharding import PartitionSpec as P
 
@@ -187,33 +188,37 @@
         ).astype(jnp.bfloat16)
 
 
-def activation_back_kernel(pair_ref, grad_ref, out_ref):
+def activation_kernel(pair_ref, grad_ref, act_ref, out_ref):
     units = grad_ref.shape[1]
     gate, up = pair_ref[:, :units], pair_ref[:, units:]
     grad = grad_ref[...]
     sigmoid_gate = 1.0 / (1.0 + jnp.exp(-gate))
+    act_ref[...] = (gate * sigmoid_gate * up).astype(jnp.bfloat16)
     grad_gate = grad * up * sigmoid_gate * (1.0 + gate * (1.0 - sigmoid_gate))
     out_ref[:, :units] = grad_gate.astype(jnp.bfloat16)
     out_ref[:, units:] = (grad * gate * sigmoid_gate).astype(jnp.bfloat16)
 
 
-def activation_back(pair, grad):
+def activation_both(pair, grad):
     rows, units = grad.shape
-    block = min(rows, 128)
+    block = min(rows, 256)
 
     def at(row):
         return (row, 0)
 
     return pl.pallas_call(
-        activation_back_kernel,
-        out_shape=jax.ShapeDtypeStruct(pair.shape, jnp.bfloat16),
+        activation_kernel,
+        out_shape=(
+            jax.ShapeDtypeStruct(grad.shape, jnp.bfloat16),
+            jax.ShapeDtypeStruct(pair.shape, jnp.bfloat16),
+        ),
         grid=(rows // block,),
         in_specs=[pl.BlockSpec((block, 2 * units), at), pl.BlockSpec((block, units), at)],
-        out_specs=pl.BlockSpec((block, 2 * units), at),
+        out_specs=(pl.BlockSpec((block, units), at), pl.BlockSpec((block, 2 * units), at)),
         cost_estimate=pl.CostEstimate(
-            flops=20 * pair.size, bytes_accessed=8 * pair.size, transcendentals=pair.size
-        ),
-        name="activation_back",
+            flops=20 * pair.size, bytes_accessed=9 * pair.size, transcendentals=pair.size
+        ),
+        name="activation_both",
     )(pair, grad)
 
 
@@ -270,7 +275,7 @@
     return [(i, i ^ mask) for i in range(count)]
 
 
-def gather_rows_plain(block, axis):
+def gather_rows(block, axis, relative=False):
     count = lax.axis_size(axis)
     if count != 4:
         return lax.all_gather(block, axis, axis=0, tiled=True)
@@ -281,6 +286,8 @@
     from_y = lax.ppermute(block, axis, shift_pairs(count, 2))
     far_top = lax.ppermute(from_x[:half], axis, shift_pairs(count, 2))
     far_low = lax.ppermute(from_y[half:], axis, shift_pairs(count, 1))
+    if relative:
+        return jnp.concatenate([block, from_x, from_y, far_top, far_low], axis=0)
     whole = jnp.zeros((count * rows, block.shape[1]), block.dtype)
     for mask, piece, extra in (
         (0, block, 0),
@@ -290,14 +297,14 @@
         (3, far_low, half),
     ):
         whole = lax.dynamic_update_slice(whole, piece, ((me ^ mask) * rows + extra, 0))
-    return whole
-
-
-def scatter_rows_plain(partial, axis):
+    return row_major(whole)
+
+
+def scatter_rows(partial, axis, relative=False):
     count = lax.axis_size(axis)
     if count != 4:
         return lax.psum_scatter(partial, axis, scatter_dimension=0, tiled=True).astype(jnp.float32)
-    me = lax.axis_index(axis)
+    me = 0 if relative else lax.axis_index(axis)
     rows = partial.shape[0] // count
     half = rows // 2
 
@@ -311,11 +318,76 @@
     relay_low = send(part(3, half), 2).astype(jnp.float32)
     near_top = send(part(1, 0), 1).astype(jnp.float32)
     near_low = send(part(2, half), 2).astype(jnp.float32)
-    joined_top = send((part(2, 0) + relay_top).astype(jnp.bfloat16), 2).astype(jnp.float32)
-    joined_low = send((part(1, half) + relay_low).astype(jnp.bfloat16), 1).astype(jnp.float32)
+    joined_top = send(narrow(part(2, 0) + relay_top), 2).astype(jnp.float32)
+    joined_low = send(narrow(part(1, half) + relay_low), 1).astype(jnp.float32)
     return jnp.concatenate(
         [part(0, 0) + near_top + joined_top, part(0, half) + near_low + joined_low], axis=0
     )
+
+
+def paired():
+    count = lax.axis_size("dp")
+    return count > 2 and count % 2 == 0
+
+
+def row_major(value):
+    return with_layout_constraint(value, Layout(major_to_minor=(0, 1)))
+
+
+def split_columns(rows):
+    count = lax.axis_size("dp")
+    if not paired():
+        return rows, None
+    width = rows.shape[1] // count
+    core = lax.axis_index("dp") % 2
+
+    def half(which):
+        return row_major(
+            jnp.concatenate(
+                [
+                    lax.dynamic_slice_in_dim(rows, (first + which) * width, width, 1)
+                    for first in range(0, count, 2)
+                ],
+                axis=1,
+            )
+        )
+
+    return half(core), half(1 - core)
+
+
+def weight_sums(pairs):
+    keeps = []
+    for (keep_rows, send_rows), right in pairs:
+        if send_rows is None:
+            keeps.append(narrow(contract(keep_rows, right, 0, 0)))
+            continue
+        sent = narrow(contract(send_rows, right, 0, 0))
+        count = lax.axis_size("dp")
+        got = lax.ppermute(sent, "dp", shift_pairs(count, 1))
+        keeps.append(narrow(contract(keep_rows, right, 0, 0) + got.astype(jnp.float32)))
+    return row_major(jnp.concatenate(keeps, axis=1))
+
+
+def sum_shards(partial):
+    count = lax.axis_size("dp")
+    groups = [list(range(core, count, 2)) for core in range(2)] if paired() else None
+    summed = lax.psum_scatter(
+        partial, "dp", scatter_dimension=0, tiled=True, axis_index_groups=groups
+    )
+    return summed.astype(jnp.float32)
+
+
+def sum_everywhere(value):
+    for axis in ("tensor", "dp"):
+        count = lax.axis_size(axis)
+        if count & (count - 1):
+            value = lax.psum(value, axis)
+            continue
+        step = 1
+        while step < count:
+            value = value + lax.ppermute(value, axis, shift_pairs(count, step))
+            step *= 2
+    return value
 
 
 def product(left, right):
@@ -333,10 +405,6 @@
 
 def ordered(*values):
     return lax.optimization_barrier(values)
-
-
-def sum_shards(partial, dimension):
-    return lax.psum_scatter(partial, "dp", scatter_dimension=dimension, tiled=True)
 
 
 def narrow(value):
@@ -367,7 +435,7 @@
     cosine, sine_part = rope_tables(positions, HEAD_SIZE)
     gains = jnp.pad(jnp.stack([attn_gain, mlp_gain], axis=1), ((0, 0), (0, 126)))
     packed = lax.all_gather(
-        jnp.concatenate([w_query, w_key, value_weight, gains, w_output.T], axis=1),
+        row_major(jnp.concatenate([w_query, w_key, value_weight, gains, w_output.T], axis=1)),
         "dp",
         axis=0,
         tiled=True,
@@ -376,54 +444,68 @@
     gain_one = packed[:, joint].astype(jnp.float32)
     gain_two = packed[:, joint + 1].astype(jnp.float32)
     full_output = packed[:, joint + gains.shape[1] :]
-    full_pair = lax.all_gather(
-        jnp.concatenate([w_gate, w_up], axis=1), "dp", axis=0, tiled=True
-    )
-    full_down = lax.all_gather(w_down, "dp", axis=1, tiled=True)
+    hidden_half = w_gate.shape[1] // 2
+    down_turned = w_down.T
+    halves = [
+        lax.all_gather(
+            row_major(
+                jnp.concatenate([w_gate[:, part], w_up[:, part], down_turned[:, part]], axis=1)
+            ),
+            "dp",
+            axis=0,
+            tiled=True,
+        )
+        for part in (slice(0, hidden_half), slice(hidden_half, 2 * hidden_half))
+    ]
 
     grad_out = out_grad.astype(jnp.float32)
     head_count = query_cols // HEAD_SIZE
     kv_heads = key_cols // HEAD_SIZE
     residual = inputs.astype(jnp.float32)
     scale_one, unit_one = rms_stats(residual)
-    inputs_all = gather_rows_plain(inputs, "tensor")
-    cotangent_all = gather_rows_plain(out_grad, "tensor")
-    normed_one_all = narrow(rms_stats(inputs_all.astype(jnp.float32))[1] * gain_one)
-    grad_mlp_all = cotangent_all * narrow(valid_rows)[:, None]
+    inputs_all = gather_rows(inputs, "tensor")
+    grad_mlp_all = gather_rows(narrow(grad_out * valid_own), "tensor", relative=True)
+    normed_one_all = row_major(narrow(rms_stats(inputs_all.astype(jnp.float32))[1] * gain_one))
     seg_row, seg_col = document_segment[None, :], document_segment[:, None]
     joint_turned = contract(full_joint, normed_one_all, 0, 1)
     rotated, attended, log_total = attend(
         joint_turned, cosine, sine_part, seg_row, seg_col, head_count, kv_heads, QBLK
     )
-    attn_out = scatter_rows_plain(narrow(contract(attended, full_output, 0, 1)), "tensor")
+    attn_out = scatter_rows(narrow(contract(attended, full_output, 0, 1)), "tensor")
     hidden = residual + valid_own * attn_out
     scale_two, unit_two = rms_stats(hidden)
-    normed_two_all = gather_rows_plain(narrow(unit_two * gain_two), "tensor")
-    hidden_units = w_gate.shape[1]
-    pair_pre = product(normed_two_all, full_pair)
-    gate_pre, up_proj = pair_pre[:, :hidden_units], pair_pre[:, hidden_units:]
-    activation = narrow(gate_pre * jax.nn.sigmoid(gate_pre) * up_proj)
-    down_part = narrow(product(activation.T, grad_mlp_all))
-    pair_pre, down_part = ordered(pair_pre, down_part)
-    w_down_grad = sum_shards(down_part, 1)
-    grad_act = product(grad_mlp_all, full_down.T)
-    grad_pair = activation_back(pair_pre, grad_act)
-    normed_part = narrow(contract(grad_pair, full_pair, 1, 1))
-    grad_pair, normed_part = ordered(grad_pair, normed_part)
-    grad_normed_two = scatter_rows_plain(normed_part, "tensor")
-    pair_part = narrow(contract(normed_two_all, grad_pair, 0, 0))
-    grad_normed_two, pair_part = ordered(grad_normed_two, pair_part)
-    pair_grad = sum_shards(pair_part, 0).astype(jnp.float32)
+    normed_two_all = gather_rows(narrow(unit_two * gain_two), "tensor", relative=True)
+    pair_cols = 2 * hidden_half
+    normed_split, cotangent_split = split_columns(normed_two_all), split_columns(grad_mlp_all)
+    normed_total = mlp_total = None
+    weight_grads = []
+    for number, weights in enumerate(halves):
+        pair_weights, down_weights = weights[:, :pair_cols], weights[:, pair_cols:]
+        pair_pre = product(normed_two_all, pair_weights)
+        grad_act = product(grad_mlp_all, down_weights)
+        activation, grad_pair = activation_both(pair_pre, grad_act)
+        if number == 1:
+            normed_total = narrow(normed_total + contract(grad_pair, pair_weights, 1, 1))
+            grad_pair, activation, normed_total = ordered(grad_pair, activation, normed_total)
+            grad_normed_two = scatter_rows(normed_total, "tensor", relative=True)
+        partial = weight_sums(((normed_split, grad_pair), (cotangent_split, activation)))
+        if number == 0:
+            grad_pair, activation, partial = ordered(grad_pair, activation, partial)
+            normed_total = contract(grad_pair, pair_weights, 1, 1)
+            mlp_total = contract(activation, down_weights, 1, 1)
+            normed_two_all, grad_mlp_all, partial, normed_total, mlp_total = ordered(
+                normed_two_all, grad_mlp_all, partial, normed_total, mlp_total
+            )
+        weight_grads.append(sum_shards(partial))
     mlp_gain_part = jnp.sum(grad_normed_two * unit_two, axis=0)
     grad_hidden = grad_out + norm_backward(grad_normed_two, unit_two, scale_two, gain_two)
     grad_attn = narrow(grad_hidden * valid_own)
     activation, grad_attn = ordered(activation, grad_attn)
-    grad_attn_all = gather_rows_plain(grad_attn, "tensor")
-    mlp_part = narrow(product(activation, full_down))
+    grad_attn_all = gather_rows(grad_attn, "tensor")
+    mlp_part = narrow(mlp_total + contract(activation, down_weights, 1, 1))
     grad_attn_all, mlp_part = ordered(grad_attn_all, mlp_part)
-    mlp_out = scatter_rows_plain(mlp_part, "tensor")
+    mlp_out = scatter_rows(mlp_part, "tensor", relative=True)
     output = hidden + valid_own * mlp_out
-    out_part = narrow(contract(grad_attn_all, attended, 0, 1))
     grad_attended = narrow(contract(full_output, grad_attn_all, 0, 1))
     joint_back = attend_back(
         rotated,
@@ -438,12 +520,19 @@
         kv_heads,
         QBLK,
     )
-    joint_part = narrow(contract(normed_one_all, joint_back, 0, 1))
-    tail_grad = sum_shards(jnp.concatenate([joint_part, out_part], axis=1), 0).astype(jnp.float32)
-    grad_normed_one = scatter_rows_plain(narrow(contract(joint_back, full_joint, 0, 1)), "tensor")
+    last_part = narrow(contract(joint_back, full_joint, 0, 1))
+    joint_back, last_part = ordered(joint_back, last_part)
+    grad_normed_one = scatter_rows(last_part, "tensor")
+    tail = weight_sums(
+        (
+            (split_columns(normed_one_all), joint_back.T),
+            (split_columns(grad_attn_all), attended.T),
+        ),
+    )
+    tail_grad = sum_shards(tail)
     attn_gain_part = jnp.sum(grad_normed_one * unit_one, axis=0)
     input_grad = grad_hidden + norm_backward(grad_normed_one, unit_one, scale_one, gain_one)
-    gain_sums = lax.psum(jnp.stack([attn_gain_part, mlp_gain_part]), ("dp", "tensor"))
+    gain_sums = sum_everywhere(jnp.stack([attn_gain_part, mlp_gain_part]))
     gain_rows = attn_gain.shape[0]
     gain_own = lax.dynamic_slice_in_dim(gain_sums, lax.axis_index("dp") * gain_rows, gain_rows, 1)
     return (
@@ -455,9 +544,9 @@
         tail_grad[:, query_cols + key_cols : joint],
         tail_grad[:, joint:].T,
         gain_own[1],
-        pair_grad[:, :hidden_units],
-        pair_grad[:, hidden_units:],
-        w_down_grad.astype(jnp.float32),
+        jnp.concatenate([half[:, :hidden_half] for half in weight_grads], axis=1),
+        jnp.concatenate([half[:, hidden_half:pair_cols] for half in weight_grads], axis=1),
+        jnp.concatenate([half[:, pair_cols:].T for half in weight_grads], axis=0),
     )
 
 

time: 866 us -> 799 us (0.923)
  waiting for transfers between devices: 436 us -> 380 us
  blocking collectives: 40.7 us -> 0 us
  other arithmetic: 43.6 us -> 72.1 us
  matrix products: 144 us -> 154 us
  local copies, waits for them, and re-layouts: 65.2 us -> 56.3 us
    all_gather x3, waiting for transfers between devices: 75.9 us -> 10.6 us  [the longest x1 10.6 us: whole_block(): lax.all_gather(row_major(jnp.concatenate([w_query, w_key, value_weight, g...]
    psum x1 -> x0, blocking collectives: 40.7 us -> none  [whole_block(): lax.psum(jnp.stack([attn_gain_part, mlp_gain_part]), ('dp', 'tensor'))]
    reduce_scatter x3, waiting for transfers between devices: 177 us -> 142 us  [sum_shards(): lax.psum_scatter(partial, 'dp', scatter_dimension=0, tiled=True, axis_ind...]
    dot_general x8 -> x20, matrix products: 81.2 us -> 111 us  [contract(): lax.dot_general(left, right, (((left_axis,), (right_axis,)), ((), ())), p...]
    ppermute x16 -> x27, waiting for transfers between devices: 73.9 us -> 99.3 us  [the longest x4 37.3 us: gather_rows(): far_top = lax.ppermute(from_x[:half], axis, shift_pairs(count, 2))]
    convert_element_type x3 -> x8, other arithmetic: 3.32 us -> 25.1 us  [narrow(): return value.astype(jnp.bfloat16)]
    ppermute x24, waiting for transfers between devices: 107 us -> 127 us  [send(): return lax.ppermute(piece, axis, shift_pairs(count, mask))]
    dot_general x4, matrix products: 62.9 us -> 43.4 us  [product(): return jnp.dot(left, right, preferred_element_type=jnp.float32)]
  transfers between devices with their start and end apart: 46 -> 57, of which waited for: 30 -> 39; matrix products, arithmetic and copies ran while one was open for 17% -> 24% of each run, Pallas kernels for 3% -> 4%
where the time goes in v3:
time: 799 us; the launch traced here: 790 us
  waiting for transfers between devices  380 us (48%)
  matrix products  154 us (19%)
  other arithmetic  72.1 us (9%)
  Pallas kernels  64.6 us (8%)
  local copies, waits for them, and re-layouts  56.3 us (7%)
  starting transfers between devices  47.6 us (6%)
  between operations  15.9 us (2%)
    reduce_scatter x3, waiting for transfers between devices, sum_shards(): lax.psum_scatter(partial, 'dp', scatter_dimension=0, tiled=True, axis_ind...  142 us
    ppermute x24, waiting for transfers between devices, send(): return lax.ppermute(piece, axis, shift_pairs(count, mask))  127 us
    dot_general x20, matrix products, contract(): lax.dot_general(left, right, (((left_axis,), (right_axis,)), ((), ())), p...  111 us
    dot_general x4, matrix products, product(): return jnp.dot(left, right, preferred_element_type=jnp.float32)  43.4 us
    ppermute x4, waiting for transfers between devices, gather_rows(): far_top = lax.ppermute(from_x[:half], axis, shift_pairs(count, 2))  37.3 us
    ppermute x4, waiting for transfers between devices, gather_rows(): from_x = lax.ppermute(block, axis, shift_pairs(count, 1))  30 us
    pallas_call x1, Pallas kernels, attend(): pl.pallas_call(functools.partial(attend_kernel, heads, kv_heads, block),...  25.9 us
    convert_element_type x8, other arithmetic, narrow(): return value.astype(jnp.bfloat16)  25.1 us
  transfers between devices with their start and end apart: 57, of which 39 were waited for; matrix products, arithmetic and copies ran while one was open for 24% of the time, Pallas kernels for 4%

profile of v3, /device:TPU:0, one launch (start us, length us, event | category | flops | bytes accessed | tf_op | source)
XLA Modules:
  0.0 790.1 jit_solution(8916048486098194719)
XLA Ops:
  29.7 15.0 %collective-permute-done = bf16[256,2048]{1,0:T(8,128)(2,1)S(1)} collective-permute-done((bf16[256,2048]{1,0:T(8,128)(2,1)S(1)}, bf16[256,2048]{1,0:T(8,128)(2,1)S(1)}, u32[]{:S(2)}, u32[]{:S(2)}) %collective-permute-start) | collective-permute-done | bytes 1048608 | tf_op jit(solution)/shard_map/ppermute | solution.py:285
  53.3 5.8 collective-permute-done.2
  66.2 10.6 %all-gather.4.cloned.1.call-done = bf16[2048,1408]{1,0:T(8,128)(2,1)} async-done(((bf16[256,1408]{1,0:T(8,128)(2,1)}), bf16[2048,1408]{1,0:T(8,128)(2,1)}) %all-gather.4.cloned.1.call-update) | async-done | bytes 5767184 | tf_op jit(solution)/shard_map/all_gather | solution.py:437
  82.6 5.1 fusion.23.joint_ref
  87.7 25.9 %attend.1 = (bf16[768,1024]{1,0:T(8,128)(2,1)}, bf16[512,1024]{1,0:T(8,128)(2,1)}, f32[8,1024]{1,0:T(8,128)}) custom-call(f32[768,1024]{1,0:T(8,128)} %fusion.23.joint_ref, f32[32,1024]{1,0:T(8,128)} %get-tuple-element.189.cos_ref, f32[32,1024]{1,0:T(8,128)} %get-tuple-element.188.sin_ref, s32[1,1024]{1,0:T(1,128)} %bitcast.50, s32[1024,1]{1,0:T(8,128)} %copy.56.seg_col_ref), custom_call_target="tpu_custom_call" | custom-call | flops 8589934592 | bytes 6291456 | tf_op jit(solution)/shard_map/attend/pallas_call | solution.py:232
  113.6 4.3 convolution_convert_fusion
  122.9 11.0 %collective-permute-done.5 = bf16[128,2048]{1,0:T(8,128)(2,1)S(1)} collective-permute-done((bf16[128,2048]{1,0:T(8,128)(2,1)S(1)}, bf16[128,2048]{1,0:T(8,128)(2,1)S(1)}, u32[]{:S(2)}, u32[]{:S(2)}) %collective-permute-start.5) | collective-permute-done | bytes 524320 | tf_op jit(solution)/shard_map/ppermute | solution.py:315
  137.0 7.5 collective-permute-done.4
  161.2 6.8 collective-permute-done.9
  177.0 13.4 %collective-permute-done.14 = bf16[256,2048]{1,0:T(8,128)(2,1)S(1)} collective-permute-done((bf16[256,2048]{1,0:T(8,128)(2,1)}, bf16[256,2048]{1,0:T(8,128)(2,1)S(1)}, u32[]{:S(2)}, u32[]{:S(2)}) %collective-permute-start.14) | collective-permute-done | bytes 1048608 | tf_op jit(solution)/shard_map/ppermute | solution.py:285
  199.6 15.8 %collective-permute-done.16 = bf16[128,2048]{1,0:T(8,128)(2,1)} collective-permute-done((bf16[128,2048]{1,0:T(8,128)(2,1)}, bf16[128,2048]{1,0:T(8,128)(2,1)}, u32[]{:S(2)}, u32[]{:S(2)}) %collective-permute-start.16) | collective-permute-done | bytes 524320 | tf_op jit(solution)/shard_map/ppermute | solution.py:287
  221.6 7.6 collective-permute-done.12
  236.2 11.0 %fusion.17.grad_ref = f32[1024,1024]{1,0:T(8,128)} fusion(bf16[1024,2048]{1,0:T(8,128)(2,1)} %constant_dynamic-update-slice_fusion.8, bf16[2048,3072]{1,0:T(8,128)(2,1)} %all-gather.6.cloned.1.call-done), kind=kOutput, calls=%fused_computation.31 | convolution fusion | flops 4294967296 | bytes 12582912 | tf_op jit(solution)/shard_map/dot_general | solution.py:394
  247.2 11.1 %fusion.9.pair_ref = f32[1024,2048]{1,0:T(8,128)} fusion(bf16[1024,2048]{1,0:T(8,128)(2,1)S(1)} %copy-done.14, bf16[2048,3072]{1,0:T(8,128)(2,1)S(1)} %copy-done.79), kind=kOutput, calls=%fused_computation.15 | convolution fusion | flops 8589934592 | bytes 20971520 | tf_op jit(solution)/shard_map/dot_general | solution.py:394
  258.3 8.0 %activation_both.2 = (bf16[1024,1024]{1,0:T(8,128)(2,1)}, bf16[1024,2048]{1,0:T(8,128)(2,1)}) custom-call(f32[1024,2048]{1,0:T(8,128)} %fusion.9.pair_ref, f32[1024,1024]{1,0:T(8,128)} %fusion.17.grad_ref), custom_call_target="tpu_custom_call" | custom-call | flops 41943040 | bytes 18874368 | tf_op jit(solution)/shard_map/activation_both/pallas_call | solution.py:209
  266.4 7.5 convolution_convert_fusion.3
  277.0 7.7 collective-permute-done.19
  287.2 5.1 add_convert_fusion.3
  295.6 9.3 %fusion.15 = f32[1024,2048]{1,0:T(8,128)} fusion(bf16[1024,1024]{1,0:T(8,128)(2,1)S(1)} %copy-done.86, bf16[2048,3072]{1,0:T(8,128)(2,1)} %all-gather.6.cloned.1.call-done), kind=kOutput, calls=%fused_computation.29 | convolution fusion | flops 4294967296 | bytes 14680064 | tf_op jit(solution)/shard_map/dot_general | solution.py:398
  304.9 13.3 %fusion.7 = f32[1024,2048]{1,0:T(8,128)} fusion(bf16[1024,2048]{1,0:T(8,128)(2,1)S(1)} %copy-done.82, bf16[2048,3072]{1,0:T(8,128)(2,1)} %all-gather.6.cloned.1.call-done), kind=kOutput, calls=%fused_computation.13 | convolution fusion | flops 8589934592 | bytes 20971520 | tf_op jit(solution)/shard_map/dot_general | solution.py:398
  318.2 10.1 %fusion.13.grad_ref = f32[1024,1024]{1,0:T(8,128)} fusion(bf16[1024,2048]{1,0:T(8,128)(2,1)} %constant_dynamic-update-slice_fusion.8, bf16[2048,3072]{1,0:T(8,128)(2,1)} %all-gather.8.cloned.1.call-done), kind=kOutput, calls=%fused_computation.27 | convolution fusion | flops 4294967296 | bytes 12582912 | tf_op jit(solution)/shard_map/dot_general | solution.py:394
  328.3 11.2 %fusion.5.pair_ref = f32[1024,2048]{1,0:T(8,128)} fusion(bf16[1024,2048]{1,0:T(8,128)(2,1)S(1)} %copy-done.15, bf16[2048,3072]{1,0:T(8,128)(2,1)S(1)} %copy-done.78), kind=kOutput, calls=%fused_computation.11 | convolution fusion | flops 8589934592 | bytes 20971520 | tf_op jit(solution)/shard_map/dot_general | solution.py:394
  339.5 8.2 %activation_both.3 = (bf16[1024,1024]{1,0:T(8,128)(2,1)}, bf16[1024,2048]{1,0:T(8,128)(2,1)}) custom-call(f32[1024,2048]{1,0:T(8,128)} %fusion.5.pair_ref, f32[1024,1024]{1,0:T(8,128)} %fusion.13.grad_ref), custom_call_target="tpu_custom_call" | custom-call | flops 41943040 | bytes 18874368 | tf_op jit(solution)/shard_map/activation_both/pallas_call | solution.py:209
  347.6 14.5 %fusion.3 = f32[1024,2048]{1,0:T(8,128)} fusion(bf16[1024,2048]{1,0:T(8,128)(2,1)} %get-tuple-element.58, bf16[2048,3072]{1,0:T(8,128)(2,1)} %all-gather.8.cloned.1.call-done), kind=kOutput, calls=%fused_computation.9 | convolution fusion | flops 8589934592 | bytes 20971520 | tf_op jit(solution)/shard_map/dot_general | solution.py:398
  362.1 7.2 add_convert_fusion.2
  372.5 11.9 %collective-permute-done.21 = bf16[128,2048]{1,0:T(8,128)(2,1)S(1)} collective-permute-done((bf16[128,2048]{1,0:T(8,128)(2,1)S(1)}, bf16[128,2048]{1,0:T(8,128)(2,1)S(1)}, u32[]{:S(2)}, u32[]{:S(2)}) %collective-permute-start.21) | collective-permute-done | bytes 524320 | tf_op jit(solution)/shard_map/ppermute | solution.py:315
  386.6 8.2 %collective-permute-done.20 = bf16[128,2048]{1,0:T(8,128)(2,1)S(1)} collective-permute-done((bf16[128,2048]{1,0:T(8,128)(2,1)S(1)}, bf16[128,2048]{1,0:T(8,128)(2,1)S(1)}, u32[]{:S(2)}, u32[]{:S(2)}) %collective-permute-start.20) | collective-permute-done | bytes 524320 | tf_op jit(solution)/shard_map/ppermute | solution.py:315
  394.8 4.6 collective-permute-done.22
  403.3 4.8 collective-permute-done.23
  415.4 9.1 %fusion.11 = f32[1024,2048]{1,0:T(8,128)} fusion(bf16[1024,1024]{1,0:T(8,128)(2,1)S(1)} %copy-done.83, bf16[2048,3072]{1,0:T(8,128)(2,1)} %all-gather.8.cloned.1.call-done), kind=kOutput, calls=%fused_computation.25 | convolution fusion | flops 4294967296 | bytes 14680064 | tf_op jit(solution)/shard_map/dot_general | solution.py:398
  424.5 9.2 %add_convert_fusion.1 = bf16[1024,2048]{1,0:T(8,128)(2,1)} fusion(f32[1024,2048]{1,0:T(8,128)} %fusion.15, f32[1024,2048]{1,0:T(8,128)} %fusion.11), kind=kLoop, calls=%fused_computation.6 | loop fusion | flops 4194304 | bytes 20971520 | tf_op jit(solution)/shard_map/convert_element_type | solution.py:411
  439.0 8.1 %collective-permute-done.28 = bf16[128,2048]{1,0:T(8,128)(2,1)S(1)} collective-permute-done((bf16[128,2048]{1,0:T(8,128)(2,1)S(1)}, bf16[128,2048]{1,0:T(8,128)(2,1)S(1)}, u32[]{:S(2)}, u32[]{:S(2)}) %collective-permute-start.28) | collective-permute-done | bytes 524320 | tf_op jit(solution)/shard_map/ppermute | solution.py:287
  450.1 5.0 fusion.76.out_ref
  455.1 22.6 %attend_back.1 = bf16[768,1024]{1,0:T(8,128)(2,1)} custom-call(bf16[768,1024]{1,0:T(8,128)(2,1)} %get-tuple-element.52.rot_ref, bf16[512,1024]{1,0:T(8,128)(2,1)} %get-tuple-element.35.att_ref, bf16[512,1024]{1,0:T(8,128)(2,1)} %fusion.76.out_ref, f32[8,1024]{1,0:T(8,128)} %get-tuple-element.54.log_ref, f32[32,1024]{1,0:T(8,128)} %get-tuple-element.189.cos_ref, ...), custom_call_target="tpu_custom_call" | custom-call | flops 21474836480 | bytes 6291456 | tf_op jit(solution)/shard_map/attend_back/pallas_call | solution.py:255
  477.8 8.0 %convolution_convert_fusion.1 = bf16[1024,2048]{1,0:T(8,128)(2,1)} fusion(bf16[768,1024]{1,0:T(8,128)(2,1)} %attend_back.1, bf16[2048,1408]{1,0:T(8,128)(2,1)} %all-gather.4.cloned.1.call-done), kind=kOutput, calls=%fused_computation.22 | convolution fusion | flops 3223322624 | bytes 8912896 | tf_op jit(solution)/shard_map/dot_general | solution.py:398
  498.7 8.0 %convolution_convert_fusion.2 = bf16[1024,2048]{1,0:T(8,128)(2,1)S(1)} fusion(bf16[1024,2048]{1,0:T(8,128)(2,1)} %get-tuple-element.58, bf16[1024,256]{1,0:T(8,128)(2,1)} %get-tuple-element.200, bf16[1024,256]{1,0:T(8,128)(2,1)} %get-tuple-element.199, bf16[1024,256]{1,0:T(8,128)(2,1)} %get-tuple-element.198, bf16[1024,256]{1,0:T(8,128)(2,1)} %get-tuple-element.197), kind=kOutput, calls=%fused_computation.23 | convolution fusion | flops 4305453056 | bytes 10485760 | tf_op jit(solution)/shard_map/dot_general | solution.py:398
  509.9 7.1 collective-permute-done.50
  519.5 5.3 add_convert_fusion
  533.1 12.6 %collective-permute-done.37 = bf16[128,2048]{1,0:T(8,128)(2,1)S(1)} collective-permute-done((bf16[128,2048]{1,0:T(8,128)(2,1)S(1)}, bf16[128,2048]{1,0:T(8,128)(2,1)S(1)}, u32[]{:S(2)}, u32[]{:S(2)}) %collective-permute-start.37) | collective-permute-done | bytes 524320 | tf_op jit(solution)/shard_map/ppermute | solution.py:315
  551.4 5.5 collective-permute-done.36
  556.9 5.8 collective-permute-done.38
  568.7 5.1 collective-permute-done.39
  574.0 5.3 collective-permute-done.41
  581.4 8.5 %collective-permute-done.30 = bf16[128,2048]{1,0:T(8,128)(2,1)S(1)} collective-permute-done((bf16[128,2048]{1,0:T(8,128)(2,1)S(1)}, bf16[128,2048]{1,0:T(8,128)(2,1)S(1)}, u32[]{:S(2)}, u32[]{:S(2)}) %collective-permute-start.30) | collective-permute-done | bytes 524320 | tf_op jit(solution)/shard_map/ppermute | solution.py:315
  589.9 15.2 %collective-permute-done.32 = bf16[128,2048]{1,0:T(8,128)(2,1)S(1)} collective-permute-done((bf16[128,2048]{1,0:T(8,128)(2,1)S(1)}, bf16[128,2048]{1,0:T(8,128)(2,1)S(1)}, u32[]{:S(2)}, u32[]{:S(2)}) %collective-permute-start.32) | collective-permute-done | bytes 524320 | tf_op jit(solution)/shard_map/ppermute | solution.py:315
  612.0 5.2 collective-permute-done.35
  628.0 32.1 %reduce-scatter.6.cloned.1.call-done = bf16[256,3072]{1,0:T(8,128)(2,1)} async-done(((bf16[1024,3072]{1,0:T(8,128)(2,1)}), bf16[256,3072]{1,0:T(8,128)(2,1)}) %reduce-scatter.6.cloned.1.call-update) | async-done | bytes 1572880 | tf_op jit(solution)/shard_map/reduce_scatter | solution.py:374
  663.7 109.9 %reduce-scatter.8.cloned.1.call-done = bf16[256,3072]{1,0:T(8,128)(2,1)} async-done(((bf16[1024,3072]{1,0:T(8,128)(2,1)}), bf16[256,3072]{1,0:T(8,128)(2,1)}) %reduce-scatter.8.cloned.1.call-update) | async-done | bytes 1572880 | tf_op jit(solution)/shard_map/reduce_scatter | solution.py:374
  (391 shorter events, 204.2 us)
Async XLA Ops:
  7.2 69.6 %all-gather.4.cloned.1.call-start = ((), (), s32[]{:S(2)}) async-start(), calls=%async_computation.3 | async-start | bytes 6488064 | tf_op jit(solution)/shard_map/all_gather | solution.py:437
  13.6 222.5 %all-gather.6.cloned.1.call-start = ((), (), s32[]{:S(2)}) async-start(), calls=%async_computation.4 | async-start | bytes 14155776 | tf_op jit(solution)/shard_map/all_gather | solution.py:450
  18.4 299.8 %all-gather.8.cloned.1.call-start = ((), (), s32[]{:S(2)}) async-start(), calls=%async_computation.5 | async-start | bytes 14155776 | tf_op jit(solution)/shard_map/all_gather | solution.py:450
  18.5 26.2 %collective-permute-start = (bf16[256,2048]{1,0:T(8,128)(2,1)S(1)}, bf16[256,2048]{1,0:T(8,128)(2,1)S(1)}, u32[]{:S(2)}, u32[]{:S(2)}) collective-permute-start(bf16[256,2048]{1,0:T(8,128)(2,1)S(1)} %copy-done.4), channel_id=1, source_target_pairs={{0,1},{1,0},{2,3},{3,2},{4,5},{5,4},{6,7},{7,6},{8,9},{9,8},{10,11... | collective-permute-start | bytes 3145736 | tf_op jit(solution)/shard_map/ppermute | solution.py:285
  21.5 28.0 %collective-permute-start.1 = (bf16[256,2048]{1,0:T(8,128)(2,1)S(1)}, bf16[256,2048]{1,0:T(8,128)(2,1)S(1)}, u32[]{:S(2)}, u32[]{:S(2)}) collective-permute-start(bf16[256,2048]{1,0:T(8,128)(2,1)S(1)} %copy-done.4), channel_id=1, source_target_pairs={{0,2},{1,3},{2,0},{3,1},{4,6},{5,7},{6,4},{7,5},{8,10},{9,11},{10,... | collective-permute-start | bytes 3145736 | tf_op jit(solution)/shard_map/ppermute | solution.py:286
  25.8 598.3 %reduce-scatter.4.cloned.1.call-start = ((), (), s32[]{:S(2)}) async-start(), calls=%async_computation.6 | async-start | bytes 3276800 | tf_op jit(solution)/shard_map/reduce_scatter | solution.py:374
  45.5 13.5 %collective-permute-start.2 = (bf16[128,2048]{1,0:T(8,128)(2,1)}, bf16[128,2048]{1,0:T(8,128)(2,1)}, u32[]{:S(2)}, u32[]{:S(2)}) collective-permute-start(bf16[128,2048]{1,0:T(8,128)(2,1)} %slice.137), channel_id=1, source_target_pairs={{0,2},{1,3},{2,0},{3,1},{4,6},{5,7},{6,4},{7,5},{8,10},{9,11},{10,... | collective-permute-start | bytes 1572872 | tf_op jit(solution)/shard_map/ppermute | solution.py:287
  49.6 12.7 %collective-permute-start.3 = (bf16[128,2048]{1,0:T(8,128)(2,1)S(1)}, bf16[128,2048]{1,0:T(8,128)(2,1)S(1)}, u32[]{:S(2)}, u32[]{:S(2)}) collective-permute-start(bf16[128,2048]{1,0:T(8,128)(2,1)S(1)} %slice.138), channel_id=1, source_target_pairs={{0,1},{1,0},{2,3},{3,2},{4,5},{5,4},{6,7},{7,6},{8,9},{9,8},{10,11... | collective-permute-start | bytes 1572872 | tf_op jit(solution)/shard_map/ppermute | solution.py:288
  119.1 14.8 %collective-permute-start.5 = (bf16[128,2048]{1,0:T(8,128)(2,1)S(1)}, bf16[128,2048]{1,0:T(8,128)(2,1)S(1)}, u32[]{:S(2)}, u32[]{:S(2)}) collective-permute-start(bf16[128,2048]{1,0:T(8,128)(2,1)S(1)} %get-tuple-element.174), channel_id=1, source_target_pairs={{0,1},{1,0},{2,3},{3,2},{4,5},{5,4},{6,7},{7,6},{8,9},{9,8},{10,11... | collective-permute-start | bytes 1572872 | tf_op jit(solution)/shard_map/ppermute | solution.py:315
  120.9 23.6 %collective-permute-start.4 = (bf16[128,2048]{1,0:T(8,128)(2,1)}, bf16[128,2048]{1,0:T(8,128)(2,1)S(1)}, u32[]{:S(2)}, u32[]{:S(2)}) collective-permute-start(bf16[128,2048]{1,0:T(8,128)(2,1)} %get-tuple-element.171), channel_id=1, source_target_pairs={{0,1},{1,0},{2,3},{3,2},{4,5},{5,4},{6,7},{7,6},{8,9},{9,8},{10,11... | collective-permute-start | bytes 1572872 | tf_op jit(solution)/shard_map/ppermute | solution.py:315
  121.2 23.4 %collective-permute-start.8 = (bf16[128,2048]{1,0:T(8,128)(2,1)}, bf16[128,2048]{1,0:T(8,128)(2,1)S(1)}, u32[]{:S(2)}, u32[]{:S(2)}) collective-permute-start(bf16[128,2048]{1,0:T(8,128)(2,1)} %get-tuple-element.172), channel_id=1, source_target_pairs={{0,2},{1,3},{2,0},{3,1},{4,6},{5,7},{6,4},{7,5},{8,10},{9,11},{10,... | collective-permute-start | bytes 1572872 | tf_op jit(solution)/shard_map/ppermute | solution.py:315
  134.9 15.1 %collective-permute-start.6 = (bf16[128,2048]{1,0:T(8,128)(2,1)}, bf16[128,2048]{1,0:T(8,128)(2,1)}, u32[]{:S(2)}, u32[]{:S(2)}) collective-permute-start(bf16[128,2048]{1,0:T(8,128)(2,1)} %add_convert_fusion.15), channel_id=1, source_target_pairs={{0,2},{1,3},{2,0},{3,1},{4,6},{5,7},{6,4},{7,5},{8,10},{9,11},{10,... | collective-permute-start | bytes 1572872 | tf_op jit(solution)/shard_map/ppermute | solution.py:315
  136.8 24.5 %collective-permute-start.7 = (bf16[128,2048]{1,0:T(8,128)(2,1)}, bf16[128,2048]{1,0:T(8,128)(2,1)}, u32[]{:S(2)}, u32[]{:S(2)}) collective-permute-start(bf16[128,2048]{1,0:T(8,128)(2,1)} %get-tuple-element.173), channel_id=1, source_target_pairs={{0,2},{1,3},{2,0},{3,1},{4,6},{5,7},{6,4},{7,5},{8,10},{9,11},{10,... | collective-permute-start | bytes 1572872 | tf_op jit(solution)/shard_map/ppermute | solution.py:315
  152.9 15.1 %collective-permute-start.9 = (bf16[128,2048]{1,0:T(8,128)(2,1)}, bf16[128,2048]{1,0:T(8,128)(2,1)}, u32[]{:S(2)}, u32[]{:S(2)}) collective-permute-start(bf16[128,2048]{1,0:T(8,128)(2,1)} %get-tuple-element.170), channel_id=1, source_target_pairs={{0,1},{1,0},{2,3},{3,2},{4,5},{5,4},{6,7},{7,6},{8,9},{9,8},{10,11... | collective-permute-start | bytes 1572872 | tf_op jit(solution)/shard_map/ppermute | solution.py:315
  156.3 34.1 %collective-permute-start.14 = (bf16[256,2048]{1,0:T(8,128)(2,1)}, bf16[256,2048]{1,0:T(8,128)(2,1)S(1)}, u32[]{:S(2)}, u32[]{:S(2)}) collective-permute-start(bf16[256,2048]{1,0:T(8,128)(2,1)} %get-tuple-element.114), channel_id=1, source_target_pairs={{0,1},{1,0},{2,3},{3,2},{4,5},{5,4},{6,7},{7,6},{8,9},{9,8},{10,11... | collective-permute-start | bytes 3145736 | tf_op jit(solution)/shard_map/ppermute | solution.py:285
  156.5 36.5 %collective-permute-start.15 = (bf16[256,2048]{1,0:T(8,128)(2,1)}, bf16[256,2048]{1,0:T(8,128)(2,1)}, u32[]{:S(2)}, u32[]{:S(2)}) collective-permute-start(bf16[256,2048]{1,0:T(8,128)(2,1)} %get-tuple-element.114), channel_id=1, source_target_pairs={{0,2},{1,3},{2,0},{3,1},{4,6},{5,7},{6,4},{7,5},{8,10},{9,11},{10,... | collective-permute-start | bytes 3145736 | tf_op jit(solution)/shard_map/ppermute | solution.py:286
  173.8 43.5 %collective-permute-start.10 = (bf16[256,2048]{1,0:T(8,128)(2,1)}, bf16[256,2048]{1,0:T(8,128)(2,1)S(1)}, u32[]{:S(2)}, u32[]{:S(2)}) collective-permute-start(bf16[256,2048]{1,0:T(8,128)(2,1)} %get-tuple-element.116), channel_id=1, source_target_pairs={{0,1},{1,0},{2,3},{3,2},{4,5},{5,4},{6,7},{7,6},{8,9},{9,8},{10,11... | collective-permute-start | bytes 3145736 | tf_op jit(solution)/shard_map/ppermute | solution.py:285
  175.5 44.4 %collective-permute-start.11 = (bf16[256,2048]{1,0:T(8,128)(2,1)}, bf16[256,2048]{1,0:T(8,128)(2,1)S(1)}, u32[]{:S(2)}, u32[]{:S(2)}) collective-permute-start(bf16[256,2048]{1,0:T(8,128)(2,1)} %get-tuple-element.116), channel_id=1, source_target_pairs={{0,2},{1,3},{2,0},{3,1},{4,6},{5,7},{6,4},{7,5},{8,10},{9,11},{10,... | collective-permute-start | bytes 3145736 | tf_op jit(solution)/shard_map/ppermute | solution.py:286
  191.2 24.1 %collective-permute-start.16 = (bf16[128,2048]{1,0:T(8,128)(2,1)}, bf16[128,2048]{1,0:T(8,128)(2,1)}, u32[]{:S(2)}, u32[]{:S(2)}) collective-permute-start(bf16[128,2048]{1,0:T(8,128)(2,1)} %slice.144), channel_id=1, source_target_pairs={{0,2},{1,3},{2,0},{3,1},{4,6},{5,7},{6,4},{7,5},{8,10},{9,11},{10,... | collective-permute-start | bytes 1572872 | tf_op jit(solution)/shard_map/ppermute | solution.py:287
  194.1 25.0 %collective-permute-start.17 = (bf16[128,2048]{1,0:T(8,128)(2,1)S(1)}, bf16[128,2048]{1,0:T(8,128)(2,1)S(1)}, u32[]{:S(2)}, u32[]{:S(2)}) collective-permute-start(bf16[128,2048]{1,0:T(8,128)(2,1)S(1)} %slice.145), channel_id=1, source_target_pairs={{0,1},{1,0},{2,3},{3,2},{4,5},{5,4},{6,7},{7,6},{8,9},{9,8},{10,11... | collective-permute-start | bytes 1572872 | tf_op jit(solution)/shard_map/ppermute | solution.py:288
  217.3 11.9 %collective-permute-start.12 = (bf16[128,2048]{1,0:T(8,128)(2,1)S(1)}, bf16[128,2048]{1,0:T(8,128)(2,1)S(1)}, u32[]{:S(2)}, u32[]{:S(2)}) collective-permute-start(bf16[128,2048]{1,0:T(8,128)(2,1)S(1)} %slice.142), channel_id=1, source_target_pairs={{0,2},{1,3},{2,0},{3,1},{4,6},{5,7},{6,4},{7,5},{8,10},{9,11},{10,... | collective-permute-start | bytes 1572872 | tf_op jit(solution)/shard_map/ppermute | solution.py:287
  220.0 11.3 %collective-permute-start.13 = (bf16[128,2048]{1,0:T(8,128)(2,1)S(1)}, bf16[128,2048]{1,0:T(8,128)(2,1)S(1)}, u32[]{:S(2)}, u32[]{:S(2)}) collective-permute-start(bf16[128,2048]{1,0:T(8,128)(2,1)S(1)} %slice.143), channel_id=1, source_target_pairs={{0,1},{1,0},{2,3},{3,2},{4,5},{5,4},{6,7},{7,6},{8,9},{9,8},{10,11... | collective-permute-start | bytes 1572872 | tf_op jit(solution)/shard_map/ppermute | solution.py:288
  273.9 13.2 %collective-permute-start.18 = (bf16[1024,2048]{1,0:T(8,128)(2,1)S(1)}, bf16[1024,2048]{1,0:T(8,128)(2,1)S(1)}, u32[]{:S(2)}, u32[]{:S(2)}) collective-permute-start(bf16[1024,2048]{1,0:T(8,128)(2,1)S(1)} %convolution_convert_fusion.3), channel_id=1, source_target_pairs={{0,4},{4,0},{8,12},{12,8},{16,20},{20,16},{24,28},{28,24},{1,5},{5... | collective-permute-start | bytes 12582920 | tf_op jit(solution)/shard_map/ppermute | solution.py:366
  369.5 14.9 %collective-permute-start.21 = (bf16[128,2048]{1,0:T(8,128)(2,1)S(1)}, bf16[128,2048]{1,0:T(8,128)(2,1)S(1)}, u32[]{:S(2)}, u32[]{:S(2)}) collective-permute-start(bf16[128,2048]{1,0:T(8,128)(2,1)S(1)} %get-tuple-element.152), channel_id=1, source_target_pairs={{0,1},{1,0},{2,3},{3,2},{4,5},{5,4},{6,7},{7,6},{8,9},{9,8},{10,11... | collective-permute-start | bytes 1572872 | tf_op jit(solution)/shard_map/ppermute | solution.py:315
  371.1 23.7 %collective-permute-start.20 = (bf16[128,2048]{1,0:T(8,128)(2,1)S(1)}, bf16[128,2048]{1,0:T(8,128)(2,1)S(1)}, u32[]{:S(2)}, u32[]{:S(2)}) collective-permute-start(bf16[128,2048]{1,0:T(8,128)(2,1)S(1)} %get-tuple-element.149), channel_id=1, source_target_pairs={{0,1},{1,0},{2,3},{3,2},{4,5},{5,4},{6,7},{7,6},{8,9},{9,8},{10,11... | collective-permute-start | bytes 1572872 | tf_op jit(solution)/shard_map/ppermute | solution.py:315
  371.6 23.2 %collective-permute-start.24 = (bf16[128,2048]{1,0:T(8,128)(2,1)S(1)}, bf16[128,2048]{1,0:T(8,128)(2,1)S(1)}, u32[]{:S(2)}, u32[]{:S(2)}) collective-permute-start(bf16[128,2048]{1,0:T(8,128)(2,1)S(1)} %get-tuple-element.150), channel_id=1, source_target_pairs={{0,2},{1,3},{2,0},{3,1},{4,6},{5,7},{6,4},{7,5},{8,10},{9,11},{10,... | collective-permute-start | bytes 1572872 | tf_op jit(solution)/shard_map/ppermute | solution.py:315
  384.5 14.9 %collective-permute-start.22 = (bf16[128,2048]{1,0:T(8,128)(2,1)S(1)}, bf16[128,2048]{1,0:T(8,128)(2,1)S(1)}, u32[]{:S(2)}, u32[]{:S(2)}) collective-permute-start(bf16[128,2048]{1,0:T(8,128)(2,1)S(1)} %add_convert_fusion.13), channel_id=1, source_target_pairs={{0,2},{1,3},{2,0},{3,1},{4,6},{5,7},{6,4},{7,5},{8,10},{9,11},{10,... | collective-permute-start | bytes 1572872 | tf_op jit(solution)/shard_map/ppermute | solution.py:315
  385.5 22.6 %collective-permute-start.23 = (bf16[128,2048]{1,0:T(8,128)(2,1)S(1)}, bf16[128,2048]{1,0:T(8,128)(2,1)S(1)}, u32[]{:S(2)}, u32[]{:S(2)}) collective-permute-start(bf16[128,2048]{1,0:T(8,128)(2,1)S(1)} %get-tuple-element.151), channel_id=1, source_target_pairs={{0,2},{1,3},{2,0},{3,1},{4,6},{5,7},{6,4},{7,5},{8,10},{9,11},{10,... | collective-permute-start | bytes 1572872 | tf_op jit(solution)/shard_map/ppermute | solution.py:315
  399.9 9.2 %collective-permute-start.25 = (bf16[128,2048]{1,0:T(8,128)(2,1)S(1)}, bf16[128,2048]{1,0:T(8,128)(2,1)S(1)}, u32[]{:S(2)}, u32[]{:S(2)}) collective-permute-start(bf16[128,2048]{1,0:T(8,128)(2,1)S(1)} %get-tuple-element.148), channel_id=1, source_target_pairs={{0,1},{1,0},{2,3},{3,2},{4,5},{5,4},{6,7},{7,6},{8,9},{9,8},{10,11... | collective-permute-start | bytes 1572872 | tf_op jit(solution)/shard_map/ppermute | solution.py:315
  413.1 22.1 %collective-permute-start.26 = (bf16[256,2048]{1,0:T(8,128)(2,1)S(1)}, bf16[256,2048]{1,0:T(8,128)(2,1)S(1)}, u32[]{:S(2)}, u32[]{:S(2)}) collective-permute-start(bf16[256,2048]{1,0:T(8,128)(2,1)S(1)} %get-tuple-element.48), channel_id=1, source_target_pairs={{0,1},{1,0},{2,3},{3,2},{4,5},{5,4},{6,7},{7,6},{8,9},{9,8},{10,11... | collective-permute-start | bytes 3145736 | tf_op jit(solution)/shard_map/ppermute | solution.py:285
  414.6 24.1 %collective-permute-start.27 = (bf16[256,2048]{1,0:T(8,128)(2,1)S(1)}, bf16[256,2048]{1,0:T(8,128)(2,1)S(1)}, u32[]{:S(2)}, u32[]{:S(2)}) collective-permute-start(bf16[256,2048]{1,0:T(8,128)(2,1)S(1)} %get-tuple-element.48), channel_id=1, source_target_pairs={{0,2},{1,3},{2,0},{3,1},{4,6},{5,7},{6,4},{7,5},{8,10},{9,11},{10,... | collective-permute-start | bytes 3145736 | tf_op jit(solution)/shard_map/ppermute | solution.py:286
  435.3 11.8 %collective-permute-start.28 = (bf16[128,2048]{1,0:T(8,128)(2,1)S(1)}, bf16[128,2048]{1,0:T(8,128)(2,1)S(1)}, u32[]{:S(2)}, u32[]{:S(2)}) collective-permute-start(bf16[128,2048]{1,0:T(8,128)(2,1)S(1)} %slice.152), channel_id=1, source_target_pairs={{0,2},{1,3},{2,0},{3,1},{4,6},{5,7},{6,4},{7,5},{8,10},{9,11},{10,... | collective-permute-start | bytes 1572872 | tf_op jit(solution)/shard_map/ppermute | solution.py:287
  497.6 162.5 %reduce-scatter.6.cloned.1.call-start = ((), (), s32[]{:S(2)}) async-start(), calls=%async_computation.7 | async-start | bytes 7864320 | tf_op jit(solution)/shard_map/reduce_scatter | solution.py:374
  498.2 275.3 %reduce-scatter.8.cloned.1.call-start = ((), (), s32[]{:S(2)}) async-start(), calls=%async_computation.8 | async-start | bytes 7864320 | tf_op jit(solution)/shard_map/reduce_scatter | solution.py:374
  506.8 12.7 %collective-permute-start.49 = (bf16[1024,2048]{1,0:T(8,128)(2,1)S(1)}, bf16[1024,2048]{1,0:T(8,128)(2,1)S(1)}, u32[]{:S(2)}, u32[]{:S(2)}) collective-permute-start(bf16[1024,2048]{1,0:T(8,128)(2,1)S(1)} %convolution_convert_fusion.2), channel_id=1, source_target_pairs={{0,4},{4,0},{8,12},{12,8},{16,20},{20,16},{24,28},{28,24},{1,5},{5... | collective-permute-start | bytes 12582920 | tf_op jit(solution)/shard_map/ppermute | solution.py:366
  530.8 14.8 %collective-permute-start.37 = (bf16[128,2048]{1,0:T(8,128)(2,1)S(1)}, bf16[128,2048]{1,0:T(8,128)(2,1)S(1)}, u32[]{:S(2)}, u32[]{:S(2)}) collective-permute-start(bf16[128,2048]{1,0:T(8,128)(2,1)S(1)} %get-tuple-element.140), channel_id=1, source_target_pairs={{0,1},{1,0},{2,3},{3,2},{4,5},{5,4},{6,7},{7,6},{8,9},{9,8},{10,11... | collective-permute-start | bytes 1572872 | tf_op jit(solution)/shard_map/ppermute | solution.py:315
  530.8 26.0 %collective-permute-start.36 = (bf16[128,2048]{1,0:T(8,128)(2,1)}, bf16[128,2048]{1,0:T(8,128)(2,1)S(1)}, u32[]{:S(2)}, u32[]{:S(2)}) collective-permute-start(bf16[128,2048]{1,0:T(8,128)(2,1)} %get-tuple-element.137), channel_id=1, source_target_pairs={{0,1},{1,0},{2,3},{3,2},{4,5},{5,4},{6,7},{7,6},{8,9},{9,8},{10,11... | collective-permute-start | bytes 1572872 | tf_op jit(solution)/shard_map/ppermute | solution.py:315
  532.9 24.0 %collective-permute-start.40 = (bf16[128,2048]{1,0:T(8,128)(2,1)}, bf16[128,2048]{1,0:T(8,128)(2,1)S(1)}, u32[]{:S(2)}, u32[]{:S(2)}) collective-permute-start(bf16[128,2048]{1,0:T(8,128)(2,1)} %get-tuple-element.138), channel_id=1, source_target_pairs={{0,2},{1,3},{2,0},{3,1},{4,6},{5,7},{6,4},{7,5},{8,10},{9,11},{10,... | collective-permute-start | bytes 1572872 | tf_op jit(solution)/shard_map/ppermute | solution.py:315
  547.6 15.1 %collective-permute-start.38 = (bf16[128,2048]{1,0:T(8,128)(2,1)}, bf16[128,2048]{1,0:T(8,128)(2,1)}, u32[]{:S(2)}, u32[]{:S(2)}) collective-permute-start(bf16[128,2048]{1,0:T(8,128)(2,1)} %add_convert_fusion.9), channel_id=1, source_target_pairs={{0,2},{1,3},{2,0},{3,1},{4,6},{5,7},{6,4},{7,5},{8,10},{9,11},{10,... | collective-permute-start | bytes 1572872 | tf_op jit(solution)/shard_map/ppermute | solution.py:315
  547.8 26.0 %collective-permute-start.39 = (bf16[128,2048]{1,0:T(8,128)(2,1)}, bf16[128,2048]{1,0:T(8,128)(2,1)S(1)}, u32[]{:S(2)}, u32[]{:S(2)}) collective-permute-start(bf16[128,2048]{1,0:T(8,128)(2,1)} %get-tuple-element.139), channel_id=1, source_target_pairs={{0,2},{1,3},{2,0},{3,1},{4,6},{5,7},{6,4},{7,5},{8,10},{9,11},{10,... | collective-permute-start | bytes 1572872 | tf_op jit(solution)/shard_map/ppermute | solution.py:315
  551.3 16.8 %collective-permute-start.31 = (bf16[128,2048]{1,0:T(8,128)(2,1)S(1)}, bf16[128,2048]{1,0:T(8,128)(2,1)S(1)}, u32[]{:S(2)}, u32[]{:S(2)}) collective-permute-start(bf16[128,2048]{1,0:T(8,128)(2,1)S(1)} %get-tuple-element.146), channel_id=1, source_target_pairs={{0,1},{1,0},{2,3},{3,2},{4,5},{5,4},{6,7},{7,6},{8,9},{9,8},{10,11... | collective-permute-start | bytes 1572872 | tf_op jit(solution)/shard_map/ppermute | solution.py:315
  564.5 14.9 %collective-permute-start.41 = (bf16[128,2048]{1,0:T(8,128)(2,1)S(1)}, bf16[128,2048]{1,0:T(8,128)(2,1)S(1)}, u32[]{:S(2)}, u32[]{:S(2)}) collective-permute-start(bf16[128,2048]{1,0:T(8,128)(2,1)S(1)} %get-tuple-element.136), channel_id=1, source_target_pairs={{0,1},{1,0},{2,3},{3,2},{4,5},{5,4},{6,7},{7,6},{8,9},{9,8},{10,11... | collective-permute-start | bytes 1572872 | tf_op jit(solution)/shard_map/ppermute | solution.py:315
  564.6 25.3 %collective-permute-start.30 = (bf16[128,2048]{1,0:T(8,128)(2,1)S(1)}, bf16[128,2048]{1,0:T(8,128)(2,1)S(1)}, u32[]{:S(2)}, u32[]{:S(2)}) collective-permute-start(bf16[128,2048]{1,0:T(8,128)(2,1)S(1)} %get-tuple-element.143), channel_id=1, source_target_pairs={{0,1},{1,0},{2,3},{3,2},{4,5},{5,4},{6,7},{7,6},{8,9},{9,8},{10,11... | collective-permute-start | bytes 1572872 | tf_op jit(solution)/shard_map/ppermute | solution.py:315
  566.6 23.3 %collective-permute-start.34 = (bf16[128,2048]{1,0:T(8,128)(2,1)S(1)}, bf16[128,2048]{1,0:T(8,128)(2,1)S(1)}, u32[]{:S(2)}, u32[]{:S(2)}) collective-permute-start(bf16[128,2048]{1,0:T(8,128)(2,1)S(1)} %get-tuple-element.144), channel_id=1, source_target_pairs={{0,2},{1,3},{2,0},{3,1},{4,6},{5,7},{6,4},{7,5},{8,10},{9,11},{10,... | collective-permute-start | bytes 1572872 | tf_op jit(solution)/shard_map/ppermute | solution.py:315
  568.1 43.9 %collective-permute-start.33 = (bf16[128,2048]{1,0:T(8,128)(2,1)S(1)}, bf16[128,2048]{1,0:T(8,128)(2,1)S(1)}, u32[]{:S(2)}, u32[]{:S(2)}) collective-permute-start(bf16[128,2048]{1,0:T(8,128)(2,1)S(1)} %get-tuple-element.145), channel_id=1, source_target_pairs={{0,2},{1,3},{2,0},{3,1},{4,6},{5,7},{6,4},{7,5},{8,10},{9,11},{10,... | collective-permute-start | bytes 1572872 | tf_op jit(solution)/shard_map/ppermute | solution.py:315
  573.8 31.3 %collective-permute-start.32 = (bf16[128,2048]{1,0:T(8,128)(2,1)S(1)}, bf16[128,2048]{1,0:T(8,128)(2,1)S(1)}, u32[]{:S(2)}, u32[]{:S(2)}) collective-permute-start(bf16[128,2048]{1,0:T(8,128)(2,1)S(1)} %add_convert_fusion.11), channel_id=1, source_target_pairs={{0,2},{1,3},{2,0},{3,1},{4,6},{5,7},{6,4},{7,5},{8,10},{9,11},{10,... | collective-permute-start | bytes 1572872 | tf_op jit(solution)/shard_map/ppermute | solution.py:315
  581.3 24.8 %collective-permute-start.42 = (f32[2,2048]{1,0:T(2,128)S(1)}, f32[2,2048]{1,0:T(2,128)S(1)}, u32[]{:S(2)}, u32[]{:S(2)}) collective-permute-start(f32[2,2048]{1,0:T(2,128)S(1)} %pad_maximum_fusion.22), channel_id=1, source_target_pairs={{0,1},{1,0},{2,3},{3,2},{4,5},{5,4},{6,7},{7,6},{8,9},{9,8},{10,11... | collective-permute-start | bytes 49160 | tf_op jit(solution)/shard_map/ppermute | solution.py:388
  605.5 11.7 %collective-permute-start.35 = (bf16[128,2048]{1,0:T(8,128)(2,1)S(1)}, bf16[128,2048]{1,0:T(8,128)(2,1)S(1)}, u32[]{:S(2)}, u32[]{:S(2)}) collective-permute-start(bf16[128,2048]{1,0:T(8,128)(2,1)S(1)} %get-tuple-element.142), channel_id=1, source_target_pairs={{0,1},{1,0},{2,3},{3,2},{4,5},{5,4},{6,7},{7,6},{8,9},{9,8},{10,11... | collective-permute-start | bytes 1572872 | tf_op jit(solution)/shard_map/ppermute | solution.py:315
  (98 other events, 1255.7 us)
Sparse Core Ops, SparseCore 0:
  13.7 63.0 all-gather.3
  79.1 115.3 all-gather.5
  196.7 114.8 all-gather.7
  497.8 49.0 reduce-scatter.3
  549.0 111.0 reduce-scatter.5
  662.2 111.2 reduce-scatter.7

commit v4 on v3

--- a/solution.py
+++ b/solution.py
@@ -377,8 +377,8 @@
     return summed.astype(jnp.float32)
 
 
-def sum_everywhere(value):
-    for axis in ("tensor", "dp"):
+def sum_everywhere(value, axes):
+    for axis in axes:
         count = lax.axis_size(axis)
         if count & (count - 1):
             value = lax.psum(value, axis)
@@ -433,18 +433,26 @@
     document_segment, positions, valid_rows = layout(doc_lengths[0], total_rows)
     valid_own = lax.dynamic_slice_in_dim(valid_rows, tensor_rank * own_rows, own_rows, 0)[:, None]
     cosine, sine_part = rope_tables(positions, HEAD_SIZE)
-    gains = jnp.pad(jnp.stack([attn_gain, mlp_gain], axis=1), ((0, 0), (0, 126)))
+    gain_rows = attn_gain.shape[0]
+    gains = sum_everywhere(
+        lax.dynamic_update_slice(
+            jnp.zeros((2, inputs.shape[1]), jnp.float32),
+            jnp.stack([attn_gain, mlp_gain]).astype(jnp.float32),
+            (0, lax.axis_index("dp") * gain_rows),
+        ),
+        ("dp",),
+    )
+    gain_one, gain_two = gains[0], gains[1]
     packed = lax.all_gather(
-        row_major(jnp.concatenate([w_query, w_key, value_weight, gains, w_output.T], axis=1)),
+        row_major(jnp.concatenate([w_query, w_key, value_weight, w_output.T], axis=1)),
         "dp",
         axis=0,
         tiled=True,
     )
     full_joint = packed[:, :joint]
-    gain_one = packed[:, joint].astype(jnp.float32)
-    gain_two = packed[:, joint + 1].astype(jnp.float32)
-    full_output = packed[:, joint + gains.shape[1] :]
-    hidden_half = w_gate.shape[1] // 2
+    full_output = packed[:, joint:]
+    hidden_units = w_gate.shape[1]
+    cut = max(128, hidden_units * 5 // 8 // 128 * 128)
     down_turned = w_down.T
     halves = [
         lax.all_gather(
@@ -455,7 +463,7 @@
             axis=0,
             tiled=True,
         )
-        for part in (slice(0, hidden_half), slice(hidden_half, 2 * hidden_half))
+        for part in (slice(0, cut), slice(cut, hidden_units))
     ]
 
     grad_out = out_grad.astype(jnp.float32)
@@ -475,24 +483,24 @@
     hidden = residual + valid_own * attn_out
     scale_two, unit_two = rms_stats(hidden)
     normed_two_all = gather_rows(narrow(unit_two * gain_two), "tensor", relative=True)
-    pair_cols = 2 * hidden_half
     normed_split, cotangent_split = split_columns(normed_two_all), split_columns(grad_mlp_all)
     normed_total = mlp_total = None
     weight_grads = []
     for number, weights in enumerate(halves):
+        pair_cols = 2 * (weights.shape[1] // 3)
         pair_weights, down_weights = weights[:, :pair_cols], weights[:, pair_cols:]
         pair_pre = product(normed_two_all, pair_weights)
         grad_act = product(grad_mlp_all, down_weights)
         activation, grad_pair = activation_both(pair_pre, grad_act)
         if number == 1:
-            normed_total = narrow(normed_total + contract(grad_pair, pair_weights, 1, 1))
+            normed_total = narrow(contract(grad_pair, pair_weights, 1, 1) + normed_total.astype(jnp.float32))
             grad_pair, activation, normed_total = ordered(grad_pair, activation, normed_total)
             grad_normed_two = scatter_rows(normed_total, "tensor", relative=True)
         partial = weight_sums(((normed_split, grad_pair), (cotangent_split, activation)))
         if number == 0:
             grad_pair, activation, partial = ordered(grad_pair, activation, partial)
-            normed_total = contract(grad_pair, pair_weights, 1, 1)
-            mlp_total = contract(activation, down_weights, 1, 1)
+            normed_total = narrow(contract(grad_pair, pair_weights, 1, 1))
+            mlp_total = narrow(contract(activation, down_weights, 1, 1))
             normed_two_all, grad_mlp_all, partial, normed_total, mlp_total = ordered(
                 normed_two_all, grad_mlp_all, partial, normed_total, mlp_total
             )
@@ -502,7 +510,7 @@
     grad_attn = narrow(grad_hidden * valid_own)
     activation, grad_attn = ordered(activation, grad_attn)
     grad_attn_all = gather_rows(grad_attn, "tensor")
-    mlp_part = narrow(mlp_total + contract(activation, down_weights, 1, 1))
+    mlp_part = narrow(contract(activation, down_weights, 1, 1) + mlp_total.astype(jnp.float32))
     grad_attn_all, mlp_part = ordered(grad_attn_all, mlp_part)
     mlp_out = scatter_rows(mlp_part, "tensor", relative=True)
     output = hidden + valid_own * mlp_out
@@ -520,9 +528,6 @@
         kv_heads,
         QBLK,
     )
-    last_part = narrow(contract(joint_back, full_joint, 0, 1))
-    joint_back, last_part = ordered(joint_back, last_part)
-    grad_normed_one = scatter_rows(last_part, "tensor")
     tail = weight_sums(
         (
             (split_columns(normed_one_all), joint_back.T),
@@ -530,10 +535,11 @@
         ),
     )
     tail_grad = sum_shards(tail)
+    last_part = narrow(contract(joint_back, full_joint, 0, 1))
+    grad_normed_one = scatter_rows(last_part, "tensor")
     attn_gain_part = jnp.sum(grad_normed_one * unit_one, axis=0)
     input_grad = grad_hidden + norm_backward(grad_normed_one, unit_one, scale_one, gain_one)
-    gain_sums = sum_everywhere(jnp.stack([attn_gain_part, mlp_gain_part]))
-    gain_rows = attn_gain.shape[0]
+    gain_sums = sum_everywhere(jnp.stack([attn_gain_part, mlp_gain_part]), ("tensor", "dp"))
     gain_own = lax.dynamic_slice_in_dim(gain_sums, lax.axis_index("dp") * gain_rows, gain_rows, 1)
     return (
         output,
@@ -544,9 +550,14 @@
         tail_grad[:, query_cols + key_cols : joint],
         tail_grad[:, joint:].T,
         gain_own[1],
-        jnp.concatenate([half[:, :hidden_half] for half in weight_grads], axis=1),
-        jnp.concatenate([half[:, hidden_half:pair_cols] for half in weight_grads], axis=1),
-        jnp.concatenate([half[:, pair_cols:].T for half in weight_grads], axis=0),
+        jnp.concatenate([part[:, : part.shape[1] // 3] for part in weight_grads], axis=1),
+        jnp.concatenate(
+            [part[:, part.shape[1] // 3 : 2 * (part.shape[1] // 3)] for part in weight_grads],
+            axis=1,
+        ),
+        jnp.concatenate(
+            [part[:, 2 * (part.shape[1] // 3) :].T for part in weight_grads], axis=0
+        ),
     )
 
 

time: 799 us -> 791 us (0.990)
  starting transfers between devices: 47.6 us -> 60.4 us
  other arithmetic: 72.1 us -> 62.1 us
  local copies, waits for them, and re-layouts: 56.3 us -> 46.9 us
    ppermute x4, waiting for transfers between devices: 37.3 us -> 18.2 us  [gather_rows(): far_top = lax.ppermute(from_x[:half], axis, shift_pairs(count, 2))]
    ppermute x4, waiting for transfers between devices: 4.3 us -> 16.7 us  [gather_rows(): far_low = lax.ppermute(from_y[half:], axis, shift_pairs(count, 1))]
    ppermute x4, waiting for transfers between devices: 30 us -> 39.7 us  [gather_rows(): from_x = lax.ppermute(block, axis, shift_pairs(count, 1))]
    unnamed x192 -> x176, local copies, waits for them, and re-layouts: 22.1 us -> 18.6 us
  transfers between devices with their start and end apart: 57 -> 60, of which waited for: 39 -> 42; matrix products, arithmetic and copies ran while one was open for 24% -> 25% of each run, Pallas kernels for 4% -> 4%
where the time goes in v4:
time: 791 us; the launch traced here: 784 us
  waiting for transfers between devices  379 us (48%)
  matrix products  156 us (20%)
  Pallas kernels  63.8 us (8%)
  other arithmetic  62.1 us (8%)
  starting transfers between devices  60.4 us (8%)
  local copies, waits for them, and re-layouts  46.9 us (6%)
  between operations  16.2 us (2%)
    reduce_scatter x3, waiting for transfers between devices, sum_shards(): lax.psum_scatter(partial, 'dp', scatter_dimension=0, tiled=True, axis_ind...  146 us
    ppermute x24, waiting for transfers between devices, send(): return lax.ppermute(piece, axis, shift_pairs(count, mask))  121 us
    dot_general x20, matrix products, contract(): lax.dot_general(left, right, (((left_axis,), (right_axis,)), ((), ())), p...  111 us
    dot_general x4, matrix products, product(): return jnp.dot(left, right, preferred_element_type=jnp.float32)  44.8 us
    ppermute x4, waiting for transfers between devices, gather_rows(): from_x = lax.ppermute(block, axis, shift_pairs(count, 1))  39.7 us
    ppermute x24, starting transfers between devices, send(): return lax.ppermute(piece, axis, shift_pairs(count, mask))  26.7 us
    pallas_call x1, Pallas kernels, attend(): pl.pallas_call(functools.partial(attend_kernel, heads, kv_heads, block),...  25.6 us
    pallas_call x1, Pallas kernels, attend_back(): pl.pallas_call(functools.partial(attend_back_kernel, heads, kv_heads, blo...  22.5 us
  transfers between devices with their start and end apart: 60, of which 42 were waited for; matrix products, arithmetic and copies ran while one was open for 25% of the time, Pallas kernels for 4%

profile of v4, /device:TPU:0, one launch (start us, length us, event | category | flops | bytes accessed | tf_op | source)
XLA Modules:
  0.0 783.5 jit_solution(10515525057765405260)
XLA Ops:
  32.3 7.4 collective-permute-done
  47.7 5.4 collective-permute-done.2
  59.4 5.2 fusion.6
  64.6 5.3 all-gather.4.cloned.1.call-done
  69.9 8.2 %fusion.29.joint_ref = f32[768,1024]{1,0:T(8,128)} fusion(bf16[1024,2048]{1,0:T(8,128)(2,1)} %fusion.6, bf16[2048,1280]{1,0:T(8,128)(2,1)} %all-gather.4.cloned.1.call-done), kind=kOutput, calls=%fused_computation.44 | convolution fusion | flops 3221225472 | bytes 10485760 | tf_op jit(solution)/shard_map/dot_general | solution.py:398
  78.1 25.6 %attend.1 = (bf16[768,1024]{1,0:T(8,128)(2,1)}, bf16[512,1024]{1,0:T(8,128)(2,1)}, f32[8,1024]{1,0:T(8,128)}) custom-call(f32[768,1024]{1,0:T(8,128)} %fusion.29.joint_ref, f32[32,1024]{1,0:T(8,128)} %get-tuple-element.168.cos_ref, f32[32,1024]{1,0:T(8,128)} %get-tuple-element.167.sin_ref, s32[1,1024]{1,0:T(1,128)} %bitcast.59, s32[1024,1]{1,0:T(8,128)} %copy.40.seg_col_ref), custom_call_target="tpu_custom_call" | custom-call | flops 8589934592 | bytes 6291456 | tf_op jit(solution)/shard_map/attend/pallas_call | solution.py:232
  112.8 11.2 %collective-permute-done.8 = bf16[128,2048]{1,0:T(8,128)(2,1)S(1)} collective-permute-done((bf16[128,2048]{1,0:T(8,128)(2,1)S(1)}, bf16[128,2048]{1,0:T(8,128)(2,1)S(1)}, u32[]{:S(2)}, u32[]{:S(2)}) %collective-permute-start.8) | collective-permute-done | bytes 524320 | tf_op jit(solution)/shard_map/ppermute | solution.py:315
  130.0 5.2 collective-permute-done.7
  146.0 11.8 %collective-permute-done.17 = bf16[256,2048]{1,0:T(8,128)(2,1)} collective-permute-done((bf16[256,2048]{1,0:T(8,128)(2,1)}, bf16[256,2048]{1,0:T(8,128)(2,1)}, u32[]{:S(2)}, u32[]{:S(2)}) %collective-permute-start.17) | collective-permute-done | bytes 1048608 | tf_op jit(solution)/shard_map/ppermute | solution.py:285
  161.2 7.1 collective-permute-done.12
  186.9 12.9 %collective-permute-done.13 = bf16[256,2048]{1,0:T(8,128)(2,1)S(1)} collective-permute-done((bf16[256,2048]{1,0:T(8,128)(2,1)S(1)}, bf16[256,2048]{1,0:T(8,128)(2,1)S(1)}, u32[]{:S(2)}, u32[]{:S(2)}) %collective-permute-start.13) | collective-permute-done | bytes 1048608 | tf_op jit(solution)/shard_map/ppermute | solution.py:285
  201.4 8.0 %collective-permute-done.20 = bf16[128,2048]{1,0:T(8,128)(2,1)S(1)} collective-permute-done((bf16[128,2048]{1,0:T(8,128)(2,1)S(1)}, bf16[128,2048]{1,0:T(8,128)(2,1)S(1)}, u32[]{:S(2)}, u32[]{:S(2)}) %collective-permute-start.20) | collective-permute-done | bytes 524320 | tf_op jit(solution)/shard_map/ppermute | solution.py:288
  216.4 6.4 collective-permute-done.16
  227.7 12.1 %fusion.13.grad_ref = f32[1024,1280]{1,0:T(8,128)} fusion(bf16[1024,2048]{1,0:T(8,128)(2,1)} %constant_dynamic-update-slice_fusion.5, bf16[2048,3840]{1,0:T(8,128)(2,1)} %all-gather.6.cloned.1.call-done), kind=kOutput, calls=%fused_computation.23 | convolution fusion | flops 5368709120 | bytes 14680064 | tf_op jit(solution)/shard_map/dot_general | solution.py:394
  239.8 13.5 %fusion.2.pair_ref = f32[1024,2560]{1,0:T(8,128)} fusion(bf16[1024,2048]{1,0:T(8,128)(2,1)S(1)} %copy-done.12, bf16[2048,3840]{1,0:T(8,128)(2,1)S(1)} %copy-done.72), kind=kOutput, calls=%fused_computation.5 | convolution fusion | flops 10737418240 | bytes 25165824 | tf_op jit(solution)/shard_map/dot_general | solution.py:394
  253.4 9.2 %activation_both.2 = (bf16[1024,1280]{1,0:T(8,128)(2,1)}, bf16[1024,2560]{1,0:T(8,128)(2,1)}) custom-call(f32[1024,2560]{1,0:T(8,128)} %fusion.2.pair_ref, f32[1024,1280]{1,0:T(8,128)} %fusion.13.grad_ref), custom_call_target="tpu_custom_call" | custom-call | flops 52428800 | bytes 23592960 | tf_op jit(solution)/shard_map/activation_both/pallas_call | solution.py:209
  262.6 8.2 %convolution_convert_fusion = bf16[1024,2560]{1,0:T(8,128)(2,1)S(1)} fusion(bf16[1024,2560]{1,0:T(8,128)(2,1)} %get-tuple-element.37, bf16[1024,256]{1,0:T(8,128)(2,1)} %get-tuple-element.177, bf16[1024,256]{1,0:T(8,128)(2,1)} %get-tuple-element.176, bf16[1024,256]{1,0:T(8,128)(2,1)} %get-tuple-element.175, bf16[1024,256]{1,0:T(8,128)(2,1)S(1)} %get-tuple-element.174), kind=kOutput, calls=%fused_computation.14 | convolution fusion | flops 5379719168 | bytes 12582912 | tf_op jit(solution)/shard_map/dot_general | solution.py:398
  275.0 8.9 %collective-permute-done.22 = bf16[1024,1280]{1,0:T(8,128)(2,1)S(1)} collective-permute-done((bf16[1024,1280]{1,0:T(8,128)(2,1)S(1)}, bf16[1024,1280]{1,0:T(8,128)(2,1)S(1)}, u32[]{:S(2)}, u32[]{:S(2)}) %collective-permute-start.22) | collective-permute-done | bytes 2621472 | tf_op jit(solution)/shard_map/ppermute | solution.py:366
  287.8 7.6 add_convert_fusion
  295.4 6.1 pad_maximum_fusion
  301.5 10.1 %fusion.15 = bf16[1024,2048]{1,0:T(8,128)(2,1)} fusion(bf16[1024,1280]{1,0:T(8,128)(2,1)} %get-tuple-element.38, bf16[2048,3840]{1,0:T(8,128)(2,1)} %all-gather.6.cloned.1.call-done), kind=kOutput, calls=%fused_computation.25 | convolution fusion | flops 5370806272 | bytes 12058624 | tf_op jit(solution)/shard_map/dot_general | solution.py:398
  311.6 16.6 %fusion.18 = bf16[1024,2048]{1,0:T(8,128)(2,1)} fusion(bf16[1024,2560]{1,0:T(8,128)(2,1)} %get-tuple-element.37, bf16[2048,3840]{1,0:T(8,128)(2,1)} %all-gather.6.cloned.1.call-done), kind=kOutput, calls=%fused_computation.30 | convolution fusion | flops 10739515392 | bytes 19922944 | tf_op jit(solution)/shard_map/dot_general | solution.py:398
  328.2 12.1 %fusion.9.pair_ref = f32[1024,1536]{1,0:T(8,128)} fusion(bf16[1024,2048]{1,0:T(8,128)(2,1)} %copy-done.11, bf16[2048,2304]{1,0:T(8,128)(2,1)} %all-gather.8.cloned.1.call-done), kind=kOutput, calls=%fused_computation.17 | convolution fusion | flops 6442450944 | bytes 16777216 | tf_op jit(solution)/shard_map/dot_general | solution.py:394
  340.3 7.0 fusion.26.grad_ref
  347.3 6.5 activation_both.3
  353.8 10.2 %fusion.7 = f32[1024,2048]{1,0:T(8,128)S(1)} fusion(bf16[1024,1536]{1,0:T(8,128)(2,1)} %get-tuple-element.54, bf16[2048,2304]{1,0:T(8,128)(2,1)} %all-gather.8.cloned.1.call-done), kind=kOutput, calls=%fused_computation.15 | convolution fusion | flops 6442450944 | bytes 17825792 | tf_op jit(solution)/shard_map/dot_general | solution.py:398
  371.6 11.1 %collective-permute-done.24 = bf16[128,2048]{1,0:T(8,128)(2,1)S(1)} collective-permute-done((bf16[128,2048]{1,0:T(8,128)(2,1)S(1)}, bf16[128,2048]{1,0:T(8,128)(2,1)S(1)}, u32[]{:S(2)}, u32[]{:S(2)}) %collective-permute-start.24) | collective-permute-done | bytes 524320 | tf_op jit(solution)/shard_map/ppermute | solution.py:315
  385.0 8.3 %collective-permute-done.23 = bf16[128,2048]{1,0:T(8,128)(2,1)S(1)} collective-permute-done((bf16[128,2048]{1,0:T(8,128)(2,1)S(1)}, bf16[128,2048]{1,0:T(8,128)(2,1)S(1)}, u32[]{:S(2)}, u32[]{:S(2)}) %collective-permute-start.23) | collective-permute-done | bytes 524320 | tf_op jit(solution)/shard_map/ppermute | solution.py:315
  393.3 4.5 collective-permute-done.25
  402.0 4.8 collective-permute-done.26
  413.8 5.3 fusion.24
  419.1 5.8 add_convert_fusion.1
  425.0 7.6 collective-permute-done.29
  437.1 8.1 %collective-permute-done.31 = bf16[128,2048]{1,0:T(8,128)(2,1)S(1)} collective-permute-done((bf16[128,2048]{1,0:T(8,128)(2,1)S(1)}, bf16[128,2048]{1,0:T(8,128)(2,1)S(1)}, u32[]{:S(2)}, u32[]{:S(2)}) %collective-permute-start.31) | collective-permute-done | bytes 524320 | tf_op jit(solution)/shard_map/ppermute | solution.py:287
  448.1 5.2 fusion.82.out_ref
  453.3 22.5 %attend_back.1 = bf16[768,1024]{1,0:T(8,128)(2,1)} custom-call(bf16[768,1024]{1,0:T(8,128)(2,1)} %get-tuple-element.50.rot_ref, bf16[512,1024]{1,0:T(8,128)(2,1)} %get-tuple-element.33.att_ref, bf16[512,1024]{1,0:T(8,128)(2,1)} %fusion.82.out_ref, f32[8,1024]{1,0:T(8,128)} %get-tuple-element.52.log_ref, f32[32,1024]{1,0:T(8,128)} %get-tuple-element.168.cos_ref, ...), custom_call_target="tpu_custom_call" | custom-call | flops 21474836480 | bytes 6291456 | tf_op jit(solution)/shard_map/attend_back/pallas_call | solution.py:255
  490.4 6.1 convolution_convert_fusion.2
  499.2 5.4 collective-permute-done.53
  513.8 5.9 convolution_convert_fusion.3
  523.3 11.5 %collective-permute-done.40 = bf16[128,2048]{1,0:T(8,128)(2,1)S(1)} collective-permute-done((bf16[128,2048]{1,0:T(8,128)(2,1)S(1)}, bf16[128,2048]{1,0:T(8,128)(2,1)S(1)}, u32[]{:S(2)}, u32[]{:S(2)}) %collective-permute-start.40) | collective-permute-done | bytes 524320 | tf_op jit(solution)/shard_map/ppermute | solution.py:315
  537.5 8.5 %collective-permute-done.39 = bf16[128,2048]{1,0:T(8,128)(2,1)S(1)} collective-permute-done((bf16[128,2048]{1,0:T(8,128)(2,1)S(1)}, bf16[128,2048]{1,0:T(8,128)(2,1)S(1)}, u32[]{:S(2)}, u32[]{:S(2)}) %collective-permute-start.39) | collective-permute-done | bytes 524320 | tf_op jit(solution)/shard_map/ppermute | solution.py:315
  562.3 6.2 collective-permute-done.44
  569.8 9.3 %collective-permute-done.33 = bf16[128,2048]{1,0:T(8,128)(2,1)S(1)} collective-permute-done((bf16[128,2048]{1,0:T(8,128)(2,1)S(1)}, bf16[128,2048]{1,0:T(8,128)(2,1)S(1)}, u32[]{:S(2)}, u32[]{:S(2)}) %collective-permute-start.33) | collective-permute-done | bytes 524320 | tf_op jit(solution)/shard_map/ppermute | solution.py:315
  579.1 13.2 %collective-permute-done.35 = bf16[128,2048]{1,0:T(8,128)(2,1)S(1)} collective-permute-done((bf16[128,2048]{1,0:T(8,128)(2,1)S(1)}, bf16[128,2048]{1,0:T(8,128)(2,1)S(1)}, u32[]{:S(2)}, u32[]{:S(2)}) %collective-permute-start.35) | collective-permute-done | bytes 524320 | tf_op jit(solution)/shard_map/ppermute | solution.py:315
  599.1 5.4 collective-permute-done.38
  607.8 5.4 collective-permute-done.49
  617.7 9.8 %reduce-scatter.8.cloned.1.call-done = bf16[256,2304]{1,0:T(8,128)(2,1)} async-done(((bf16[1024,2304]{1,0:T(8,128)(2,1)}), bf16[256,2304]{1,0:T(8,128)(2,1)}) %reduce-scatter.8.cloned.1.call-update) | async-done | bytes 1179664 | tf_op jit(solution)/shard_map/reduce_scatter | solution.py:374
  630.1 136.3 %reduce-scatter.6.cloned.1.call-done = bf16[256,3840]{1,0:T(8,128)(2,1)} async-done(((bf16[1024,3840]{1,0:T(8,128)(2,1)}), bf16[256,3840]{1,0:T(8,128)(2,1)}) %reduce-scatter.6.cloned.1.call-update) | async-done | bytes 1966096 | tf_op jit(solution)/shard_map/reduce_scatter | solution.py:374
  (393 shorter events, 213.3 us)
Async XLA Ops:
  7.2 62.7 %all-gather.4.cloned.1.call-start = ((), (), s32[]{:S(2)}) async-start(), calls=%async_computation.3 | async-start | bytes 5898240 | tf_op jit(solution)/shard_map/all_gather | solution.py:446
  10.4 217.3 %all-gather.6.cloned.1.call-start = ((), (), s32[]{:S(2)}) async-start(), calls=%async_computation.4 | async-start | bytes 17694720 | tf_op jit(solution)/shard_map/all_gather | solution.py:458
  13.5 314.7 %all-gather.8.cloned.1.call-start = ((), (), s32[]{:S(2)}) async-start(), calls=%async_computation.5 | async-start | bytes 10616832 | tf_op jit(solution)/shard_map/all_gather | solution.py:458
  13.5 26.2 %collective-permute-start = (bf16[256,2048]{1,0:T(8,128)(2,1)S(1)}, bf16[256,2048]{1,0:T(8,128)(2,1)S(1)}, u32[]{:S(2)}, u32[]{:S(2)}) collective-permute-start(bf16[256,2048]{1,0:T(8,128)(2,1)S(1)} %copy-done.2), channel_id=1, source_target_pairs={{0,1},{1,0},{2,3},{3,2},{4,5},{5,4},{6,7},{7,6},{8,9},{9,8},{10,11... | collective-permute-start | bytes 3145736 | tf_op jit(solution)/shard_map/ppermute | solution.py:285
  16.6 25.1 %collective-permute-start.1 = (bf16[256,2048]{1,0:T(8,128)(2,1)S(1)}, bf16[256,2048]{1,0:T(8,128)(2,1)}, u32[]{:S(2)}, u32[]{:S(2)}) collective-permute-start(bf16[256,2048]{1,0:T(8,128)(2,1)S(1)} %copy-done.2), channel_id=1, source_target_pairs={{0,2},{1,3},{2,0},{3,1},{4,6},{5,7},{6,4},{7,5},{8,10},{9,11},{10,... | collective-permute-start | bytes 3145736 | tf_op jit(solution)/shard_map/ppermute | solution.py:286
  39.8 13.3 %collective-permute-start.2 = (bf16[128,2048]{1,0:T(8,128)(2,1)S(1)}, bf16[128,2048]{1,0:T(8,128)(2,1)S(1)}, u32[]{:S(2)}, u32[]{:S(2)}) collective-permute-start(bf16[128,2048]{1,0:T(8,128)(2,1)S(1)} %slice.137), channel_id=1, source_target_pairs={{0,2},{1,3},{2,0},{3,1},{4,6},{5,7},{6,4},{7,5},{8,10},{9,11},{10,... | collective-permute-start | bytes 1572872 | tf_op jit(solution)/shard_map/ppermute | solution.py:287
  42.8 12.7 %collective-permute-start.3 = (bf16[128,2048]{1,0:T(8,128)(2,1)S(1)}, bf16[128,2048]{1,0:T(8,128)(2,1)S(1)}, u32[]{:S(2)}, u32[]{:S(2)}) collective-permute-start(bf16[128,2048]{1,0:T(8,128)(2,1)S(1)} %slice.138), channel_id=1, source_target_pairs={{0,1},{1,0},{2,3},{3,2},{4,5},{5,4},{6,7},{7,6},{8,9},{9,8},{10,11... | collective-permute-start | bytes 1572872 | tf_op jit(solution)/shard_map/ppermute | solution.py:288
  109.2 14.8 %collective-permute-start.8 = (bf16[128,2048]{1,0:T(8,128)(2,1)S(1)}, bf16[128,2048]{1,0:T(8,128)(2,1)S(1)}, u32[]{:S(2)}, u32[]{:S(2)}) collective-permute-start(bf16[128,2048]{1,0:T(8,128)(2,1)S(1)} %get-tuple-element.157), channel_id=1, source_target_pairs={{0,1},{1,0},{2,3},{3,2},{4,5},{5,4},{6,7},{7,6},{8,9},{9,8},{10,11... | collective-permute-start | bytes 1572872 | tf_op jit(solution)/shard_map/ppermute | solution.py:315
  110.8 19.3 %collective-permute-start.11 = (bf16[128,2048]{1,0:T(8,128)(2,1)}, bf16[128,2048]{1,0:T(8,128)(2,1)S(1)}, u32[]{:S(2)}, u32[]{:S(2)}) collective-permute-start(bf16[128,2048]{1,0:T(8,128)(2,1)} %get-tuple-element.155), channel_id=1, source_target_pairs={{0,2},{1,3},{2,0},{3,1},{4,6},{5,7},{6,4},{7,5},{8,10},{9,11},{10,... | collective-permute-start | bytes 1572872 | tf_op jit(solution)/shard_map/ppermute | solution.py:315
  112.3 22.9 %collective-permute-start.7 = (bf16[128,2048]{1,0:T(8,128)(2,1)}, bf16[128,2048]{1,0:T(8,128)(2,1)S(1)}, u32[]{:S(2)}, u32[]{:S(2)}) collective-permute-start(bf16[128,2048]{1,0:T(8,128)(2,1)} %get-tuple-element.154), channel_id=1, source_target_pairs={{0,1},{1,0},{2,3},{3,2},{4,5},{5,4},{6,7},{7,6},{8,9},{9,8},{10,11... | collective-permute-start | bytes 1572872 | tf_op jit(solution)/shard_map/ppermute | solution.py:315
  124.9 15.1 %collective-permute-start.9 = (bf16[128,2048]{1,0:T(8,128)(2,1)}, bf16[128,2048]{1,0:T(8,128)(2,1)}, u32[]{:S(2)}, u32[]{:S(2)}) collective-permute-start(bf16[128,2048]{1,0:T(8,128)(2,1)} %add_convert_fusion.15), channel_id=1, source_target_pairs={{0,2},{1,3},{2,0},{3,1},{4,6},{5,7},{6,4},{7,5},{8,10},{9,11},{10,... | collective-permute-start | bytes 1572872 | tf_op jit(solution)/shard_map/ppermute | solution.py:315
  128.0 29.8 %collective-permute-start.17 = (bf16[256,2048]{1,0:T(8,128)(2,1)}, bf16[256,2048]{1,0:T(8,128)(2,1)}, u32[]{:S(2)}, u32[]{:S(2)}) collective-permute-start(bf16[256,2048]{1,0:T(8,128)(2,1)} %get-tuple-element.97), channel_id=1, source_target_pairs={{0,1},{1,0},{2,3},{3,2},{4,5},{5,4},{6,7},{7,6},{8,9},{9,8},{10,11... | collective-permute-start | bytes 3145736 | tf_op jit(solution)/shard_map/ppermute | solution.py:285
  129.5 31.7 %collective-permute-start.10 = (bf16[128,2048]{1,0:T(8,128)(2,1)}, bf16[128,2048]{1,0:T(8,128)(2,1)}, u32[]{:S(2)}, u32[]{:S(2)}) collective-permute-start(bf16[128,2048]{1,0:T(8,128)(2,1)} %get-tuple-element.156), channel_id=1, source_target_pairs={{0,2},{1,3},{2,0},{3,1},{4,6},{5,7},{6,4},{7,5},{8,10},{9,11},{10,... | collective-permute-start | bytes 1572872 | tf_op jit(solution)/shard_map/ppermute | solution.py:315
  143.0 25.3 %collective-permute-start.12 = (bf16[128,2048]{1,0:T(8,128)(2,1)}, bf16[128,2048]{1,0:T(8,128)(2,1)}, u32[]{:S(2)}, u32[]{:S(2)}) collective-permute-start(bf16[128,2048]{1,0:T(8,128)(2,1)} %get-tuple-element.153), channel_id=1, source_target_pairs={{0,1},{1,0},{2,3},{3,2},{4,5},{5,4},{6,7},{7,6},{8,9},{9,8},{10,11... | collective-permute-start | bytes 1572872 | tf_op jit(solution)/shard_map/ppermute | solution.py:315
  144.5 33.5 %collective-permute-start.18 = (bf16[256,2048]{1,0:T(8,128)(2,1)}, bf16[256,2048]{1,0:T(8,128)(2,1)}, u32[]{:S(2)}, u32[]{:S(2)}) collective-permute-start(bf16[256,2048]{1,0:T(8,128)(2,1)} %get-tuple-element.97), channel_id=1, source_target_pairs={{0,2},{1,3},{2,0},{3,1},{4,6},{5,7},{6,4},{7,5},{8,10},{9,11},{10,... | collective-permute-start | bytes 3145736 | tf_op jit(solution)/shard_map/ppermute | solution.py:286
  159.7 25.3 %collective-permute-start.19 = (bf16[128,2048]{1,0:T(8,128)(2,1)}, bf16[128,2048]{1,0:T(8,128)(2,1)}, u32[]{:S(2)}, u32[]{:S(2)}) collective-permute-start(bf16[128,2048]{1,0:T(8,128)(2,1)} %slice.144), channel_id=1, source_target_pairs={{0,2},{1,3},{2,0},{3,1},{4,6},{5,7},{6,4},{7,5},{8,10},{9,11},{10,... | collective-permute-start | bytes 1572872 | tf_op jit(solution)/shard_map/ppermute | solution.py:287
  173.7 26.0 %collective-permute-start.13 = (bf16[256,2048]{1,0:T(8,128)(2,1)S(1)}, bf16[256,2048]{1,0:T(8,128)(2,1)S(1)}, u32[]{:S(2)}, u32[]{:S(2)}) collective-permute-start(bf16[256,2048]{1,0:T(8,128)(2,1)S(1)} %get-tuple-element.99), channel_id=1, source_target_pairs={{0,1},{1,0},{2,3},{3,2},{4,5},{5,4},{6,7},{7,6},{8,9},{9,8},{10,11... | collective-permute-start | bytes 3145736 | tf_op jit(solution)/shard_map/ppermute | solution.py:285
  175.2 35.0 %collective-permute-start.14 = (bf16[256,2048]{1,0:T(8,128)(2,1)S(1)}, bf16[256,2048]{1,0:T(8,128)(2,1)S(1)}, u32[]{:S(2)}, u32[]{:S(2)}) collective-permute-start(bf16[256,2048]{1,0:T(8,128)(2,1)S(1)} %get-tuple-element.99), channel_id=1, source_target_pairs={{0,2},{1,3},{2,0},{3,1},{4,6},{5,7},{6,4},{7,5},{8,10},{9,11},{10,... | collective-permute-start | bytes 3145736 | tf_op jit(solution)/shard_map/ppermute | solution.py:286
  177.9 435.9 %reduce-scatter.4.cloned.1.call-start = ((), (), s32[]{:S(2)}) async-start(), calls=%async_computation.6 | async-start | bytes 3276800 | tf_op jit(solution)/shard_map/reduce_scatter | solution.py:374
  179.0 30.4 %collective-permute-start.20 = (bf16[128,2048]{1,0:T(8,128)(2,1)S(1)}, bf16[128,2048]{1,0:T(8,128)(2,1)S(1)}, u32[]{:S(2)}, u32[]{:S(2)}) collective-permute-start(bf16[128,2048]{1,0:T(8,128)(2,1)S(1)} %slice.145), channel_id=1, source_target_pairs={{0,1},{1,0},{2,3},{3,2},{4,5},{5,4},{6,7},{7,6},{8,9},{9,8},{10,11... | collective-permute-start | bytes 1572872 | tf_op jit(solution)/shard_map/ppermute | solution.py:288
  199.8 16.5 %collective-permute-start.15 = (bf16[128,2048]{1,0:T(8,128)(2,1)S(1)}, bf16[128,2048]{1,0:T(8,128)(2,1)S(1)}, u32[]{:S(2)}, u32[]{:S(2)}) collective-permute-start(bf16[128,2048]{1,0:T(8,128)(2,1)S(1)} %slice.142), channel_id=1, source_target_pairs={{0,2},{1,3},{2,0},{3,1},{4,6},{5,7},{6,4},{7,5},{8,10},{9,11},{10,... | collective-permute-start | bytes 1572872 | tf_op jit(solution)/shard_map/ppermute | solution.py:287
  210.3 12.5 %collective-permute-start.16 = (bf16[128,2048]{1,0:T(8,128)(2,1)S(1)}, bf16[128,2048]{1,0:T(8,128)(2,1)S(1)}, u32[]{:S(2)}, u32[]{:S(2)}) collective-permute-start(bf16[128,2048]{1,0:T(8,128)(2,1)S(1)} %slice.143), channel_id=1, source_target_pairs={{0,1},{1,0},{2,3},{3,2},{4,5},{5,4},{6,7},{7,6},{8,9},{9,8},{10,11... | collective-permute-start | bytes 1572872 | tf_op jit(solution)/shard_map/ppermute | solution.py:288
  270.9 16.8 %collective-permute-start.21 = (bf16[1024,2560]{1,0:T(8,128)(2,1)S(1)}, bf16[1024,2560]{1,0:T(8,128)(2,1)S(1)}, u32[]{:S(2)}, u32[]{:S(2)}) collective-permute-start(bf16[1024,2560]{1,0:T(8,128)(2,1)S(1)} %convolution_convert_fusion), channel_id=1, source_target_pairs={{0,4},{4,0},{8,12},{12,8},{16,20},{20,16},{24,28},{28,24},{1,5},{5... | collective-permute-start | bytes 15728648 | tf_op jit(solution)/shard_map/ppermute | solution.py:366
  274.5 9.5 %collective-permute-start.22 = (bf16[1024,1280]{1,0:T(8,128)(2,1)S(1)}, bf16[1024,1280]{1,0:T(8,128)(2,1)S(1)}, u32[]{:S(2)}, u32[]{:S(2)}) collective-permute-start(bf16[1024,1280]{1,0:T(8,128)(2,1)S(1)} %convolution_convert_fusion.4), channel_id=1, source_target_pairs={{0,4},{4,0},{8,12},{12,8},{16,20},{20,16},{24,28},{28,24},{1,5},{5... | collective-permute-start | bytes 7864328 | tf_op jit(solution)/shard_map/ppermute | solution.py:366
  367.9 14.9 %collective-permute-start.24 = (bf16[128,2048]{1,0:T(8,128)(2,1)S(1)}, bf16[128,2048]{1,0:T(8,128)(2,1)S(1)}, u32[]{:S(2)}, u32[]{:S(2)}) collective-permute-start(bf16[128,2048]{1,0:T(8,128)(2,1)S(1)} %get-tuple-element.135), channel_id=1, source_target_pairs={{0,1},{1,0},{2,3},{3,2},{4,5},{5,4},{6,7},{7,6},{8,9},{9,8},{10,11... | collective-permute-start | bytes 1572872 | tf_op jit(solution)/shard_map/ppermute | solution.py:315
  369.6 23.7 %collective-permute-start.23 = (bf16[128,2048]{1,0:T(8,128)(2,1)S(1)}, bf16[128,2048]{1,0:T(8,128)(2,1)S(1)}, u32[]{:S(2)}, u32[]{:S(2)}) collective-permute-start(bf16[128,2048]{1,0:T(8,128)(2,1)S(1)} %get-tuple-element.132), channel_id=1, source_target_pairs={{0,1},{1,0},{2,3},{3,2},{4,5},{5,4},{6,7},{7,6},{8,9},{9,8},{10,11... | collective-permute-start | bytes 1572872 | tf_op jit(solution)/shard_map/ppermute | solution.py:315
  370.0 23.3 %collective-permute-start.27 = (bf16[128,2048]{1,0:T(8,128)(2,1)S(1)}, bf16[128,2048]{1,0:T(8,128)(2,1)S(1)}, u32[]{:S(2)}, u32[]{:S(2)}) collective-permute-start(bf16[128,2048]{1,0:T(8,128)(2,1)S(1)} %get-tuple-element.133), channel_id=1, source_target_pairs={{0,2},{1,3},{2,0},{3,1},{4,6},{5,7},{6,4},{7,5},{8,10},{9,11},{10,... | collective-permute-start | bytes 1572872 | tf_op jit(solution)/shard_map/ppermute | solution.py:315
  382.9 14.9 %collective-permute-start.25 = (bf16[128,2048]{1,0:T(8,128)(2,1)S(1)}, bf16[128,2048]{1,0:T(8,128)(2,1)S(1)}, u32[]{:S(2)}, u32[]{:S(2)}) collective-permute-start(bf16[128,2048]{1,0:T(8,128)(2,1)S(1)} %add_convert_fusion.13), channel_id=1, source_target_pairs={{0,2},{1,3},{2,0},{3,1},{4,6},{5,7},{6,4},{7,5},{8,10},{9,11},{10,... | collective-permute-start | bytes 1572872 | tf_op jit(solution)/shard_map/ppermute | solution.py:315
  384.6 22.1 %collective-permute-start.26 = (bf16[128,2048]{1,0:T(8,128)(2,1)S(1)}, bf16[128,2048]{1,0:T(8,128)(2,1)S(1)}, u32[]{:S(2)}, u32[]{:S(2)}) collective-permute-start(bf16[128,2048]{1,0:T(8,128)(2,1)S(1)} %get-tuple-element.134), channel_id=1, source_target_pairs={{0,2},{1,3},{2,0},{3,1},{4,6},{5,7},{6,4},{7,5},{8,10},{9,11},{10,... | collective-permute-start | bytes 1572872 | tf_op jit(solution)/shard_map/ppermute | solution.py:315
  410.6 22.0 %collective-permute-start.29 = (bf16[256,2048]{1,0:T(8,128)(2,1)S(1)}, bf16[256,2048]{1,0:T(8,128)(2,1)S(1)}, u32[]{:S(2)}, u32[]{:S(2)}) collective-permute-start(bf16[256,2048]{1,0:T(8,128)(2,1)S(1)} %get-tuple-element.46), channel_id=1, source_target_pairs={{0,1},{1,0},{2,3},{3,2},{4,5},{5,4},{6,7},{7,6},{8,9},{9,8},{10,11... | collective-permute-start | bytes 3145736 | tf_op jit(solution)/shard_map/ppermute | solution.py:285
  412.3 24.4 %collective-permute-start.30 = (bf16[256,2048]{1,0:T(8,128)(2,1)S(1)}, bf16[256,2048]{1,0:T(8,128)(2,1)S(1)}, u32[]{:S(2)}, u32[]{:S(2)}) collective-permute-start(bf16[256,2048]{1,0:T(8,128)(2,1)S(1)} %get-tuple-element.46), channel_id=1, source_target_pairs={{0,2},{1,3},{2,0},{3,1},{4,6},{5,7},{6,4},{7,5},{8,10},{9,11},{10,... | collective-permute-start | bytes 3145736 | tf_op jit(solution)/shard_map/ppermute | solution.py:286
  432.6 12.6 %collective-permute-start.31 = (bf16[128,2048]{1,0:T(8,128)(2,1)S(1)}, bf16[128,2048]{1,0:T(8,128)(2,1)S(1)}, u32[]{:S(2)}, u32[]{:S(2)}) collective-permute-start(bf16[128,2048]{1,0:T(8,128)(2,1)S(1)} %slice.152), channel_id=1, source_target_pairs={{0,2},{1,3},{2,0},{3,1},{4,6},{5,7},{6,4},{7,5},{8,10},{9,11},{10,... | collective-permute-start | bytes 1572872 | tf_op jit(solution)/shard_map/ppermute | solution.py:287
  490.2 137.4 %reduce-scatter.8.cloned.1.call-start = ((), (), s32[]{:S(2)}) async-start(), calls=%async_computation.8 | async-start | bytes 5898240 | tf_op jit(solution)/shard_map/reduce_scatter | solution.py:374
  496.6 9.9 %collective-permute-start.52 = (bf16[1024,1536]{1,0:T(8,128)(2,1)S(1)}, bf16[1024,1536]{1,0:T(8,128)(2,1)S(1)}, u32[]{:S(2)}, u32[]{:S(2)}) collective-permute-start(bf16[1024,1536]{1,0:T(8,128)(2,1)S(1)} %convolution_convert_fusion.2), channel_id=1, source_target_pairs={{0,4},{4,0},{8,12},{12,8},{16,20},{20,16},{24,28},{28,24},{1,5},{5... | collective-permute-start | bytes 9437192 | tf_op jit(solution)/shard_map/ppermute | solution.py:366
  513.2 253.1 %reduce-scatter.6.cloned.1.call-start = ((), (), s32[]{:S(2)}) async-start(), calls=%async_computation.7 | async-start | bytes 9830400 | tf_op jit(solution)/shard_map/reduce_scatter | solution.py:374
  519.9 14.9 %collective-permute-start.40 = (bf16[128,2048]{1,0:T(8,128)(2,1)S(1)}, bf16[128,2048]{1,0:T(8,128)(2,1)S(1)}, u32[]{:S(2)}, u32[]{:S(2)}) collective-permute-start(bf16[128,2048]{1,0:T(8,128)(2,1)S(1)} %get-tuple-element.123), channel_id=1, source_target_pairs={{0,1},{1,0},{2,3},{3,2},{4,5},{5,4},{6,7},{7,6},{8,9},{9,8},{10,11... | collective-permute-start | bytes 1572872 | tf_op jit(solution)/shard_map/ppermute | solution.py:315
  520.2 25.8 %collective-permute-start.39 = (bf16[128,2048]{1,0:T(8,128)(2,1)S(1)}, bf16[128,2048]{1,0:T(8,128)(2,1)S(1)}, u32[]{:S(2)}, u32[]{:S(2)}) collective-permute-start(bf16[128,2048]{1,0:T(8,128)(2,1)S(1)} %get-tuple-element.120), channel_id=1, source_target_pairs={{0,1},{1,0},{2,3},{3,2},{4,5},{5,4},{6,7},{7,6},{8,9},{9,8},{10,11... | collective-permute-start | bytes 1572872 | tf_op jit(solution)/shard_map/ppermute | solution.py:315
  522.0 24.0 %collective-permute-start.43 = (bf16[128,2048]{1,0:T(8,128)(2,1)S(1)}, bf16[128,2048]{1,0:T(8,128)(2,1)S(1)}, u32[]{:S(2)}, u32[]{:S(2)}) collective-permute-start(bf16[128,2048]{1,0:T(8,128)(2,1)S(1)} %get-tuple-element.121), channel_id=1, source_target_pairs={{0,2},{1,3},{2,0},{3,1},{4,6},{5,7},{6,4},{7,5},{8,10},{9,11},{10,... | collective-permute-start | bytes 1572872 | tf_op jit(solution)/shard_map/ppermute | solution.py:315
  534.9 14.9 %collective-permute-start.41 = (bf16[128,2048]{1,0:T(8,128)(2,1)S(1)}, bf16[128,2048]{1,0:T(8,128)(2,1)S(1)}, u32[]{:S(2)}, u32[]{:S(2)}) collective-permute-start(bf16[128,2048]{1,0:T(8,128)(2,1)S(1)} %add_convert_fusion.9), channel_id=1, source_target_pairs={{0,2},{1,3},{2,0},{3,1},{4,6},{5,7},{6,4},{7,5},{8,10},{9,11},{10,... | collective-permute-start | bytes 1572872 | tf_op jit(solution)/shard_map/ppermute | solution.py:315
  536.3 24.7 %collective-permute-start.42 = (bf16[128,2048]{1,0:T(8,128)(2,1)S(1)}, bf16[128,2048]{1,0:T(8,128)(2,1)S(1)}, u32[]{:S(2)}, u32[]{:S(2)}) collective-permute-start(bf16[128,2048]{1,0:T(8,128)(2,1)S(1)} %get-tuple-element.122), channel_id=1, source_target_pairs={{0,2},{1,3},{2,0},{3,1},{4,6},{5,7},{6,4},{7,5},{8,10},{9,11},{10,... | collective-permute-start | bytes 1572872 | tf_op jit(solution)/shard_map/ppermute | solution.py:315
  537.2 20.1 %collective-permute-start.34 = (bf16[128,2048]{1,0:T(8,128)(2,1)S(1)}, bf16[128,2048]{1,0:T(8,128)(2,1)S(1)}, u32[]{:S(2)}, u32[]{:S(2)}) collective-permute-start(bf16[128,2048]{1,0:T(8,128)(2,1)S(1)} %get-tuple-element.129), channel_id=1, source_target_pairs={{0,1},{1,0},{2,3},{3,2},{4,5},{5,4},{6,7},{7,6},{8,9},{9,8},{10,11... | collective-permute-start | bytes 1572872 | tf_op jit(solution)/shard_map/ppermute | solution.py:315
  550.2 18.3 %collective-permute-start.44 = (bf16[128,2048]{1,0:T(8,128)(2,1)S(1)}, bf16[128,2048]{1,0:T(8,128)(2,1)S(1)}, u32[]{:S(2)}, u32[]{:S(2)}) collective-permute-start(bf16[128,2048]{1,0:T(8,128)(2,1)S(1)} %get-tuple-element.119), channel_id=1, source_target_pairs={{0,1},{1,0},{2,3},{3,2},{4,5},{5,4},{6,7},{7,6},{8,9},{9,8},{10,11... | collective-permute-start | bytes 1572872 | tf_op jit(solution)/shard_map/ppermute | solution.py:315
  550.5 28.5 %collective-permute-start.33 = (bf16[128,2048]{1,0:T(8,128)(2,1)S(1)}, bf16[128,2048]{1,0:T(8,128)(2,1)S(1)}, u32[]{:S(2)}, u32[]{:S(2)}) collective-permute-start(bf16[128,2048]{1,0:T(8,128)(2,1)S(1)} %get-tuple-element.126), channel_id=1, source_target_pairs={{0,1},{1,0},{2,3},{3,2},{4,5},{5,4},{6,7},{7,6},{8,9},{9,8},{10,11... | collective-permute-start | bytes 1572872 | tf_op jit(solution)/shard_map/ppermute | solution.py:315
  552.3 26.8 %collective-permute-start.37 = (bf16[128,2048]{1,0:T(8,128)(2,1)S(1)}, bf16[128,2048]{1,0:T(8,128)(2,1)S(1)}, u32[]{:S(2)}, u32[]{:S(2)}) collective-permute-start(bf16[128,2048]{1,0:T(8,128)(2,1)S(1)} %get-tuple-element.127), channel_id=1, source_target_pairs={{0,2},{1,3},{2,0},{3,1},{4,6},{5,7},{6,4},{7,5},{8,10},{9,11},{10,... | collective-permute-start | bytes 1572872 | tf_op jit(solution)/shard_map/ppermute | solution.py:315
  557.3 41.8 %collective-permute-start.36 = (bf16[128,2048]{1,0:T(8,128)(2,1)S(1)}, bf16[128,2048]{1,0:T(8,128)(2,1)S(1)}, u32[]{:S(2)}, u32[]{:S(2)}) collective-permute-start(bf16[128,2048]{1,0:T(8,128)(2,1)S(1)} %get-tuple-element.128), channel_id=1, source_target_pairs={{0,2},{1,3},{2,0},{3,1},{4,6},{5,7},{6,4},{7,5},{8,10},{9,11},{10,... | collective-permute-start | bytes 1572872 | tf_op jit(solution)/shard_map/ppermute | solution.py:315
  561.0 31.3 %collective-permute-start.35 = (bf16[128,2048]{1,0:T(8,128)(2,1)S(1)}, bf16[128,2048]{1,0:T(8,128)(2,1)S(1)}, u32[]{:S(2)}, u32[]{:S(2)}) collective-permute-start(bf16[128,2048]{1,0:T(8,128)(2,1)S(1)} %add_convert_fusion.11), channel_id=1, source_target_pairs={{0,2},{1,3},{2,0},{3,1},{4,6},{5,7},{6,4},{7,5},{8,10},{9,11},{10,... | collective-permute-start | bytes 1572872 | tf_op jit(solution)/shard_map/ppermute | solution.py:315
  569.4 23.7 %collective-permute-start.45 = (f32[2,2048]{1,0:T(2,128)S(1)}, f32[2,2048]{1,0:T(2,128)S(1)}, u32[]{:S(2)}, u32[]{:S(2)}) collective-permute-start(f32[2,2048]{1,0:T(2,128)S(1)} %pad_maximum_fusion.23), channel_id=1, source_target_pairs={{0,1},{1,0},{2,3},{3,2},{4,5},{5,4},{6,7},{7,6},{8,9},{9,8},{10,11... | collective-permute-start | bytes 49160 | tf_op jit(solution)/shard_map/ppermute | solution.py:388
  592.7 11.7 %collective-permute-start.38 = (bf16[128,2048]{1,0:T(8,128)(2,1)S(1)}, bf16[128,2048]{1,0:T(8,128)(2,1)S(1)}, u32[]{:S(2)}, u32[]{:S(2)}) collective-permute-start(bf16[128,2048]{1,0:T(8,128)(2,1)S(1)} %get-tuple-element.125), channel_id=1, source_target_pairs={{0,1},{1,0},{2,3},{3,2},{4,5},{5,4},{6,7},{7,6},{8,9},{9,8},{10,11... | collective-permute-start | bytes 1572872 | tf_op jit(solution)/shard_map/ppermute | solution.py:315
  (99 other events, 1251.5 us)
Sparse Core Ops, SparseCore 0:
  10.5 59.3 all-gather.3
  72.1 141.0 all-gather.5
  215.5 88.8 all-gather.7
  490.3 49.4 reduce-scatter.3
  541.9 85.5 reduce-scatter.7
  629.7 136.6 reduce-scatter.5

commit v5 on v4

--- a/solution.py
+++ b/solution.py
@@ -318,11 +318,25 @@
     relay_low = send(part(3, half), 2).astype(jnp.float32)
     near_top = send(part(1, 0), 1).astype(jnp.float32)
     near_low = send(part(2, half), 2).astype(jnp.float32)
-    joined_top = send(narrow(part(2, 0) + relay_top), 2).astype(jnp.float32)
-    joined_low = send(narrow(part(1, half) + relay_low), 1).astype(jnp.float32)
+    top_sum, low_sum = ordered(narrow(part(2, 0) + relay_top), narrow(part(1, half) + relay_low))
+    joined_top = send(top_sum, 2).astype(jnp.float32)
+    joined_low = send(low_sum, 1).astype(jnp.float32)
     return jnp.concatenate(
         [part(0, 0) + near_top + joined_top, part(0, half) + near_low + joined_low], axis=0
     )
+
+
+def scatter_direct(partial, axis):
+    count = lax.axis_size(axis)
+    if count != 4:
+        return lax.psum_scatter(partial, axis, scatter_dimension=0, tiled=True).astype(jnp.float32)
+    rows = partial.shape[0] // count
+    total = partial[:rows].astype(jnp.float32)
+    for mask in (3, 1, 2):
+        piece = partial[mask * rows : (mask + 1) * rows]
+        got = lax.ppermute(piece, axis, shift_pairs(count, mask))
+        total = total + got.astype(jnp.float32)
+    return total
 
 
 def paired():
@@ -484,7 +498,7 @@
     scale_two, unit_two = rms_stats(hidden)
     normed_two_all = gather_rows(narrow(unit_two * gain_two), "tensor", relative=True)
     normed_split, cotangent_split = split_columns(normed_two_all), split_columns(grad_mlp_all)
-    normed_total = mlp_total = None
+    normed_total = first_act = None
     weight_grads = []
     for number, weights in enumerate(halves):
         pair_cols = 2 * (weights.shape[1] // 3)
@@ -500,19 +514,21 @@
         if number == 0:
             grad_pair, activation, partial = ordered(grad_pair, activation, partial)
             normed_total = narrow(contract(grad_pair, pair_weights, 1, 1))
-            mlp_total = narrow(contract(activation, down_weights, 1, 1))
-            normed_two_all, grad_mlp_all, partial, normed_total, mlp_total = ordered(
-                normed_two_all, grad_mlp_all, partial, normed_total, mlp_total
+            first_act, first_down = activation, down_weights
+            normed_two_all, grad_mlp_all, normed_total = ordered(
+                normed_two_all, grad_mlp_all, normed_total
             )
         weight_grads.append(sum_shards(partial))
     mlp_gain_part = jnp.sum(grad_normed_two * unit_two, axis=0)
     grad_hidden = grad_out + norm_backward(grad_normed_two, unit_two, scale_two, gain_two)
     grad_attn = narrow(grad_hidden * valid_own)
-    activation, grad_attn = ordered(activation, grad_attn)
+    activation, first_act, grad_attn = ordered(activation, first_act, grad_attn)
     grad_attn_all = gather_rows(grad_attn, "tensor")
-    mlp_part = narrow(contract(activation, down_weights, 1, 1) + mlp_total.astype(jnp.float32))
+    mlp_part = narrow(
+        contract(first_act, first_down, 1, 1) + contract(activation, down_weights, 1, 1)
+    )
     grad_attn_all, mlp_part = ordered(grad_attn_all, mlp_part)
-    mlp_out = scatter_rows(mlp_part, "tensor", relative=True)
+    mlp_out = scatter_direct(mlp_part, "tensor")
     output = hidden + valid_own * mlp_out
     grad_attended = narrow(contract(full_output, grad_attn_all, 0, 1))
     joint_back = attend_back(
@@ -539,7 +555,21 @@
     grad_normed_one = scatter_rows(last_part, "tensor")
     attn_gain_part = jnp.sum(grad_normed_one * unit_one, axis=0)
     input_grad = grad_hidden + norm_backward(grad_normed_one, unit_one, scale_one, gain_one)
-    gain_sums = sum_everywhere(jnp.stack([attn_gain_part, mlp_gain_part]), ("tensor", "dp"))
+    w_gate_grad = jnp.concatenate(
+        [part[:, : part.shape[1] // 3] for part in weight_grads], axis=1
+    )
+    w_up_grad = jnp.concatenate(
+        [part[:, part.shape[1] // 3 : 2 * (part.shape[1] // 3)] for part in weight_grads], axis=1
+    )
+    w_down_grad = jnp.concatenate(
+        [part[:, 2 * (part.shape[1] // 3) :].T for part in weight_grads], axis=0
+    )
+    attn_gain_part, w_gate_grad, w_up_grad, w_down_grad = ordered(
+        attn_gain_part, w_gate_grad, w_up_grad, w_down_grad
+    )
+    gain_sums = sum_everywhere(
+        jnp.stack([attn_gain_part, mlp_gain_part]), ("tensor", "dp")
+    )
     gain_own = lax.dynamic_slice_in_dim(gain_sums, lax.axis_index("dp") * gain_rows, gain_rows, 1)
     return (
         output,
@@ -550,14 +580,9 @@
         tail_grad[:, query_cols + key_cols : joint],
         tail_grad[:, joint:].T,
         gain_own[1],
-        jnp.concatenate([part[:, : part.shape[1] // 3] for part in weight_grads], axis=1),
-        jnp.concatenate(
-            [part[:, part.shape[1] // 3 : 2 * (part.shape[1] // 3)] for part in weight_grads],
-            axis=1,
-        ),
-        jnp.concatenate(
-            [part[:, 2 * (part.shape[1] // 3) :].T for part in weight_grads], axis=0
-        ),
+        w_gate_grad,
+        w_up_grad,
+        w_down_grad,
     )
 
 

time: 791 us -> 690 us (0.87)
  waiting for transfers between devices: 379 us -> 279 us
    reduce_scatter x3, waiting for transfers between devices: 146 us -> 61.1 us  [sum_shards(): lax.psum_scatter(partial, 'dp', scatter_dimension=0, tiled=True, axis_ind...]
    ppermute x24 -> x18, waiting for transfers between devices: 121 us -> 104 us  [send(): return lax.ppermute(piece, axis, shift_pairs(count, mask))]
    ppermute x24 -> x18, starting transfers between devices: 26.7 us -> 18 us  [send(): return lax.ppermute(piece, axis, shift_pairs(count, mask))]
    convert_element_type x8 -> x6, other arithmetic: 18 us -> 15.6 us  [narrow(): return value.astype(jnp.bfloat16)]
    unnamed x176 -> x178, local copies, waits for them, and re-layouts: 18.6 us -> 18.2 us
  transfers between devices with their start and end apart: 60 -> 57, of which waited for: 42 -> 33; matrix products, arithmetic and copies ran while one was open for 25% -> 31% of each run, Pallas kernels for 4% -> 9%
where the time goes in v5:
time: 690 us; the launch traced here: 683 us
  waiting for transfers between devices  279 us (40%)
  matrix products  155 us (22%)
  Pallas kernels  64.7 us (9%)
  other arithmetic  64.4 us (9%)
  starting transfers between devices  54 us (8%)
  local copies, waits for them, and re-layouts  50.2 us (7%)
  between operations  16.1 us (2%)
    dot_general x20, matrix products, contract(): lax.dot_general(left, right, (((left_axis,), (right_axis,)), ((), ())), p...  110 us
    ppermute x18, waiting for transfers between devices, send(): return lax.ppermute(piece, axis, shift_pairs(count, mask))  104 us
    reduce_scatter x3, waiting for transfers between devices, sum_shards(): lax.psum_scatter(partial, 'dp', scatter_dimension=0, tiled=True, axis_ind...  61.1 us
    ppermute x4, waiting for transfers between devices, gather_rows(): from_x = lax.ppermute(block, axis, shift_pairs(count, 1))  46 us
    dot_general x4, matrix products, product(): return jnp.dot(left, right, preferred_element_type=jnp.float32)  44.7 us
    pallas_call x1, Pallas kernels, attend(): pl.pallas_call(functools.partial(attend_kernel, heads, kv_heads, block),...  25.6 us
    pallas_call x1, Pallas kernels, attend_back(): pl.pallas_call(functools.partial(attend_back_kernel, heads, kv_heads, blo...  23.5 us
    ppermute x4, waiting for transfers between devices, gather_rows(): far_low = lax.ppermute(from_y[half:], axis, shift_pairs(count, 1))  21.1 us
  transfers between devices with their start and end apart: 57, of which 33 were waited for; matrix products, arithmetic and copies ran while one was open for 31% of the time, Pallas kernels for 9%

profile of v5, /device:TPU:0, one launch (start us, length us, event | category | flops | bytes accessed | tf_op | source)
XLA Modules:
  0.0 682.8 jit_solution(10128498615982032019)
XLA Ops:
  32.3 7.4 %collective-permute-done = bf16[256,2048]{1,0:T(8,128)(2,1)S(1)} collective-permute-done((bf16[256,2048]{1,0:T(8,128)(2,1)S(1)}, bf16[256,2048]{1,0:T(8,128)(2,1)S(1)}, u32[]{:S(2)}, u32[]{:S(2)}) %collective-permute-start) | collective-permute-done | bytes 1048608 | tf_op jit(solution)/shard_map/ppermute | solution.py:285
  47.7 5.3 collective-permute-done.2
  59.4 5.2 fusion.6
  64.6 5.3 all-gather.4.cloned.1.call-done
  69.9 8.2 %fusion.25.joint_ref = f32[768,1024]{1,0:T(8,128)} fusion(bf16[1024,2048]{1,0:T(8,128)(2,1)} %fusion.6, bf16[2048,1280]{1,0:T(8,128)(2,1)} %all-gather.4.cloned.1.call-done), kind=kOutput, calls=%fused_computation.42 | convolution fusion | flops 3221225472 | bytes 10485760 | tf_op jit(solution)/shard_map/dot_general | solution.py:412
  78.1 25.6 %attend.1 = (bf16[768,1024]{1,0:T(8,128)(2,1)}, bf16[512,1024]{1,0:T(8,128)(2,1)}, f32[8,1024]{1,0:T(8,128)}) custom-call(f32[768,1024]{1,0:T(8,128)} %fusion.25.joint_ref, f32[32,1024]{1,0:T(8,128)} %get-tuple-element.189.cos_ref, f32[32,1024]{1,0:T(8,128)} %get-tuple-element.188.sin_ref, s32[1,1024]{1,0:T(1,128)} %bitcast.59, s32[1024,1]{1,0:T(8,128)} %copy.40.seg_col_ref), custom_call_target="tpu_custom_call" | custom-call | flops 8589934592 | bytes 6291456 | tf_op jit(solution)/shard_map/attend/pallas_call | solution.py:232
  103.7 4.3 convolution_convert_fusion.1
  118.4 8.0 %collective-permute-done.8 = bf16[128,2048]{1,0:T(8,128)(2,1)} collective-permute-done((bf16[128,2048]{1,0:T(8,128)(2,1)}, bf16[128,2048]{1,0:T(8,128)(2,1)}, u32[]{:S(2)}, u32[]{:S(2)}) %collective-permute-start.8) | collective-permute-done | bytes 524320 | tf_op jit(solution)/shard_map/ppermute | solution.py:315
  132.9 15.9 %collective-permute-done.17 = bf16[256,2048]{1,0:T(8,128)(2,1)S(1)} collective-permute-done((bf16[256,2048]{1,0:T(8,128)(2,1)}, bf16[256,2048]{1,0:T(8,128)(2,1)S(1)}, u32[]{:S(2)}, u32[]{:S(2)}) %collective-permute-start.17) | collective-permute-done | bytes 1048608 | tf_op jit(solution)/shard_map/ppermute | solution.py:285
  151.6 8.5 %collective-permute-done.7 = bf16[128,2048]{1,0:T(8,128)(2,1)} collective-permute-done((bf16[128,2048]{1,0:T(8,128)(2,1)}, bf16[128,2048]{1,0:T(8,128)(2,1)}, u32[]{:S(2)}, u32[]{:S(2)}) %collective-permute-start.7) | collective-permute-done | bytes 524320 | tf_op jit(solution)/shard_map/ppermute | solution.py:315
  160.1 10.5 %collective-permute-done.12 = bf16[128,2048]{1,0:T(8,128)(2,1)} collective-permute-done((bf16[128,2048]{1,0:T(8,128)(2,1)}, bf16[128,2048]{1,0:T(8,128)(2,1)}, u32[]{:S(2)}, u32[]{:S(2)}) %collective-permute-start.12) | collective-permute-done | bytes 524320 | tf_op jit(solution)/shard_map/ppermute | solution.py:315
  188.3 15.1 %collective-permute-done.13 = bf16[256,2048]{1,0:T(8,128)(2,1)S(1)} collective-permute-done((bf16[256,2048]{1,0:T(8,128)(2,1)}, bf16[256,2048]{1,0:T(8,128)(2,1)S(1)}, u32[]{:S(2)}, u32[]{:S(2)}) %collective-permute-start.13) | collective-permute-done | bytes 1048608 | tf_op jit(solution)/shard_map/ppermute | solution.py:285
  205.0 8.1 %collective-permute-done.20 = bf16[128,2048]{1,0:T(8,128)(2,1)S(1)} collective-permute-done((bf16[128,2048]{1,0:T(8,128)(2,1)S(1)}, bf16[128,2048]{1,0:T(8,128)(2,1)S(1)}, u32[]{:S(2)}, u32[]{:S(2)}) %collective-permute-start.20) | collective-permute-done | bytes 524320 | tf_op jit(solution)/shard_map/ppermute | solution.py:288
  218.2 9.5 %collective-permute-done.16 = bf16[128,2048]{1,0:T(8,128)(2,1)S(1)} collective-permute-done((bf16[128,2048]{1,0:T(8,128)(2,1)S(1)}, bf16[128,2048]{1,0:T(8,128)(2,1)S(1)}, u32[]{:S(2)}, u32[]{:S(2)}) %collective-permute-start.16) | collective-permute-done | bytes 524320 | tf_op jit(solution)/shard_map/ppermute | solution.py:288
  232.6 12.2 %fusion.13.grad_ref = f32[1024,1280]{1,0:T(8,128)} fusion(bf16[1024,2048]{1,0:T(8,128)(2,1)} %constant_dynamic-update-slice_fusion.5, bf16[2048,3840]{1,0:T(8,128)(2,1)} %all-gather.6.cloned.1.call-done), kind=kOutput, calls=%fused_computation.23 | convolution fusion | flops 5368709120 | bytes 14680064 | tf_op jit(solution)/shard_map/dot_general | solution.py:408
  244.8 13.5 %fusion.2.pair_ref = f32[1024,2560]{1,0:T(8,128)} fusion(bf16[1024,2048]{1,0:T(8,128)(2,1)S(1)} %copy-done.14, bf16[2048,3840]{1,0:T(8,128)(2,1)S(1)} %copy-done.71), kind=kOutput, calls=%fused_computation.5 | convolution fusion | flops 10737418240 | bytes 25165824 | tf_op jit(solution)/shard_map/dot_general | solution.py:408
  258.3 9.1 %activation_both.2 = (bf16[1024,1280]{1,0:T(8,128)(2,1)}, bf16[1024,2560]{1,0:T(8,128)(2,1)}) custom-call(f32[1024,2560]{1,0:T(8,128)} %fusion.2.pair_ref, f32[1024,1280]{1,0:T(8,128)} %fusion.13.grad_ref), custom_call_target="tpu_custom_call" | custom-call | flops 52428800 | bytes 23592960 | tf_op jit(solution)/shard_map/activation_both/pallas_call | solution.py:209
  267.5 8.3 %convolution_convert_fusion = bf16[1024,2560]{1,0:T(8,128)(2,1)S(1)} fusion(bf16[1024,2560]{1,0:T(8,128)(2,1)} %get-tuple-element.47, bf16[1024,256]{1,0:T(8,128)(2,1)} %get-tuple-element.198, bf16[1024,256]{1,0:T(8,128)(2,1)} %get-tuple-element.197, bf16[1024,256]{1,0:T(8,128)(2,1)} %get-tuple-element.196, bf16[1024,256]{1,0:T(8,128)(2,1)S(1)} %get-tuple-element.195), kind=kOutput, calls=%fused_computation.14 | convolution fusion | flops 5379719168 | bytes 12582912 | tf_op jit(solution)/shard_map/dot_general | solution.py:412
  279.9 9.2 %collective-permute-done.22 = bf16[1024,1280]{1,0:T(8,128)(2,1)S(1)} collective-permute-done((bf16[1024,1280]{1,0:T(8,128)(2,1)S(1)}, bf16[1024,1280]{1,0:T(8,128)(2,1)S(1)}, u32[]{:S(2)}, u32[]{:S(2)}) %collective-permute-start.22) | collective-permute-done | bytes 2621472 | tf_op jit(solution)/shard_map/ppermute | solution.py:380
  289.1 3.7 add_convert_fusion.4
  292.9 7.7 %add_convert_fusion = bf16[1024,2560]{1,0:T(8,128)(2,1)} fusion(bf16[1024,2560]{1,0:T(8,128)(2,1)S(1)} %collective-permute-done.21, bf16[1024,2560]{1,0:T(8,128)(2,1)S(1)} %bitcast.67, bf16[1024,256]{1,0:T(8,128)(2,1)S(1)} %copy-done.27, bf16[1024,256]{1,0:T(8,128)(2,1)S(1)} %copy-done.25, bf16[1024,256]{1,0:T(8,128)(2,1)S(1)} %get-tuple-element.192, ...), kind=kOutput, calls=%fused_computation.2 | convolution fusion | flops 5384962048 | bytes 17825792 | tf_op jit(solution)/shard_map/dot_general | solution.py:412
  300.5 6.1 pad_maximum_fusion
  306.7 16.6 %fusion.15 = bf16[1024,2048]{1,0:T(8,128)(2,1)} fusion(bf16[1024,2560]{1,0:T(8,128)(2,1)} %get-tuple-element.47, bf16[2048,3840]{1,0:T(8,128)(2,1)} %all-gather.6.cloned.1.call-done), kind=kOutput, calls=%fused_computation.29 | convolution fusion | flops 10739515392 | bytes 19922944 | tf_op jit(solution)/shard_map/dot_general | solution.py:412
  323.3 11.9 %fusion.9.pair_ref = f32[1024,1536]{1,0:T(8,128)} fusion(bf16[1024,2048]{1,0:T(8,128)(2,1)} %copy-done.13, bf16[2048,2304]{1,0:T(8,128)(2,1)} %all-gather.8.cloned.1.call-done), kind=kOutput, calls=%fused_computation.17 | convolution fusion | flops 6442450944 | bytes 16777216 | tf_op jit(solution)/shard_map/dot_general | solution.py:408
  335.2 7.0 %fusion.22.grad_ref = f32[1024,768]{1,0:T(8,128)} fusion(bf16[1024,2048]{1,0:T(8,128)(2,1)S(1)} %copy-done.11, bf16[2048,2304]{1,0:T(8,128)(2,1)} %all-gather.8.cloned.1.call-done), kind=kOutput, calls=%fused_computation.39 | convolution fusion | flops 3221225472 | bytes 10485760 | tf_op jit(solution)/shard_map/dot_general | solution.py:408
  342.2 6.5 activation_both.3
  348.7 10.3 %fusion.7 = f32[1024,2048]{1,0:T(8,128)S(1)} fusion(bf16[1024,1536]{1,0:T(8,128)(2,1)} %get-tuple-element.68, bf16[2048,2304]{1,0:T(8,128)(2,1)} %all-gather.8.cloned.1.call-done), kind=kOutput, calls=%fused_computation.15 | convolution fusion | flops 6442450944 | bytes 17825792 | tf_op jit(solution)/shard_map/dot_general | solution.py:412
  359.0 3.4 add_convert_fusion.2
  362.5 5.8 convolution_convert_fusion.2
  371.0 5.4 collective-permute-done.43
  378.4 4.0 add_convert_fusion.3
  391.6 10.7 %collective-permute-done.24 = bf16[128,2048]{1,0:T(8,128)(2,1)S(1)} collective-permute-done((bf16[128,2048]{1,0:T(8,128)(2,1)S(1)}, bf16[128,2048]{1,0:T(8,128)(2,1)S(1)}, u32[]{:S(2)}, u32[]{:S(2)}) %collective-permute-start.24) | collective-permute-done | bytes 524320 | tf_op jit(solution)/shard_map/ppermute | solution.py:315
  409.5 4.2 collective-permute-done.23
  415.1 10.1 %collective-permute-done.26 = bf16[128,2048]{1,0:T(8,128)(2,1)S(1)} collective-permute-done((bf16[128,2048]{1,0:T(8,128)(2,1)S(1)}, bf16[128,2048]{1,0:T(8,128)(2,1)S(1)}, u32[]{:S(2)}, u32[]{:S(2)}) %collective-permute-start.26) | collective-permute-done | bytes 524320 | tf_op jit(solution)/shard_map/ppermute | solution.py:315
  431.8 7.6 %fusion.11 = f32[1024,2048]{1,0:T(8,128)S(1)} fusion(bf16[1024,1280]{1,0:T(8,128)(2,1)S(1)} %copy-done.74, bf16[2048,3840]{1,0:T(8,128)(2,1)} %all-gather.6.cloned.1.call-done), kind=kOutput, calls=%fused_computation.21 | convolution fusion | flops 5368709120 | bytes 16252928 | tf_op jit(solution)/shard_map/dot_general | solution.py:412
  439.4 7.0 %add_convert_fusion.1 = bf16[1024,2048]{1,0:T(8,128)(2,1)} fusion(f32[1024,2048]{1,0:T(8,128)S(1)} %fusion.11, bf16[1024,768]{1,0:T(8,128)(2,1)S(1)} %copy-done.76, bf16[2048,2304]{1,0:T(8,128)(2,1)} %all-gather.8.cloned.1.call-done), kind=kOutput, calls=%fused_computation.10 | convolution fusion | flops 3225419776 | bytes 17301504 | tf_op jit(solution)/shard_map/dot_general | solution.py:412
  446.3 7.6 %collective-permute-done.29 = bf16[256,2048]{1,0:T(8,128)(2,1)S(1)} collective-permute-done((bf16[256,2048]{1,0:T(8,128)(2,1)S(1)}, bf16[256,2048]{1,0:T(8,128)(2,1)S(1)}, u32[]{:S(2)}, u32[]{:S(2)}) %collective-permute-start.29) | collective-permute-done | bytes 1048608 | tf_op jit(solution)/shard_map/ppermute | solution.py:285
  457.0 9.2 %collective-permute-done.31 = bf16[128,2048]{1,0:T(8,128)(2,1)S(1)} collective-permute-done((bf16[128,2048]{1,0:T(8,128)(2,1)S(1)}, bf16[128,2048]{1,0:T(8,128)(2,1)S(1)}, u32[]{:S(2)}, u32[]{:S(2)}) %collective-permute-start.31) | collective-permute-done | bytes 524320 | tf_op jit(solution)/shard_map/ppermute | solution.py:287
  472.2 5.0 fusion.77.out_ref
  477.2 23.5 %attend_back.1 = bf16[768,1024]{1,0:T(8,128)(2,1)} custom-call(bf16[768,1024]{1,0:T(8,128)(2,1)} %get-tuple-element.62.rot_ref, bf16[512,1024]{1,0:T(8,128)(2,1)} %get-tuple-element.42.att_ref, bf16[512,1024]{1,0:T(8,128)(2,1)} %fusion.77.out_ref, f32[8,1024]{1,0:T(8,128)} %get-tuple-element.64.log_ref, f32[32,1024]{1,0:T(8,128)} %get-tuple-element.189.cos_ref, ...), custom_call_target="tpu_custom_call" | custom-call | flops 21474836480 | bytes 6291456 | tf_op jit(solution)/shard_map/attend_back/pallas_call | solution.py:255
  500.7 5.9 convolution_convert_fusion.3
  512.3 9.4 %collective-permute-done.37 = bf16[128,2048]{1,0:T(8,128)(2,1)S(1)} collective-permute-done((bf16[128,2048]{1,0:T(8,128)(2,1)S(1)}, bf16[128,2048]{1,0:T(8,128)(2,1)S(1)}, u32[]{:S(2)}, u32[]{:S(2)}) %collective-permute-start.37) | collective-permute-done | bytes 524320 | tf_op jit(solution)/shard_map/ppermute | solution.py:315
  529.4 3.6 collective-permute-done.36
  533.0 3.6 collective-permute-done.40
  537.3 31.2 %collective-permute-done.39 = bf16[128,2048]{1,0:T(8,128)(2,1)S(1)} collective-permute-done((bf16[128,2048]{1,0:T(8,128)(2,1)S(1)}, bf16[128,2048]{1,0:T(8,128)(2,1)S(1)}, u32[]{:S(2)}, u32[]{:S(2)}) %collective-permute-start.39) | collective-permute-done | bytes 524320 | tf_op jit(solution)/shard_map/ppermute | solution.py:315
  581.6 26.0 %reduce-scatter.4.cloned.1.call-done = bf16[256,3840]{1,0:T(8,128)(2,1)} async-done(((bf16[1024,3840]{1,0:T(8,128)(2,1)}), bf16[256,3840]{1,0:T(8,128)(2,1)}) %reduce-scatter.4.cloned.1.call-update) | async-done | bytes 1966096 | tf_op jit(solution)/shard_map/reduce_scatter | solution.py:388
  617.3 4.3 multiply_add_fusion
  627.5 35.1 %reduce-scatter.8.cloned.1.call-done = bf16[256,1280]{1,0:T(8,128)(2,1)} async-done(((bf16[1024,1280]{1,0:T(8,128)(2,1)}), bf16[256,1280]{1,0:T(8,128)(2,1)}) %reduce-scatter.8.cloned.1.call-update) | async-done | bytes 655376 | tf_op jit(solution)/shard_map/reduce_scatter | solution.py:388
  (382 shorter events, 185.2 us)
Async XLA Ops:
  7.2 62.7 %all-gather.4.cloned.1.call-start = ((), (), s32[]{:S(2)}) async-start(), calls=%async_computation.3 | async-start | bytes 5898240 | tf_op jit(solution)/shard_map/all_gather | solution.py:460
  10.4 222.2 %all-gather.6.cloned.1.call-start = ((), (), s32[]{:S(2)}) async-start(), calls=%async_computation.4 | async-start | bytes 17694720 | tf_op jit(solution)/shard_map/all_gather | solution.py:472
  13.5 309.8 %all-gather.8.cloned.1.call-start = ((), (), s32[]{:S(2)}) async-start(), calls=%async_computation.5 | async-start | bytes 10616832 | tf_op jit(solution)/shard_map/all_gather | solution.py:472
  13.5 26.2 %collective-permute-start = (bf16[256,2048]{1,0:T(8,128)(2,1)S(1)}, bf16[256,2048]{1,0:T(8,128)(2,1)S(1)}, u32[]{:S(2)}, u32[]{:S(2)}) collective-permute-start(bf16[256,2048]{1,0:T(8,128)(2,1)S(1)} %copy-done.2), channel_id=1, source_target_pairs={{0,1},{1,0},{2,3},{3,2},{4,5},{5,4},{6,7},{7,6},{8,9},{9,8},{10,11... | collective-permute-start | bytes 3145736 | tf_op jit(solution)/shard_map/ppermute | solution.py:285
  16.6 25.1 %collective-permute-start.1 = (bf16[256,2048]{1,0:T(8,128)(2,1)S(1)}, bf16[256,2048]{1,0:T(8,128)(2,1)}, u32[]{:S(2)}, u32[]{:S(2)}) collective-permute-start(bf16[256,2048]{1,0:T(8,128)(2,1)S(1)} %copy-done.2), channel_id=1, source_target_pairs={{0,2},{1,3},{2,0},{3,1},{4,6},{5,7},{6,4},{7,5},{8,10},{9,11},{10,... | collective-permute-start | bytes 3145736 | tf_op jit(solution)/shard_map/ppermute | solution.py:286
  39.8 13.3 %collective-permute-start.2 = (bf16[128,2048]{1,0:T(8,128)(2,1)S(1)}, bf16[128,2048]{1,0:T(8,128)(2,1)S(1)}, u32[]{:S(2)}, u32[]{:S(2)}) collective-permute-start(bf16[128,2048]{1,0:T(8,128)(2,1)S(1)} %slice.153), channel_id=1, source_target_pairs={{0,2},{1,3},{2,0},{3,1},{4,6},{5,7},{6,4},{7,5},{8,10},{9,11},{10,... | collective-permute-start | bytes 1572872 | tf_op jit(solution)/shard_map/ppermute | solution.py:287
  42.8 12.7 %collective-permute-start.3 = (bf16[128,2048]{1,0:T(8,128)(2,1)S(1)}, bf16[128,2048]{1,0:T(8,128)(2,1)S(1)}, u32[]{:S(2)}, u32[]{:S(2)}) collective-permute-start(bf16[128,2048]{1,0:T(8,128)(2,1)S(1)} %slice.154), channel_id=1, source_target_pairs={{0,1},{1,0},{2,3},{3,2},{4,5},{5,4},{6,7},{7,6},{8,9},{9,8},{10,11... | collective-permute-start | bytes 1572872 | tf_op jit(solution)/shard_map/ppermute | solution.py:288
  111.3 15.1 %collective-permute-start.8 = (bf16[128,2048]{1,0:T(8,128)(2,1)}, bf16[128,2048]{1,0:T(8,128)(2,1)}, u32[]{:S(2)}, u32[]{:S(2)}) collective-permute-start(bf16[128,2048]{1,0:T(8,128)(2,1)} %get-tuple-element.176), channel_id=1, source_target_pairs={{0,1},{1,0},{2,3},{3,2},{4,5},{5,4},{6,7},{7,6},{8,9},{9,8},{10,11... | collective-permute-start | bytes 1572872 | tf_op jit(solution)/shard_map/ppermute | solution.py:315
  112.8 15.1 %collective-permute-start.9 = (bf16[128,2048]{1,0:T(8,128)(2,1)}, bf16[128,2048]{1,0:T(8,128)(2,1)}, u32[]{:S(2)}, u32[]{:S(2)}) collective-permute-start(bf16[128,2048]{1,0:T(8,128)(2,1)} %get-tuple-element.175), channel_id=1, source_target_pairs={{0,2},{1,3},{2,0},{3,1},{4,6},{5,7},{6,4},{7,5},{8,10},{9,11},{10,... | collective-permute-start | bytes 1572872 | tf_op jit(solution)/shard_map/ppermute | solution.py:315
  115.9 32.9 %collective-permute-start.17 = (bf16[256,2048]{1,0:T(8,128)(2,1)}, bf16[256,2048]{1,0:T(8,128)(2,1)S(1)}, u32[]{:S(2)}, u32[]{:S(2)}) collective-permute-start(bf16[256,2048]{1,0:T(8,128)(2,1)} %get-tuple-element.115), channel_id=1, source_target_pairs={{0,1},{1,0},{2,3},{3,2},{4,5},{5,4},{6,7},{7,6},{8,9},{9,8},{10,11... | collective-permute-start | bytes 3145736 | tf_op jit(solution)/shard_map/ppermute | solution.py:285
  116.4 34.7 %collective-permute-start.11 = (bf16[128,2048]{1,0:T(8,128)(2,1)}, bf16[128,2048]{1,0:T(8,128)(2,1)}, u32[]{:S(2)}, u32[]{:S(2)}) collective-permute-start(bf16[128,2048]{1,0:T(8,128)(2,1)} %get-tuple-element.174), channel_id=1, source_target_pairs={{0,2},{1,3},{2,0},{3,1},{4,6},{5,7},{6,4},{7,5},{8,10},{9,11},{10,... | collective-permute-start | bytes 1572872 | tf_op jit(solution)/shard_map/ppermute | solution.py:315
  116.9 43.2 %collective-permute-start.7 = (bf16[128,2048]{1,0:T(8,128)(2,1)}, bf16[128,2048]{1,0:T(8,128)(2,1)}, u32[]{:S(2)}, u32[]{:S(2)}) collective-permute-start(bf16[128,2048]{1,0:T(8,128)(2,1)} %get-tuple-element.173), channel_id=1, source_target_pairs={{0,1},{1,0},{2,3},{3,2},{4,5},{5,4},{6,7},{7,6},{8,9},{9,8},{10,11... | collective-permute-start | bytes 1572872 | tf_op jit(solution)/shard_map/ppermute | solution.py:315
  130.8 29.3 %collective-permute-start.10 = (bf16[128,2048]{1,0:T(8,128)(2,1)}, bf16[128,2048]{1,0:T(8,128)(2,1)}, u32[]{:S(2)}, u32[]{:S(2)}) collective-permute-start(bf16[128,2048]{1,0:T(8,128)(2,1)} %get-tuple-element.43), channel_id=1, source_target_pairs={{0,2},{1,3},{2,0},{3,1},{4,6},{5,7},{6,4},{7,5},{8,10},{9,11},{10,... | collective-permute-start | bytes 1572872 | tf_op jit(solution)/shard_map/ppermute | solution.py:315
  132.3 38.3 %collective-permute-start.12 = (bf16[128,2048]{1,0:T(8,128)(2,1)}, bf16[128,2048]{1,0:T(8,128)(2,1)}, u32[]{:S(2)}, u32[]{:S(2)}) collective-permute-start(bf16[128,2048]{1,0:T(8,128)(2,1)} %get-tuple-element.44), channel_id=1, source_target_pairs={{0,1},{1,0},{2,3},{3,2},{4,5},{5,4},{6,7},{7,6},{8,9},{9,8},{10,11... | collective-permute-start | bytes 1572872 | tf_op jit(solution)/shard_map/ppermute | solution.py:315
  148.8 32.6 %collective-permute-start.18 = (bf16[256,2048]{1,0:T(8,128)(2,1)}, bf16[256,2048]{1,0:T(8,128)(2,1)S(1)}, u32[]{:S(2)}, u32[]{:S(2)}) collective-permute-start(bf16[256,2048]{1,0:T(8,128)(2,1)} %get-tuple-element.115), channel_id=1, source_target_pairs={{0,2},{1,3},{2,0},{3,1},{4,6},{5,7},{6,4},{7,5},{8,10},{9,11},{10,... | collective-permute-start | bytes 3145736 | tf_op jit(solution)/shard_map/ppermute | solution.py:286
  151.1 35.2 %collective-permute-start.19 = (bf16[128,2048]{1,0:T(8,128)(2,1)}, bf16[128,2048]{1,0:T(8,128)(2,1)}, u32[]{:S(2)}, u32[]{:S(2)}) collective-permute-start(bf16[128,2048]{1,0:T(8,128)(2,1)} %slice.160), channel_id=1, source_target_pairs={{0,2},{1,3},{2,0},{3,1},{4,6},{5,7},{6,4},{7,5},{8,10},{9,11},{10,... | collective-permute-start | bytes 1572872 | tf_op jit(solution)/shard_map/ppermute | solution.py:287
  177.2 26.2 %collective-permute-start.13 = (bf16[256,2048]{1,0:T(8,128)(2,1)}, bf16[256,2048]{1,0:T(8,128)(2,1)S(1)}, u32[]{:S(2)}, u32[]{:S(2)}) collective-permute-start(bf16[256,2048]{1,0:T(8,128)(2,1)} %get-tuple-element.117), channel_id=1, source_target_pairs={{0,1},{1,0},{2,3},{3,2},{4,5},{5,4},{6,7},{7,6},{8,9},{9,8},{10,11... | collective-permute-start | bytes 3145736 | tf_op jit(solution)/shard_map/ppermute | solution.py:285
  178.7 35.3 %collective-permute-start.14 = (bf16[256,2048]{1,0:T(8,128)(2,1)}, bf16[256,2048]{1,0:T(8,128)(2,1)}, u32[]{:S(2)}, u32[]{:S(2)}) collective-permute-start(bf16[256,2048]{1,0:T(8,128)(2,1)} %get-tuple-element.117), channel_id=1, source_target_pairs={{0,2},{1,3},{2,0},{3,1},{4,6},{5,7},{6,4},{7,5},{8,10},{9,11},{10,... | collective-permute-start | bytes 3145736 | tf_op jit(solution)/shard_map/ppermute | solution.py:286
  181.3 396.6 %reduce-scatter.6.cloned.1.call-start = ((), (), s32[]{:S(2)}) async-start(), calls=%async_computation.7 | async-start | bytes 5898240 | tf_op jit(solution)/shard_map/reduce_scatter | solution.py:388
  181.4 31.7 %collective-permute-start.20 = (bf16[128,2048]{1,0:T(8,128)(2,1)S(1)}, bf16[128,2048]{1,0:T(8,128)(2,1)S(1)}, u32[]{:S(2)}, u32[]{:S(2)}) collective-permute-start(bf16[128,2048]{1,0:T(8,128)(2,1)S(1)} %slice.161), channel_id=1, source_target_pairs={{0,1},{1,0},{2,3},{3,2},{4,5},{5,4},{6,7},{7,6},{8,9},{9,8},{10,11... | collective-permute-start | bytes 1572872 | tf_op jit(solution)/shard_map/ppermute | solution.py:288
  203.4 14.7 %collective-permute-start.15 = (bf16[128,2048]{1,0:T(8,128)(2,1)S(1)}, bf16[128,2048]{1,0:T(8,128)(2,1)S(1)}, u32[]{:S(2)}, u32[]{:S(2)}) collective-permute-start(bf16[128,2048]{1,0:T(8,128)(2,1)S(1)} %slice.158), channel_id=1, source_target_pairs={{0,2},{1,3},{2,0},{3,1},{4,6},{5,7},{6,4},{7,5},{8,10},{9,11},{10,... | collective-permute-start | bytes 1572872 | tf_op jit(solution)/shard_map/ppermute | solution.py:287
  215.2 12.6 %collective-permute-start.16 = (bf16[128,2048]{1,0:T(8,128)(2,1)S(1)}, bf16[128,2048]{1,0:T(8,128)(2,1)S(1)}, u32[]{:S(2)}, u32[]{:S(2)}) collective-permute-start(bf16[128,2048]{1,0:T(8,128)(2,1)S(1)} %slice.159), channel_id=1, source_target_pairs={{0,1},{1,0},{2,3},{3,2},{4,5},{5,4},{6,7},{7,6},{8,9},{9,8},{10,11... | collective-permute-start | bytes 1572872 | tf_op jit(solution)/shard_map/ppermute | solution.py:288
  275.8 17.0 %collective-permute-start.21 = (bf16[1024,2560]{1,0:T(8,128)(2,1)S(1)}, bf16[1024,2560]{1,0:T(8,128)(2,1)S(1)}, u32[]{:S(2)}, u32[]{:S(2)}) collective-permute-start(bf16[1024,2560]{1,0:T(8,128)(2,1)S(1)} %convolution_convert_fusion), channel_id=1, source_target_pairs={{0,4},{4,0},{8,12},{12,8},{16,20},{20,16},{24,28},{28,24},{1,5},{5... | collective-permute-start | bytes 15728648 | tf_op jit(solution)/shard_map/ppermute | solution.py:380
  368.4 9.9 %collective-permute-start.42 = (bf16[1024,1536]{1,0:T(8,128)(2,1)S(1)}, bf16[1024,1536]{1,0:T(8,128)(2,1)S(1)}, u32[]{:S(2)}, u32[]{:S(2)}) collective-permute-start(bf16[1024,1536]{1,0:T(8,128)(2,1)S(1)} %convolution_convert_fusion.2), channel_id=1, source_target_pairs={{0,4},{4,0},{8,12},{12,8},{16,20},{20,16},{24,28},{28,24},{1,5},{5... | collective-permute-start | bytes 9437192 | tf_op jit(solution)/shard_map/ppermute | solution.py:380
  384.9 222.7 %reduce-scatter.4.cloned.1.call-start = ((), (), s32[]{:S(2)}) async-start(), calls=%async_computation.6 | async-start | bytes 9830400 | tf_op jit(solution)/shard_map/reduce_scatter | solution.py:388
  385.5 277.1 %reduce-scatter.8.cloned.1.call-start = ((), (), s32[]{:S(2)}) async-start(), calls=%async_computation.8 | async-start | bytes 3276800 | tf_op jit(solution)/shard_map/reduce_scatter | solution.py:388
  387.5 14.9 %collective-permute-start.24 = (bf16[128,2048]{1,0:T(8,128)(2,1)S(1)}, bf16[128,2048]{1,0:T(8,128)(2,1)S(1)}, u32[]{:S(2)}, u32[]{:S(2)}) collective-permute-start(bf16[128,2048]{1,0:T(8,128)(2,1)S(1)} %get-tuple-element.152), channel_id=1, source_target_pairs={{0,1},{1,0},{2,3},{3,2},{4,5},{5,4},{6,7},{7,6},{8,9},{9,8},{10,11... | collective-permute-start | bytes 1572872 | tf_op jit(solution)/shard_map/ppermute | solution.py:315
  389.1 14.8 %collective-permute-start.25 = (bf16[128,2048]{1,0:T(8,128)(2,1)S(1)}, bf16[128,2048]{1,0:T(8,128)(2,1)S(1)}, u32[]{:S(2)}, u32[]{:S(2)}) collective-permute-start(bf16[128,2048]{1,0:T(8,128)(2,1)S(1)} %get-tuple-element.151), channel_id=1, source_target_pairs={{0,2},{1,3},{2,0},{3,1},{4,6},{5,7},{6,4},{7,5},{8,10},{9,11},{10,... | collective-permute-start | bytes 1572872 | tf_op jit(solution)/shard_map/ppermute | solution.py:315
  390.5 23.1 %collective-permute-start.23 = (bf16[128,2048]{1,0:T(8,128)(2,1)S(1)}, bf16[128,2048]{1,0:T(8,128)(2,1)S(1)}, u32[]{:S(2)}, u32[]{:S(2)}) collective-permute-start(bf16[128,2048]{1,0:T(8,128)(2,1)S(1)} %get-tuple-element.149), channel_id=1, source_target_pairs={{0,1},{1,0},{2,3},{3,2},{4,5},{5,4},{6,7},{7,6},{8,9},{9,8},{10,11... | collective-permute-start | bytes 1572872 | tf_op jit(solution)/shard_map/ppermute | solution.py:315
  391.1 24.0 %collective-permute-start.27 = (bf16[128,2048]{1,0:T(8,128)(2,1)S(1)}, bf16[128,2048]{1,0:T(8,128)(2,1)S(1)}, u32[]{:S(2)}, u32[]{:S(2)}) collective-permute-start(bf16[128,2048]{1,0:T(8,128)(2,1)S(1)} %get-tuple-element.150), channel_id=1, source_target_pairs={{0,2},{1,3},{2,0},{3,1},{4,6},{5,7},{6,4},{7,5},{8,10},{9,11},{10,... | collective-permute-start | bytes 1572872 | tf_op jit(solution)/shard_map/ppermute | solution.py:315
  405.5 19.8 %collective-permute-start.26 = (bf16[128,2048]{1,0:T(8,128)(2,1)S(1)}, bf16[128,2048]{1,0:T(8,128)(2,1)S(1)}, u32[]{:S(2)}, u32[]{:S(2)}) collective-permute-start(bf16[128,2048]{1,0:T(8,128)(2,1)S(1)} %get-tuple-element.56), channel_id=1, source_target_pairs={{0,2},{1,3},{2,0},{3,1},{4,6},{5,7},{6,4},{7,5},{8,10},{9,11},{10,... | collective-permute-start | bytes 1572872 | tf_op jit(solution)/shard_map/ppermute | solution.py:315
  407.0 18.2 %collective-permute-start.28 = (bf16[128,2048]{1,0:T(8,128)(2,1)S(1)}, bf16[128,2048]{1,0:T(8,128)(2,1)S(1)}, u32[]{:S(2)}, u32[]{:S(2)}) collective-permute-start(bf16[128,2048]{1,0:T(8,128)(2,1)S(1)} %get-tuple-element.57), channel_id=1, source_target_pairs={{0,1},{1,0},{2,3},{3,2},{4,5},{5,4},{6,7},{7,6},{8,9},{9,8},{10,11... | collective-permute-start | bytes 1572872 | tf_op jit(solution)/shard_map/ppermute | solution.py:315
  429.7 24.2 %collective-permute-start.29 = (bf16[256,2048]{1,0:T(8,128)(2,1)S(1)}, bf16[256,2048]{1,0:T(8,128)(2,1)S(1)}, u32[]{:S(2)}, u32[]{:S(2)}) collective-permute-start(bf16[256,2048]{1,0:T(8,128)(2,1)S(1)} %get-tuple-element.58), channel_id=1, source_target_pairs={{0,1},{1,0},{2,3},{3,2},{4,5},{5,4},{6,7},{7,6},{8,9},{9,8},{10,11... | collective-permute-start | bytes 3145736 | tf_op jit(solution)/shard_map/ppermute | solution.py:285
  430.3 25.8 %collective-permute-start.30 = (bf16[256,2048]{1,0:T(8,128)(2,1)S(1)}, bf16[256,2048]{1,0:T(8,128)(2,1)S(1)}, u32[]{:S(2)}, u32[]{:S(2)}) collective-permute-start(bf16[256,2048]{1,0:T(8,128)(2,1)S(1)} %get-tuple-element.58), channel_id=1, source_target_pairs={{0,2},{1,3},{2,0},{3,1},{4,6},{5,7},{6,4},{7,5},{8,10},{9,11},{10,... | collective-permute-start | bytes 3145736 | tf_op jit(solution)/shard_map/ppermute | solution.py:286
  453.9 12.2 %collective-permute-start.31 = (bf16[128,2048]{1,0:T(8,128)(2,1)S(1)}, bf16[128,2048]{1,0:T(8,128)(2,1)S(1)}, u32[]{:S(2)}, u32[]{:S(2)}) collective-permute-start(bf16[128,2048]{1,0:T(8,128)(2,1)S(1)} %slice.168), channel_id=1, source_target_pairs={{0,2},{1,3},{2,0},{3,1},{4,6},{5,7},{6,4},{7,5},{8,10},{9,11},{10,... | collective-permute-start | bytes 1572872 | tf_op jit(solution)/shard_map/ppermute | solution.py:287
  456.2 12.0 %collective-permute-start.32 = (bf16[128,2048]{1,0:T(8,128)(2,1)S(1)}, bf16[128,2048]{1,0:T(8,128)(2,1)S(1)}, u32[]{:S(2)}, u32[]{:S(2)}) collective-permute-start(bf16[128,2048]{1,0:T(8,128)(2,1)S(1)} %slice.169), channel_id=1, source_target_pairs={{0,1},{1,0},{2,3},{3,2},{4,5},{5,4},{6,7},{7,6},{8,9},{9,8},{10,11... | collective-permute-start | bytes 1572872 | tf_op jit(solution)/shard_map/ppermute | solution.py:288
  472.2 52.1 %collective-permute-start.50 = (bf16[1024,512]{1,0:T(8,128)(2,1)}, bf16[1024,512]{1,0:T(8,128)(2,1)}, u32[]{:S(2)}, u32[]{:S(2)}) collective-permute-start(bf16[1024,512]{1,0:T(8,128)(2,1)} %fusion.74), channel_id=1, source_target_pairs={{0,4},{4,0},{8,12},{12,8},{16,20},{20,16},{24,28},{28,24},{1,5},{5... | collective-permute-start | bytes 3145736 | tf_op jit(solution)/shard_map/ppermute | solution.py:380
  506.9 14.9 %collective-permute-start.37 = (bf16[128,2048]{1,0:T(8,128)(2,1)S(1)}, bf16[128,2048]{1,0:T(8,128)(2,1)S(1)}, u32[]{:S(2)}, u32[]{:S(2)}) collective-permute-start(bf16[128,2048]{1,0:T(8,128)(2,1)S(1)} %get-tuple-element.141), channel_id=1, source_target_pairs={{0,1},{1,0},{2,3},{3,2},{4,5},{5,4},{6,7},{7,6},{8,9},{9,8},{10,11... | collective-permute-start | bytes 1572872 | tf_op jit(solution)/shard_map/ppermute | solution.py:315
  507.7 14.7 %collective-permute-start.38 = (bf16[128,2048]{1,0:T(8,128)(2,1)S(1)}, bf16[128,2048]{1,0:T(8,128)(2,1)S(1)}, u32[]{:S(2)}, u32[]{:S(2)}) collective-permute-start(bf16[128,2048]{1,0:T(8,128)(2,1)S(1)} %get-tuple-element.140), channel_id=1, source_target_pairs={{0,2},{1,3},{2,0},{3,1},{4,6},{5,7},{6,4},{7,5},{8,10},{9,11},{10,... | collective-permute-start | bytes 1572872 | tf_op jit(solution)/shard_map/ppermute | solution.py:315
  510.6 61.3 %collective-permute-start.49 = (bf16[1024,768]{1,0:T(8,128)(2,1)S(1)}, bf16[1024,768]{1,0:T(8,128)(2,1)S(1)}, u32[]{:S(2)}, u32[]{:S(2)}) collective-permute-start(bf16[1024,768]{1,0:T(8,128)(2,1)S(1)} %fusion.69), channel_id=1, source_target_pairs={{0,4},{4,0},{8,12},{12,8},{16,20},{20,16},{24,28},{28,24},{1,5},{5... | collective-permute-start | bytes 4718600 | tf_op jit(solution)/shard_map/ppermute | solution.py:380
  511.1 21.9 %collective-permute-start.36 = (bf16[128,2048]{1,0:T(8,128)(2,1)S(1)}, bf16[128,2048]{1,0:T(8,128)(2,1)S(1)}, u32[]{:S(2)}, u32[]{:S(2)}) collective-permute-start(bf16[128,2048]{1,0:T(8,128)(2,1)S(1)} %get-tuple-element.138), channel_id=1, source_target_pairs={{0,1},{1,0},{2,3},{3,2},{4,5},{5,4},{6,7},{7,6},{8,9},{9,8},{10,11... | collective-permute-start | bytes 1572872 | tf_op jit(solution)/shard_map/ppermute | solution.py:315
  521.8 14.8 %collective-permute-start.40 = (bf16[128,2048]{1,0:T(8,128)(2,1)S(1)}, bf16[128,2048]{1,0:T(8,128)(2,1)S(1)}, u32[]{:S(2)}, u32[]{:S(2)}) collective-permute-start(bf16[128,2048]{1,0:T(8,128)(2,1)S(1)} %get-tuple-element.139), channel_id=1, source_target_pairs={{0,2},{1,3},{2,0},{3,1},{4,6},{5,7},{6,4},{7,5},{8,10},{9,11},{10,... | collective-permute-start | bytes 1572872 | tf_op jit(solution)/shard_map/ppermute | solution.py:315
  522.9 45.6 %collective-permute-start.39 = (bf16[128,2048]{1,0:T(8,128)(2,1)S(1)}, bf16[128,2048]{1,0:T(8,128)(2,1)S(1)}, u32[]{:S(2)}, u32[]{:S(2)}) collective-permute-start(bf16[128,2048]{1,0:T(8,128)(2,1)S(1)} %get-tuple-element.65), channel_id=1, source_target_pairs={{0,2},{1,3},{2,0},{3,1},{4,6},{5,7},{6,4},{7,5},{8,10},{9,11},{10,... | collective-permute-start | bytes 1572872 | tf_op jit(solution)/shard_map/ppermute | solution.py:315
  524.3 45.8 %collective-permute-start.41 = (bf16[128,2048]{1,0:T(8,128)(2,1)S(1)}, bf16[128,2048]{1,0:T(8,128)(2,1)S(1)}, u32[]{:S(2)}, u32[]{:S(2)}) collective-permute-start(bf16[128,2048]{1,0:T(8,128)(2,1)S(1)} %get-tuple-element.66), channel_id=1, source_target_pairs={{0,1},{1,0},{2,3},{3,2},{4,5},{5,4},{6,7},{7,6},{8,9},{9,8},{10,11... | collective-permute-start | bytes 1572872 | tf_op jit(solution)/shard_map/ppermute | solution.py:315
  533.0 84.3 %collective-permute-start.33 = (bf16[256,2048]{1,0:T(8,128)(2,1)}, bf16[256,2048]{1,0:T(8,128)(2,1)}, u32[]{:S(2)}, u32[]{:S(2)}) collective-permute-start(bf16[256,2048]{1,0:T(8,128)(2,1)} %get-tuple-element.144), channel_id=1, source_target_pairs={{0,3},{1,2},{2,1},{3,0},{4,7},{5,6},{6,5},{7,4},{8,11},{9,10},{10,... | collective-permute-start | bytes 3145736 | tf_op jit(solution)/shard_map/ppermute | solution.py:337
  536.6 80.8 %collective-permute-start.34 = (bf16[256,2048]{1,0:T(8,128)(2,1)}, bf16[256,2048]{1,0:T(8,128)(2,1)}, u32[]{:S(2)}, u32[]{:S(2)}) collective-permute-start(bf16[256,2048]{1,0:T(8,128)(2,1)} %get-tuple-element.146), channel_id=1, source_target_pairs={{0,1},{1,0},{2,3},{3,2},{4,5},{5,4},{6,7},{7,6},{8,9},{9,8},{10,11... | collective-permute-start | bytes 3145736 | tf_op jit(solution)/shard_map/ppermute | solution.py:337
  568.5 48.9 %collective-permute-start.35 = (bf16[256,2048]{1,0:T(8,128)(2,1)}, bf16[256,2048]{1,0:T(8,128)(2,1)}, u32[]{:S(2)}, u32[]{:S(2)}) collective-permute-start(bf16[256,2048]{1,0:T(8,128)(2,1)} %get-tuple-element.145), channel_id=1, source_target_pairs={{0,2},{1,3},{2,0},{3,1},{4,6},{5,7},{6,4},{7,5},{8,10},{9,11},{10,... | collective-permute-start | bytes 3145736 | tf_op jit(solution)/shard_map/ppermute | solution.py:337
  625.5 38.3 %collective-permute-start.46 = (f32[2,2048]{1,0:T(2,128)S(1)}, f32[2,2048]{1,0:T(2,128)S(1)}, u32[]{:S(2)}, u32[]{:S(2)}) collective-permute-start(f32[2,2048]{1,0:T(2,128)S(1)} %fusion.128), channel_id=1, source_target_pairs={{0,4},{4,0},{8,12},{12,8},{16,20},{20,16},{24,28},{28,24},{1,5},{5... | collective-permute-start | bytes 49160 | tf_op jit(solution)/shard_map/ppermute | solution.py:402
  (97 other events, 1274.5 us)
Sparse Core Ops, SparseCore 0:
  10.5 59.3 all-gather.3
  72.1 141.0 all-gather.5
  215.5 88.8 all-gather.7
  385.0 83.5 reduce-scatter.5
  470.8 136.7 reduce-scatter.3
  609.8 52.7 reduce-scatter.7

commit v6 on v5

--- a/solution.py
+++ b/solution.py
@@ -342,6 +342,28 @@
 def paired():
     count = lax.axis_size("dp")
     return count > 2 and count % 2 == 0
+
+
+def line_gather(block):
+    if not paired():
+        return lax.all_gather(block, "dp", axis=0, tiled=True)
+    count = lax.axis_size("dp")
+    lines = count // 2
+    line, core = lax.axis_index("dp") // 2, lax.axis_index("dp") % 2
+    rows, width = block.shape
+    lower, upper = [], []
+    low = high = block
+    for step in range(lines - 1):
+        low = lax.ppermute(low, "dp", [(i, i + 2) for i in range(2 * step, count - 2)])
+        high = lax.ppermute(high, "dp", [(i, i - 2) for i in range(2, count - 2 * step)])
+        lower.append(low)
+        upper.append(high)
+    around = jnp.concatenate(lower[::-1] + [block] + upper, axis=0)
+    mine = lax.dynamic_slice_in_dim(around, (lines - 1 - line) * rows, lines * rows, 0)
+    other = lax.ppermute(mine, "dp", shift_pairs(count, 1))
+    mine, other = mine.reshape(lines, 1, rows, width), other.reshape(lines, 1, rows, width)
+    even, odd = jnp.where(core == 0, mine, other), jnp.where(core == 0, other, mine)
+    return row_major(jnp.concatenate([even, odd], axis=1).reshape(count * rows, width))
 
 
 def row_major(value):
@@ -468,16 +490,18 @@
     hidden_units = w_gate.shape[1]
     cut = max(128, hidden_units * 5 // 8 // 128 * 128)
     down_turned = w_down.T
+    first, second = slice(0, cut), slice(cut, hidden_units)
     halves = [
-        lax.all_gather(
-            row_major(
-                jnp.concatenate([w_gate[:, part], w_up[:, part], down_turned[:, part]], axis=1)
-            ),
-            "dp",
-            axis=0,
-            tiled=True,
+        lax.all_gather(row_major(jnp.concatenate(parts, axis=1)), "dp", axis=0, tiled=True)
+        for parts in (
+            [w_gate[:, first], w_up[:, first], down_turned[:, first]],
+            [w_gate[:, second], w_up[:, second]],
         )
-        for part in (slice(0, cut), slice(cut, hidden_units))
+    ]
+    last_down = line_gather(row_major(down_turned[:, second]))
+    halves = [
+        (halves[0][:, : 2 * cut], halves[0][:, 2 * cut :]),
+        (halves[1], last_down),
     ]
 
     grad_out = out_grad.astype(jnp.float32)
@@ -501,8 +525,7 @@
     normed_total = first_act = None
     weight_grads = []
     for number, weights in enumerate(halves):
-        pair_cols = 2 * (weights.shape[1] // 3)
-        pair_weights, down_weights = weights[:, :pair_cols], weights[:, pair_cols:]
+        pair_weights, down_weights = weights
         pair_pre = product(normed_two_all, pair_weights)
         grad_act = product(grad_mlp_all, down_weights)
         activation, grad_pair = activation_both(pair_pre, grad_act)

time: 690 us -> 715 us (1.036)
  local copies, waits for them, and re-layouts: 50.2 us -> 60.7 us
    ppermute x4, waiting for transfers between devices: 16.8 us -> 40.1 us  [gather_rows(): far_top = lax.ppermute(from_x[:half], axis, shift_pairs(count, 2))]
    ppermute x0 -> x7, waiting for transfers between devices: none -> 20.4 us  [the longest x3 16.9 us: line_gather(): lax.ppermute(high, 'dp', [(i, i - 2) for i in range(2, count - 2 * step)])]
    ppermute x4, waiting for transfers between devices: 46 us -> 30.2 us  [gather_rows(): from_x = lax.ppermute(block, axis, shift_pairs(count, 1))]
    ppermute x4, waiting for transfers between devices: 21.1 us -> 6.07 us  [gather_rows(): far_low = lax.ppermute(from_y[half:], axis, shift_pairs(count, 1))]
    unnamed x178 -> x196, local copies, waits for them, and re-layouts: 18.2 us -> 27.5 us
    ppermute x6, waiting for transfers between devices: 14.5 us -> 5.38 us  [weight_sums(): got = lax.ppermute(sent, 'dp', shift_pairs(count, 1))]
    ppermute x0 -> x7, starting transfers between devices: none -> 9.03 us  [the longest x3 4.98 us: line_gather(): lax.ppermute(low, 'dp', [(i, i + 2) for i in range(2 * step, count - 2)])]
  transfers between devices with their start and end apart: 57 -> 64, of which waited for: 33 -> 34; matrix products, arithmetic and copies ran while one was open for 31% -> 34% of each run, Pallas kernels for 9% -> 8%
where the time goes in v6:
time: 715 us; the launch traced here: 708 us
  waiting for transfers between devices  277 us (39%)
  matrix products  162 us (23%)
  other arithmetic  67.9 us (9%)
  Pallas kernels  64.7 us (9%)
  local copies, waits for them, and re-layouts  60.7 us (8%)
  starting transfers between devices  59.6 us (8%)
  between operations  15.9 us (2%)
    dot_general x20, matrix products, contract(): lax.dot_general(left, right, (((left_axis,), (right_axis,)), ((), ())), p...  117 us
    ppermute x18, waiting for transfers between devices, send(): return lax.ppermute(piece, axis, shift_pairs(count, mask))  99.5 us
    reduce_scatter x3, waiting for transfers between devices, sum_shards(): lax.psum_scatter(partial, 'dp', scatter_dimension=0, tiled=True, axis_ind...  61.1 us
    dot_general x4, matrix products, product(): return jnp.dot(left, right, preferred_element_type=jnp.float32)  44.9 us
    ppermute x4, waiting for transfers between devices, gather_rows(): far_top = lax.ppermute(from_x[:half], axis, shift_pairs(count, 2))  40.1 us
    ppermute x4, waiting for transfers between devices, gather_rows(): from_x = lax.ppermute(block, axis, shift_pairs(count, 1))  30.2 us
    unnamed x196, local copies, waits for them, and re-layouts  27.5 us
    pallas_call x1, Pallas kernels, attend(): pl.pallas_call(functools.partial(attend_kernel, heads, kv_heads, block),...  25.5 us
  transfers between devices with their start and end apart: 64, of which 34 were waited for; matrix products, arithmetic and copies ran while one was open for 34% of the time, Pallas kernels for 8%

profile of v6, /device:TPU:0, one launch (start us, length us, event | category | flops | bytes accessed | tf_op | source)
XLA Modules:
  0.0 707.9 jit_solution(13582037694190643476)
XLA Ops:
  32.2 7.5 %collective-permute-done = bf16[256,2048]{1,0:T(8,128)(2,1)S(1)} collective-permute-done((bf16[256,2048]{1,0:T(8,128)(2,1)S(1)}, bf16[256,2048]{1,0:T(8,128)(2,1)S(1)}, u32[]{:S(2)}, u32[]{:S(2)}) %collective-permute-start) | collective-permute-done | bytes 1048608 | tf_op jit(solution)/shard_map/ppermute | solution.py:285
  47.6 5.4 collective-permute-done.2
  59.4 5.2 fusion.6
  64.5 5.2 all-gather.4.cloned.1.call-done
  69.8 8.3 %fusion.18.joint_ref = f32[768,1024]{1,0:T(8,128)} fusion(bf16[1024,2048]{1,0:T(8,128)(2,1)} %fusion.6, bf16[2048,1280]{1,0:T(8,128)(2,1)} %all-gather.4.cloned.1.call-done), kind=kOutput, calls=%fused_computation.36 | convolution fusion | flops 3221225472 | bytes 10485760 | tf_op jit(solution)/shard_map/dot_general | solution.py:434
  78.1 25.5 %attend.1 = (bf16[768,1024]{1,0:T(8,128)(2,1)}, bf16[512,1024]{1,0:T(8,128)(2,1)}, f32[8,1024]{1,0:T(8,128)}) custom-call(f32[768,1024]{1,0:T(8,128)} %fusion.18.joint_ref, f32[32,1024]{1,0:T(8,128)} %get-tuple-element.191.cos_ref, f32[32,1024]{1,0:T(8,128)} %get-tuple-element.190.sin_ref, s32[1,1024]{1,0:T(1,128)} %bitcast.75, s32[1024,1]{1,0:T(8,128)} %copy.44.seg_col_ref), custom_call_target="tpu_custom_call" | custom-call | flops 8589934592 | bytes 6291456 | tf_op jit(solution)/shard_map/attend/pallas_call | solution.py:232
  103.6 4.3 convolution_convert_fusion.1
  115.5 11.0 %collective-permute-done.8 = bf16[128,2048]{1,0:T(8,128)(2,1)} collective-permute-done((bf16[128,2048]{1,0:T(8,128)(2,1)}, bf16[128,2048]{1,0:T(8,128)(2,1)}, u32[]{:S(2)}, u32[]{:S(2)}) %collective-permute-start.8) | collective-permute-done | bytes 524320 | tf_op jit(solution)/shard_map/ppermute | solution.py:315
  142.8 7.6 %collective-permute-done.10 = bf16[128,2048]{1,0:T(8,128)(2,1)} collective-permute-done((bf16[128,2048]{1,0:T(8,128)(2,1)}, bf16[128,2048]{1,0:T(8,128)(2,1)}, u32[]{:S(2)}, u32[]{:S(2)}) %collective-permute-start.10) | collective-permute-done | bytes 524320 | tf_op jit(solution)/shard_map/ppermute | solution.py:315
  158.8 12.5 %collective-permute-done.17 = bf16[256,2048]{1,0:T(8,128)(2,1)S(1)} collective-permute-done((bf16[256,2048]{1,0:T(8,128)(2,1)}, bf16[256,2048]{1,0:T(8,128)(2,1)S(1)}, u32[]{:S(2)}, u32[]{:S(2)}) %collective-permute-start.17) | collective-permute-done | bytes 1048608 | tf_op jit(solution)/shard_map/ppermute | solution.py:285
  176.7 4.8 collective-permute-done.26
  187.2 19.4 %collective-permute-done.19 = bf16[128,2048]{1,0:T(8,128)(2,1)} collective-permute-done((bf16[128,2048]{1,0:T(8,128)(2,1)}, bf16[128,2048]{1,0:T(8,128)(2,1)}, u32[]{:S(2)}, u32[]{:S(2)}) %collective-permute-start.19) | collective-permute-done | bytes 524320 | tf_op jit(solution)/shard_map/ppermute | solution.py:287
  216.7 5.1 collective-permute-done.15
  230.1 18.4 %fusion.2.pair_ref = f32[1024,2560]{1,0:T(8,128)} fusion(bf16[1024,2048]{1,0:T(8,128)(2,1)} %copy-done.14, bf16[2048,3840]{1,0:T(8,128)(2,1)} %all-gather.6.cloned.1.call-done), kind=kOutput, calls=%fused_computation.5 | convolution fusion | flops 10737418240 | bytes 25165824 | tf_op jit(solution)/shard_map/dot_general | solution.py:430
  248.5 9.8 %fusion.9.grad_ref = f32[1024,1280]{1,0:T(8,128)} fusion(bf16[1024,2048]{1,0:T(8,128)(2,1)S(1)} %copy-done.11, bf16[2048,3840]{1,0:T(8,128)(2,1)} %all-gather.6.cloned.1.call-done), kind=kOutput, calls=%fused_computation.19 | convolution fusion | flops 5368709120 | bytes 14680064 | tf_op jit(solution)/shard_map/dot_general | solution.py:430
  258.3 9.1 %activation_both.2 = (bf16[1024,1280]{1,0:T(8,128)(2,1)}, bf16[1024,2560]{1,0:T(8,128)(2,1)}) custom-call(f32[1024,2560]{1,0:T(8,128)} %fusion.2.pair_ref, f32[1024,1280]{1,0:T(8,128)} %fusion.9.grad_ref), custom_call_target="tpu_custom_call" | custom-call | flops 52428800 | bytes 23592960 | tf_op jit(solution)/shard_map/activation_both/pallas_call | solution.py:209
  267.4 9.8 %convolution_convert_fusion = bf16[1024,2560]{1,0:T(8,128)(2,1)} fusion(bf16[1024,2560]{1,0:T(8,128)(2,1)} %get-tuple-element.47, bf16[1024,256]{1,0:T(8,128)(2,1)} %get-tuple-element.200, bf16[1024,256]{1,0:T(8,128)(2,1)} %get-tuple-element.199, bf16[1024,256]{1,0:T(8,128)(2,1)} %get-tuple-element.198, bf16[1024,256]{1,0:T(8,128)(2,1)} %get-tuple-element.197), kind=kOutput, calls=%fused_computation.14 | convolution fusion | flops 5379719168 | bytes 12582912 | tf_op jit(solution)/shard_map/dot_general | solution.py:434
  282.9 4.9 convolution_convert_fusion.4
  289.4 12.1 %collective-permute-done.28 = bf16[256,768]{1,0:T(8,128)(2,1)S(1)} collective-permute-done((bf16[256,768]{1,0:T(8,128)(2,1)}, bf16[256,768]{1,0:T(8,128)(2,1)S(1)}, u32[]{:S(2)}, u32[]{:S(2)}) %collective-permute-start.28) | collective-permute-done | bytes 393248 | tf_op jit(solution)/shard_map/ppermute | solution.py:358
  303.3 3.5 collective-permute-done.29
  311.2 6.7 add_convert_fusion.4
  317.9 9.4 %add_convert_fusion = bf16[1024,2560]{1,0:T(8,128)(2,1)} fusion(bf16[1024,2560]{1,0:T(8,128)(2,1)} %collective-permute-done.21, bf16[1024,2560]{1,0:T(8,128)(2,1)S(1)} %bitcast.83, bf16[1024,256]{1,0:T(8,128)(2,1)S(1)} %copy-done.32, bf16[1024,256]{1,0:T(8,128)(2,1)S(1)} %copy-done.30, bf16[1024,256]{1,0:T(8,128)(2,1)S(1)} %copy-done.28, ...), kind=kOutput, calls=%fused_computation.2 | convolution fusion | flops 5384962048 | bytes 17825792 | tf_op jit(solution)/shard_map/dot_general | solution.py:434
  327.3 7.0 pad_maximum_fusion
  334.4 17.1 %fusion.11 = bf16[1024,2048]{1,0:T(8,128)(2,1)} fusion(bf16[1024,2560]{1,0:T(8,128)(2,1)} %get-tuple-element.47, bf16[2048,3840]{1,0:T(8,128)(2,1)} %all-gather.6.cloned.1.call-done), kind=kOutput, calls=%fused_computation.25 | convolution fusion | flops 10739515392 | bytes 19922944 | tf_op jit(solution)/shard_map/dot_general | solution.py:434
  351.4 5.1 fusion.98.grad_ref
  356.5 11.7 %fusion.97.pair_ref = f32[1024,1536]{1,0:T(8,128)} fusion(bf16[1024,2048]{1,0:T(8,128)(2,1)} %copy-done.14, bf16[2048,1536]{1,0:T(8,128)(2,1)} %all-gather.8.cloned.1.call-done), kind=kOutput, calls=%fused_computation.234 | convolution fusion | flops 6442450944 | bytes 16777216 | tf_op jit(solution)/shard_map/dot_general | solution.py:430
  368.2 6.4 activation_both.3
  374.7 10.1 %fusion.99 = f32[1024,2048]{1,0:T(8,128)S(1)} fusion(bf16[1024,1536]{1,0:T(8,128)(2,1)} %get-tuple-element.68, bf16[2048,1536]{1,0:T(8,128)(2,1)} %all-gather.8.cloned.1.call-done), kind=kOutput, calls=%fused_computation.236 | convolution fusion | flops 6442450944 | bytes 17825792 | tf_op jit(solution)/shard_map/dot_general | solution.py:434
  384.8 3.6 add_convert_fusion.2
  388.5 5.7 convolution_convert_fusion.2
  396.8 5.4 collective-permute-done.50
  404.2 4.0 add_convert_fusion.3
  417.4 10.7 %collective-permute-done.31 = bf16[128,2048]{1,0:T(8,128)(2,1)S(1)} collective-permute-done((bf16[128,2048]{1,0:T(8,128)(2,1)S(1)}, bf16[128,2048]{1,0:T(8,128)(2,1)S(1)}, u32[]{:S(2)}, u32[]{:S(2)}) %collective-permute-start.31) | collective-permute-done | bytes 524320 | tf_op jit(solution)/shard_map/ppermute | solution.py:315
  433.9 5.6 collective-permute-done.30
  440.9 10.2 %collective-permute-done.33 = bf16[128,2048]{1,0:T(8,128)(2,1)S(1)} collective-permute-done((bf16[128,2048]{1,0:T(8,128)(2,1)S(1)}, bf16[128,2048]{1,0:T(8,128)(2,1)S(1)}, u32[]{:S(2)}, u32[]{:S(2)}) %collective-permute-start.33) | collective-permute-done | bytes 524320 | tf_op jit(solution)/shard_map/ppermute | solution.py:315
  457.0 8.1 %fusion.7 = f32[1024,2048]{1,0:T(8,128)S(1)} fusion(bf16[1024,1280]{1,0:T(8,128)(2,1)S(1)} %copy-done.80, bf16[2048,3840]{1,0:T(8,128)(2,1)} %all-gather.6.cloned.1.call-done), kind=kOutput, calls=%fused_computation.17 | convolution fusion | flops 5368709120 | bytes 16252928 | tf_op jit(solution)/shard_map/dot_general | solution.py:434
  465.2 5.1 add_convert_fusion.1
  470.2 10.1 %collective-permute-done.36 = bf16[256,2048]{1,0:T(8,128)(2,1)S(1)} collective-permute-done((bf16[256,2048]{1,0:T(8,128)(2,1)S(1)}, bf16[256,2048]{1,0:T(8,128)(2,1)S(1)}, u32[]{:S(2)}, u32[]{:S(2)}) %collective-permute-start.36) | collective-permute-done | bytes 1048608 | tf_op jit(solution)/shard_map/ppermute | solution.py:285
  482.5 10.2 %collective-permute-done.38 = bf16[128,2048]{1,0:T(8,128)(2,1)S(1)} collective-permute-done((bf16[128,2048]{1,0:T(8,128)(2,1)S(1)}, bf16[128,2048]{1,0:T(8,128)(2,1)S(1)}, u32[]{:S(2)}, u32[]{:S(2)}) %collective-permute-start.38) | collective-permute-done | bytes 524320 | tf_op jit(solution)/shard_map/ppermute | solution.py:287
  498.1 5.0 fusion.70.out_ref
  503.1 23.6 %attend_back.1 = bf16[768,1024]{1,0:T(8,128)(2,1)} custom-call(bf16[768,1024]{1,0:T(8,128)(2,1)} %get-tuple-element.62.rot_ref, bf16[512,1024]{1,0:T(8,128)(2,1)} %get-tuple-element.42.att_ref, bf16[512,1024]{1,0:T(8,128)(2,1)} %fusion.70.out_ref, f32[8,1024]{1,0:T(8,128)} %get-tuple-element.64.log_ref, f32[32,1024]{1,0:T(8,128)} %get-tuple-element.191.cos_ref, ...), custom_call_target="tpu_custom_call" | custom-call | flops 21474836480 | bytes 6291456 | tf_op jit(solution)/shard_map/attend_back/pallas_call | solution.py:255
  526.7 5.9 convolution_convert_fusion.3
  538.4 9.3 %collective-permute-done.44 = bf16[128,2048]{1,0:T(8,128)(2,1)S(1)} collective-permute-done((bf16[128,2048]{1,0:T(8,128)(2,1)S(1)}, bf16[128,2048]{1,0:T(8,128)(2,1)S(1)}, u32[]{:S(2)}, u32[]{:S(2)}) %collective-permute-start.44) | collective-permute-done | bytes 524320 | tf_op jit(solution)/shard_map/ppermute | solution.py:315
  555.4 3.6 collective-permute-done.43
  562.6 31.9 %collective-permute-done.46 = bf16[128,2048]{1,0:T(8,128)(2,1)S(1)} collective-permute-done((bf16[128,2048]{1,0:T(8,128)(2,1)S(1)}, bf16[128,2048]{1,0:T(8,128)(2,1)S(1)}, u32[]{:S(2)}, u32[]{:S(2)}) %collective-permute-start.46) | collective-permute-done | bytes 524320 | tf_op jit(solution)/shard_map/ppermute | solution.py:315
  607.6 26.1 %reduce-scatter.4.cloned.1.call-done = bf16[256,3840]{1,0:T(8,128)(2,1)} async-done(((bf16[1024,3840]{1,0:T(8,128)(2,1)}), bf16[256,3840]{1,0:T(8,128)(2,1)}) %reduce-scatter.4.cloned.1.call-update) | async-done | bytes 1966096 | tf_op jit(solution)/shard_map/reduce_scatter | solution.py:410
  643.6 4.3 multiply_add_fusion
  653.8 35.0 %reduce-scatter.8.cloned.1.call-done = bf16[256,1280]{1,0:T(8,128)(2,1)} async-done(((bf16[1024,1280]{1,0:T(8,128)(2,1)}), bf16[256,1280]{1,0:T(8,128)(2,1)}) %reduce-scatter.8.cloned.1.call-update) | async-done | bytes 655376 | tf_op jit(solution)/shard_map/reduce_scatter | solution.py:410
  (418 shorter events, 205.6 us)
Async XLA Ops:
  7.2 62.6 %all-gather.4.cloned.1.call-start = ((), (), s32[]{:S(2)}) async-start(), calls=%async_computation.3 | async-start | bytes 5898240 | tf_op jit(solution)/shard_map/all_gather | solution.py:482
  10.3 219.8 %all-gather.6.cloned.1.call-start = ((), (), s32[]{:S(2)}) async-start(), calls=%async_computation.4 | async-start | bytes 17694720 | tf_op jit(solution)/shard_map/all_gather | solution.py:495
  13.5 343.1 %all-gather.8.cloned.1.call-start = ((), (), s32[]{:S(2)}) async-start(), calls=%async_computation.5 | async-start | bytes 7077888 | tf_op jit(solution)/shard_map/all_gather | solution.py:495
  13.5 26.2 %collective-permute-start = (bf16[256,2048]{1,0:T(8,128)(2,1)S(1)}, bf16[256,2048]{1,0:T(8,128)(2,1)S(1)}, u32[]{:S(2)}, u32[]{:S(2)}) collective-permute-start(bf16[256,2048]{1,0:T(8,128)(2,1)S(1)} %copy-done.2), channel_id=1, source_target_pairs={{0,1},{1,0},{2,3},{3,2},{4,5},{5,4},{6,7},{7,6},{8,9},{9,8},{10,11... | collective-permute-start | bytes 3145736 | tf_op jit(solution)/shard_map/ppermute | solution.py:285
  16.6 25.1 %collective-permute-start.1 = (bf16[256,2048]{1,0:T(8,128)(2,1)S(1)}, bf16[256,2048]{1,0:T(8,128)(2,1)}, u32[]{:S(2)}, u32[]{:S(2)}) collective-permute-start(bf16[256,2048]{1,0:T(8,128)(2,1)S(1)} %copy-done.2), channel_id=1, source_target_pairs={{0,2},{1,3},{2,0},{3,1},{4,6},{5,7},{6,4},{7,5},{8,10},{9,11},{10,... | collective-permute-start | bytes 3145736 | tf_op jit(solution)/shard_map/ppermute | solution.py:286
  39.8 13.3 %collective-permute-start.2 = (bf16[128,2048]{1,0:T(8,128)(2,1)S(1)}, bf16[128,2048]{1,0:T(8,128)(2,1)S(1)}, u32[]{:S(2)}, u32[]{:S(2)}) collective-permute-start(bf16[128,2048]{1,0:T(8,128)(2,1)S(1)} %slice.145), channel_id=1, source_target_pairs={{0,2},{1,3},{2,0},{3,1},{4,6},{5,7},{6,4},{7,5},{8,10},{9,11},{10,... | collective-permute-start | bytes 1572872 | tf_op jit(solution)/shard_map/ppermute | solution.py:287
  111.4 15.1 %collective-permute-start.8 = (bf16[128,2048]{1,0:T(8,128)(2,1)}, bf16[128,2048]{1,0:T(8,128)(2,1)}, u32[]{:S(2)}, u32[]{:S(2)}) collective-permute-start(bf16[128,2048]{1,0:T(8,128)(2,1)} %get-tuple-element.176), channel_id=1, source_target_pairs={{0,1},{1,0},{2,3},{3,2},{4,5},{5,4},{6,7},{7,6},{8,9},{9,8},{10,11... | collective-permute-start | bytes 1572872 | tf_op jit(solution)/shard_map/ppermute | solution.py:315
  112.9 15.1 %collective-permute-start.9 = (bf16[128,2048]{1,0:T(8,128)(2,1)}, bf16[128,2048]{1,0:T(8,128)(2,1)}, u32[]{:S(2)}, u32[]{:S(2)}) collective-permute-start(bf16[128,2048]{1,0:T(8,128)(2,1)} %get-tuple-element.175), channel_id=1, source_target_pairs={{0,2},{1,3},{2,0},{3,1},{4,6},{5,7},{6,4},{7,5},{8,10},{9,11},{10,... | collective-permute-start | bytes 1572872 | tf_op jit(solution)/shard_map/ppermute | solution.py:315
  114.4 24.8 %collective-permute-start.11 = (bf16[128,2048]{1,0:T(8,128)(2,1)}, bf16[128,2048]{1,0:T(8,128)(2,1)}, u32[]{:S(2)}, u32[]{:S(2)}) collective-permute-start(bf16[128,2048]{1,0:T(8,128)(2,1)} %get-tuple-element.174), channel_id=1, source_target_pairs={{0,2},{1,3},{2,0},{3,1},{4,6},{5,7},{6,4},{7,5},{8,10},{9,11},{10,... | collective-permute-start | bytes 1572872 | tf_op jit(solution)/shard_map/ppermute | solution.py:315
  115.0 25.7 %collective-permute-start.7 = (bf16[128,2048]{1,0:T(8,128)(2,1)}, bf16[128,2048]{1,0:T(8,128)(2,1)}, u32[]{:S(2)}, u32[]{:S(2)}) collective-permute-start(bf16[128,2048]{1,0:T(8,128)(2,1)} %get-tuple-element.173), channel_id=1, source_target_pairs={{0,1},{1,0},{2,3},{3,2},{4,5},{5,4},{6,7},{7,6},{8,9},{9,8},{10,11... | collective-permute-start | bytes 1572872 | tf_op jit(solution)/shard_map/ppermute | solution.py:315
  130.9 19.5 %collective-permute-start.10 = (bf16[128,2048]{1,0:T(8,128)(2,1)}, bf16[128,2048]{1,0:T(8,128)(2,1)}, u32[]{:S(2)}, u32[]{:S(2)}) collective-permute-start(bf16[128,2048]{1,0:T(8,128)(2,1)} %get-tuple-element.43), channel_id=1, source_target_pairs={{0,2},{1,3},{2,0},{3,1},{4,6},{5,7},{6,4},{7,5},{8,10},{9,11},{10,... | collective-permute-start | bytes 1572872 | tf_op jit(solution)/shard_map/ppermute | solution.py:315
  132.4 19.3 %collective-permute-start.12 = (bf16[128,2048]{1,0:T(8,128)(2,1)}, bf16[128,2048]{1,0:T(8,128)(2,1)}, u32[]{:S(2)}, u32[]{:S(2)}) collective-permute-start(bf16[128,2048]{1,0:T(8,128)(2,1)} %get-tuple-element.44), channel_id=1, source_target_pairs={{0,1},{1,0},{2,3},{3,2},{4,5},{5,4},{6,7},{7,6},{8,9},{9,8},{10,11... | collective-permute-start | bytes 1572872 | tf_op jit(solution)/shard_map/ppermute | solution.py:315
  134.6 36.8 %collective-permute-start.17 = (bf16[256,2048]{1,0:T(8,128)(2,1)}, bf16[256,2048]{1,0:T(8,128)(2,1)S(1)}, u32[]{:S(2)}, u32[]{:S(2)}) collective-permute-start(bf16[256,2048]{1,0:T(8,128)(2,1)} %get-tuple-element.115), channel_id=1, source_target_pairs={{0,1},{1,0},{2,3},{3,2},{4,5},{5,4},{6,7},{7,6},{8,9},{9,8},{10,11... | collective-permute-start | bytes 3145736 | tf_op jit(solution)/shard_map/ppermute | solution.py:285
  139.2 35.0 %collective-permute-start.18 = (bf16[256,2048]{1,0:T(8,128)(2,1)}, bf16[256,2048]{1,0:T(8,128)(2,1)}, u32[]{:S(2)}, u32[]{:S(2)}) collective-permute-start(bf16[256,2048]{1,0:T(8,128)(2,1)} %get-tuple-element.115), channel_id=1, source_target_pairs={{0,2},{1,3},{2,0},{3,1},{4,6},{5,7},{6,4},{7,5},{8,10},{9,11},{10,... | collective-permute-start | bytes 3145736 | tf_op jit(solution)/shard_map/ppermute | solution.py:286
  140.7 33.0 %collective-permute-start.23 = (bf16[256,768]{1,0:T(8,128)(2,1)}, bf16[256,768]{1,0:T(8,128)(2,1)}, u32[]{:S(2)}, u32[]{:S(2)}) collective-permute-start(bf16[256,768]{1,0:T(8,128)(2,1)} %slice.157), channel_id=1, source_target_pairs={{0,8},{4,12},{8,16},{12,20},{16,24},{20,28},{1,9},{5,13},{9,17},{1... | collective-permute-start | bytes 1179656 | tf_op jit(solution)/shard_map/ppermute | solution.py:357
  150.5 31.0 %collective-permute-start.26 = (bf16[256,768]{1,0:T(8,128)(2,1)}, bf16[256,768]{1,0:T(8,128)(2,1)S(1)}, u32[]{:S(2)}, u32[]{:S(2)}) collective-permute-start(bf16[256,768]{1,0:T(8,128)(2,1)} %slice.157), channel_id=1, source_target_pairs={{8,0},{12,4},{16,8},{20,12},{24,16},{28,20},{9,1},{13,5},{17,9},{2... | collective-permute-start | bytes 1179656 | tf_op jit(solution)/shard_map/ppermute | solution.py:358
  158.4 51.6 %collective-permute-start.13 = (bf16[256,2048]{1,0:T(8,128)(2,1)}, bf16[256,2048]{1,0:T(8,128)(2,1)S(1)}, u32[]{:S(2)}, u32[]{:S(2)}) collective-permute-start(bf16[256,2048]{1,0:T(8,128)(2,1)} %get-tuple-element.117), channel_id=1, source_target_pairs={{0,1},{1,0},{2,3},{3,2},{4,5},{5,4},{6,7},{7,6},{8,9},{9,8},{10,11... | collective-permute-start | bytes 3145736 | tf_op jit(solution)/shard_map/ppermute | solution.py:285
  171.3 41.1 %collective-permute-start.14 = (bf16[256,2048]{1,0:T(8,128)(2,1)}, bf16[256,2048]{1,0:T(8,128)(2,1)}, u32[]{:S(2)}, u32[]{:S(2)}) collective-permute-start(bf16[256,2048]{1,0:T(8,128)(2,1)} %get-tuple-element.117), channel_id=1, source_target_pairs={{0,2},{1,3},{2,0},{3,1},{4,6},{5,7},{6,4},{7,5},{8,10},{9,11},{10,... | collective-permute-start | bytes 3145736 | tf_op jit(solution)/shard_map/ppermute | solution.py:286
  173.7 33.0 %collective-permute-start.19 = (bf16[128,2048]{1,0:T(8,128)(2,1)}, bf16[128,2048]{1,0:T(8,128)(2,1)}, u32[]{:S(2)}, u32[]{:S(2)}) collective-permute-start(bf16[128,2048]{1,0:T(8,128)(2,1)} %slice.152), channel_id=1, source_target_pairs={{0,2},{1,3},{2,0},{3,1},{4,6},{5,7},{6,4},{7,5},{8,10},{9,11},{10,... | collective-permute-start | bytes 1572872 | tf_op jit(solution)/shard_map/ppermute | solution.py:287
  181.4 30.2 %collective-permute-start.20 = (bf16[128,2048]{1,0:T(8,128)(2,1)S(1)}, bf16[128,2048]{1,0:T(8,128)(2,1)S(1)}, u32[]{:S(2)}, u32[]{:S(2)}) collective-permute-start(bf16[128,2048]{1,0:T(8,128)(2,1)S(1)} %slice.153), channel_id=1, source_target_pairs={{0,1},{1,0},{2,3},{3,2},{4,5},{5,4},{6,7},{7,6},{8,9},{9,8},{10,11... | collective-permute-start | bytes 1572872 | tf_op jit(solution)/shard_map/ppermute | solution.py:288
  186.0 92.3 %collective-permute-start.27 = (bf16[256,768]{1,0:T(8,128)(2,1)S(1)}, bf16[256,768]{1,0:T(8,128)(2,1)}, u32[]{:S(2)}, u32[]{:S(2)}) collective-permute-start(bf16[256,768]{1,0:T(8,128)(2,1)S(1)} %collective-permute-done.26), channel_id=1, source_target_pairs={{8,0},{12,4},{16,8},{20,12},{9,1},{13,5},{17,9},{21,13},{10,2},{14... | collective-permute-start | bytes 1179656 | tf_op jit(solution)/shard_map/ppermute | solution.py:358
  206.7 73.0 %collective-permute-start.25 = (bf16[256,768]{1,0:T(8,128)(2,1)}, bf16[256,768]{1,0:T(8,128)(2,1)}, u32[]{:S(2)}, u32[]{:S(2)}) collective-permute-start(bf16[256,768]{1,0:T(8,128)(2,1)} %collective-permute-done.24), channel_id=1, source_target_pairs={{16,24},{20,28},{17,25},{21,29},{18,26},{22,30},{19,27},{23,31}} | collective-permute-start | bytes 1179656 | tf_op jit(solution)/shard_map/ppermute | solution.py:357
  277.2 40.7 %collective-permute-start.21 = (bf16[1024,2560]{1,0:T(8,128)(2,1)}, bf16[1024,2560]{1,0:T(8,128)(2,1)}, u32[]{:S(2)}, u32[]{:S(2)}) collective-permute-start(bf16[1024,2560]{1,0:T(8,128)(2,1)} %convolution_convert_fusion), channel_id=1, source_target_pairs={{0,4},{4,0},{8,12},{12,8},{16,20},{20,16},{24,28},{28,24},{1,5},{5... | collective-permute-start | bytes 15728648 | tf_op jit(solution)/shard_map/ppermute | solution.py:402
  278.2 325.7 %reduce-scatter.6.cloned.1.call-start = ((), (), s32[]{:S(2)}) async-start(), calls=%async_computation.7 | async-start | bytes 5898240 | tf_op jit(solution)/shard_map/reduce_scatter | solution.py:410
  278.3 23.2 %collective-permute-start.28 = (bf16[256,768]{1,0:T(8,128)(2,1)}, bf16[256,768]{1,0:T(8,128)(2,1)S(1)}, u32[]{:S(2)}, u32[]{:S(2)}) collective-permute-start(bf16[256,768]{1,0:T(8,128)(2,1)} %collective-permute-done.27), channel_id=1, source_target_pairs={{8,0},{12,4},{9,1},{13,5},{10,2},{14,6},{11,3},{15,7}} | collective-permute-start | bytes 1179656 | tf_op jit(solution)/shard_map/ppermute | solution.py:358
  287.8 21.5 %collective-permute-start.22 = (bf16[1024,1280]{1,0:T(8,128)(2,1)}, bf16[1024,1280]{1,0:T(8,128)(2,1)}, u32[]{:S(2)}, u32[]{:S(2)}) collective-permute-start(bf16[1024,1280]{1,0:T(8,128)(2,1)} %convolution_convert_fusion.4), channel_id=1, source_target_pairs={{0,4},{4,0},{8,12},{12,8},{16,20},{20,16},{24,28},{28,24},{1,5},{5... | collective-permute-start | bytes 7864328 | tf_op jit(solution)/shard_map/ppermute | solution.py:402
  410.8 223.0 %reduce-scatter.4.cloned.1.call-start = ((), (), s32[]{:S(2)}) async-start(), calls=%async_computation.6 | async-start | bytes 9830400 | tf_op jit(solution)/shard_map/reduce_scatter | solution.py:410
  411.4 277.4 %reduce-scatter.8.cloned.1.call-start = ((), (), s32[]{:S(2)}) async-start(), calls=%async_computation.8 | async-start | bytes 3276800 | tf_op jit(solution)/shard_map/reduce_scatter | solution.py:410
  413.3 14.9 %collective-permute-start.31 = (bf16[128,2048]{1,0:T(8,128)(2,1)S(1)}, bf16[128,2048]{1,0:T(8,128)(2,1)S(1)}, u32[]{:S(2)}, u32[]{:S(2)}) collective-permute-start(bf16[128,2048]{1,0:T(8,128)(2,1)S(1)} %get-tuple-element.152), channel_id=1, source_target_pairs={{0,1},{1,0},{2,3},{3,2},{4,5},{5,4},{6,7},{7,6},{8,9},{9,8},{10,11... | collective-permute-start | bytes 1572872 | tf_op jit(solution)/shard_map/ppermute | solution.py:315
  414.9 14.8 %collective-permute-start.32 = (bf16[128,2048]{1,0:T(8,128)(2,1)S(1)}, bf16[128,2048]{1,0:T(8,128)(2,1)S(1)}, u32[]{:S(2)}, u32[]{:S(2)}) collective-permute-start(bf16[128,2048]{1,0:T(8,128)(2,1)S(1)} %get-tuple-element.151), channel_id=1, source_target_pairs={{0,2},{1,3},{2,0},{3,1},{4,6},{5,7},{6,4},{7,5},{8,10},{9,11},{10,... | collective-permute-start | bytes 1572872 | tf_op jit(solution)/shard_map/ppermute | solution.py:315
  414.9 24.5 %collective-permute-start.30 = (bf16[128,2048]{1,0:T(8,128)(2,1)S(1)}, bf16[128,2048]{1,0:T(8,128)(2,1)S(1)}, u32[]{:S(2)}, u32[]{:S(2)}) collective-permute-start(bf16[128,2048]{1,0:T(8,128)(2,1)S(1)} %get-tuple-element.149), channel_id=1, source_target_pairs={{0,1},{1,0},{2,3},{3,2},{4,5},{5,4},{6,7},{7,6},{8,9},{9,8},{10,11... | collective-permute-start | bytes 1572872 | tf_op jit(solution)/shard_map/ppermute | solution.py:315
  415.4 25.5 %collective-permute-start.34 = (bf16[128,2048]{1,0:T(8,128)(2,1)S(1)}, bf16[128,2048]{1,0:T(8,128)(2,1)S(1)}, u32[]{:S(2)}, u32[]{:S(2)}) collective-permute-start(bf16[128,2048]{1,0:T(8,128)(2,1)S(1)} %get-tuple-element.150), channel_id=1, source_target_pairs={{0,2},{1,3},{2,0},{3,1},{4,6},{5,7},{6,4},{7,5},{8,10},{9,11},{10,... | collective-permute-start | bytes 1572872 | tf_op jit(solution)/shard_map/ppermute | solution.py:315
  431.3 19.8 %collective-permute-start.33 = (bf16[128,2048]{1,0:T(8,128)(2,1)S(1)}, bf16[128,2048]{1,0:T(8,128)(2,1)S(1)}, u32[]{:S(2)}, u32[]{:S(2)}) collective-permute-start(bf16[128,2048]{1,0:T(8,128)(2,1)S(1)} %get-tuple-element.56), channel_id=1, source_target_pairs={{0,2},{1,3},{2,0},{3,1},{4,6},{5,7},{6,4},{7,5},{8,10},{9,11},{10,... | collective-permute-start | bytes 1572872 | tf_op jit(solution)/shard_map/ppermute | solution.py:315
  431.3 19.7 %collective-permute-start.35 = (bf16[128,2048]{1,0:T(8,128)(2,1)S(1)}, bf16[128,2048]{1,0:T(8,128)(2,1)S(1)}, u32[]{:S(2)}, u32[]{:S(2)}) collective-permute-start(bf16[128,2048]{1,0:T(8,128)(2,1)S(1)} %get-tuple-element.57), channel_id=1, source_target_pairs={{0,1},{1,0},{2,3},{3,2},{4,5},{5,4},{6,7},{7,6},{8,9},{9,8},{10,11... | collective-permute-start | bytes 1572872 | tf_op jit(solution)/shard_map/ppermute | solution.py:315
  456.1 24.2 %collective-permute-start.36 = (bf16[256,2048]{1,0:T(8,128)(2,1)S(1)}, bf16[256,2048]{1,0:T(8,128)(2,1)S(1)}, u32[]{:S(2)}, u32[]{:S(2)}) collective-permute-start(bf16[256,2048]{1,0:T(8,128)(2,1)S(1)} %get-tuple-element.58), channel_id=1, source_target_pairs={{0,1},{1,0},{2,3},{3,2},{4,5},{5,4},{6,7},{7,6},{8,9},{9,8},{10,11... | collective-permute-start | bytes 3145736 | tf_op jit(solution)/shard_map/ppermute | solution.py:285
  456.7 25.0 %collective-permute-start.37 = (bf16[256,2048]{1,0:T(8,128)(2,1)S(1)}, bf16[256,2048]{1,0:T(8,128)(2,1)S(1)}, u32[]{:S(2)}, u32[]{:S(2)}) collective-permute-start(bf16[256,2048]{1,0:T(8,128)(2,1)S(1)} %get-tuple-element.58), channel_id=1, source_target_pairs={{0,2},{1,3},{2,0},{3,1},{4,6},{5,7},{6,4},{7,5},{8,10},{9,11},{10,... | collective-permute-start | bytes 3145736 | tf_op jit(solution)/shard_map/ppermute | solution.py:286
  498.1 52.2 %collective-permute-start.57 = (bf16[1024,512]{1,0:T(8,128)(2,1)}, bf16[1024,512]{1,0:T(8,128)(2,1)}, u32[]{:S(2)}, u32[]{:S(2)}) collective-permute-start(bf16[1024,512]{1,0:T(8,128)(2,1)} %fusion.67), channel_id=1, source_target_pairs={{0,4},{4,0},{8,12},{12,8},{16,20},{20,16},{24,28},{28,24},{1,5},{5... | collective-permute-start | bytes 3145736 | tf_op jit(solution)/shard_map/ppermute | solution.py:402
  532.9 14.9 %collective-permute-start.44 = (bf16[128,2048]{1,0:T(8,128)(2,1)S(1)}, bf16[128,2048]{1,0:T(8,128)(2,1)S(1)}, u32[]{:S(2)}, u32[]{:S(2)}) collective-permute-start(bf16[128,2048]{1,0:T(8,128)(2,1)S(1)} %get-tuple-element.141), channel_id=1, source_target_pairs={{0,1},{1,0},{2,3},{3,2},{4,5},{5,4},{6,7},{7,6},{8,9},{9,8},{10,11... | collective-permute-start | bytes 1572872 | tf_op jit(solution)/shard_map/ppermute | solution.py:315
  533.1 16.1 %collective-permute-start.45 = (bf16[128,2048]{1,0:T(8,128)(2,1)S(1)}, bf16[128,2048]{1,0:T(8,128)(2,1)S(1)}, u32[]{:S(2)}, u32[]{:S(2)}) collective-permute-start(bf16[128,2048]{1,0:T(8,128)(2,1)S(1)} %get-tuple-element.140), channel_id=1, source_target_pairs={{0,2},{1,3},{2,0},{3,1},{4,6},{5,7},{6,4},{7,5},{8,10},{9,11},{10,... | collective-permute-start | bytes 1572872 | tf_op jit(solution)/shard_map/ppermute | solution.py:315
  536.6 61.4 %collective-permute-start.56 = (bf16[1024,768]{1,0:T(8,128)(2,1)S(1)}, bf16[1024,768]{1,0:T(8,128)(2,1)S(1)}, u32[]{:S(2)}, u32[]{:S(2)}) collective-permute-start(bf16[1024,768]{1,0:T(8,128)(2,1)S(1)} %fusion.62), channel_id=1, source_target_pairs={{0,4},{4,0},{8,12},{12,8},{16,20},{20,16},{24,28},{28,24},{1,5},{5... | collective-permute-start | bytes 4718600 | tf_op jit(solution)/shard_map/ppermute | solution.py:402
  537.1 21.8 %collective-permute-start.43 = (bf16[128,2048]{1,0:T(8,128)(2,1)S(1)}, bf16[128,2048]{1,0:T(8,128)(2,1)S(1)}, u32[]{:S(2)}, u32[]{:S(2)}) collective-permute-start(bf16[128,2048]{1,0:T(8,128)(2,1)S(1)} %get-tuple-element.138), channel_id=1, source_target_pairs={{0,1},{1,0},{2,3},{3,2},{4,5},{5,4},{6,7},{7,6},{8,9},{9,8},{10,11... | collective-permute-start | bytes 1572872 | tf_op jit(solution)/shard_map/ppermute | solution.py:315
  547.7 14.8 %collective-permute-start.47 = (bf16[128,2048]{1,0:T(8,128)(2,1)S(1)}, bf16[128,2048]{1,0:T(8,128)(2,1)S(1)}, u32[]{:S(2)}, u32[]{:S(2)}) collective-permute-start(bf16[128,2048]{1,0:T(8,128)(2,1)S(1)} %get-tuple-element.139), channel_id=1, source_target_pairs={{0,2},{1,3},{2,0},{3,1},{4,6},{5,7},{6,4},{7,5},{8,10},{9,11},{10,... | collective-permute-start | bytes 1572872 | tf_op jit(solution)/shard_map/ppermute | solution.py:315
  549.6 44.9 %collective-permute-start.46 = (bf16[128,2048]{1,0:T(8,128)(2,1)S(1)}, bf16[128,2048]{1,0:T(8,128)(2,1)S(1)}, u32[]{:S(2)}, u32[]{:S(2)}) collective-permute-start(bf16[128,2048]{1,0:T(8,128)(2,1)S(1)} %get-tuple-element.65), channel_id=1, source_target_pairs={{0,2},{1,3},{2,0},{3,1},{4,6},{5,7},{6,4},{7,5},{8,10},{9,11},{10,... | collective-permute-start | bytes 1572872 | tf_op jit(solution)/shard_map/ppermute | solution.py:315
  550.3 45.8 %collective-permute-start.48 = (bf16[128,2048]{1,0:T(8,128)(2,1)S(1)}, bf16[128,2048]{1,0:T(8,128)(2,1)S(1)}, u32[]{:S(2)}, u32[]{:S(2)}) collective-permute-start(bf16[128,2048]{1,0:T(8,128)(2,1)S(1)} %get-tuple-element.66), channel_id=1, source_target_pairs={{0,1},{1,0},{2,3},{3,2},{4,5},{5,4},{6,7},{7,6},{8,9},{9,8},{10,11... | collective-permute-start | bytes 1572872 | tf_op jit(solution)/shard_map/ppermute | solution.py:315
  559.0 84.6 %collective-permute-start.40 = (bf16[256,2048]{1,0:T(8,128)(2,1)}, bf16[256,2048]{1,0:T(8,128)(2,1)}, u32[]{:S(2)}, u32[]{:S(2)}) collective-permute-start(bf16[256,2048]{1,0:T(8,128)(2,1)} %get-tuple-element.144), channel_id=1, source_target_pairs={{0,3},{1,2},{2,1},{3,0},{4,7},{5,6},{6,5},{7,4},{8,11},{9,10},{10,... | collective-permute-start | bytes 3145736 | tf_op jit(solution)/shard_map/ppermute | solution.py:337
  562.5 81.1 %collective-permute-start.41 = (bf16[256,2048]{1,0:T(8,128)(2,1)}, bf16[256,2048]{1,0:T(8,128)(2,1)}, u32[]{:S(2)}, u32[]{:S(2)}) collective-permute-start(bf16[256,2048]{1,0:T(8,128)(2,1)} %get-tuple-element.146), channel_id=1, source_target_pairs={{0,1},{1,0},{2,3},{3,2},{4,5},{5,4},{6,7},{7,6},{8,9},{9,8},{10,11... | collective-permute-start | bytes 3145736 | tf_op jit(solution)/shard_map/ppermute | solution.py:337
  594.5 49.1 %collective-permute-start.42 = (bf16[256,2048]{1,0:T(8,128)(2,1)}, bf16[256,2048]{1,0:T(8,128)(2,1)}, u32[]{:S(2)}, u32[]{:S(2)}) collective-permute-start(bf16[256,2048]{1,0:T(8,128)(2,1)} %get-tuple-element.145), channel_id=1, source_target_pairs={{0,2},{1,3},{2,0},{3,1},{4,6},{5,7},{6,4},{7,5},{8,10},{9,11},{10,... | collective-permute-start | bytes 3145736 | tf_op jit(solution)/shard_map/ppermute | solution.py:337
  651.8 38.2 %collective-permute-start.53 = (f32[2,2048]{1,0:T(2,128)S(1)}, f32[2,2048]{1,0:T(2,128)S(1)}, u32[]{:S(2)}, u32[]{:S(2)}) collective-permute-start(f32[2,2048]{1,0:T(2,128)S(1)} %fusion.128), channel_id=1, source_target_pairs={{0,4},{4,0},{8,12},{12,8},{16,20},{20,16},{24,28},{28,24},{1,5},{5... | collective-permute-start | bytes 49160 | tf_op jit(solution)/shard_map/ppermute | solution.py:424
  (110 other events, 1237.3 us)
Sparse Core Ops, SparseCore 0:
  10.4 59.3 all-gather.3
  72.0 151.6 all-gather.5
  278.3 75.0 all-gather.7
  410.9 83.8 reduce-scatter.5
  496.9 136.7 reduce-scatter.3
  635.9 52.7 reduce-scatter.7
